TPU v7x, 32 devices: a whole 2x2x4 slice. The times are simulated.
32 devices in a mesh: dp: 8 (over z, y), seq: 4 (over x, core).
Axes of the slice: x: 2, y: 2, z: 4, core: 2. Of those that a mesh axis runs over, the one named last changes fastest.
Arguments:
- tokens: bfloat16 [16, 256, 1152], P('dp', 'seq'), may hold values from -6 to 6
- cotangent: bfloat16 [16, 256, 1152], P('dp', 'seq'), may hold values from -6 to 6
- ln1_gain: bfloat16 [1152], P('dp'), may hold values from 0.5 to 1.5
- ln1_shift: bfloat16 [1152], P('dp'), may hold values from -1.5 to 1.5
- q_weight: bfloat16 [1152, 1152], P('dp'), may hold values from -0.1875 to 0.1875
- q_bias: bfloat16 [1152], P('dp'), may hold values from -1.5 to 1.5
- k_weight: bfloat16 [1152, 1152], P('dp'), may hold values from -0.1875 to 0.1875
- v_weight: bfloat16 [1152, 1152], P('dp'), may hold values from -0.1875 to 0.1875
- v_bias: bfloat16 [1152], P('dp'), may hold values from -0.25 to 0.25
- o_weight: bfloat16 [1152, 1152], P('dp'), may hold values from -1.5 to 1.5
- o_bias: bfloat16 [1152], P('dp'), may hold values from -1.5 to 1.5
- ln2_gain: bfloat16 [1152], P('dp'), may hold values from 0.5 to 1.5
- ln2_shift: bfloat16 [1152], P('dp'), may hold values from -1.5 to 1.5
- in_weight: bfloat16 [1152, 4304], P('dp'), may hold values from -0.1875 to 0.1875
- in_bias: bfloat16 [4304], replicated, may hold values from -2.5 to 2.5
- out_weight: bfloat16 [4304, 1152], P(None, 'dp'), may hold values from -0.09375 to 0.09375
- out_bias: bfloat16 [1152], P('dp'), may hold values from -1.5 to 1.5
Outputs:
- output: bfloat16 [16, 256, 1152], P('dp', 'seq')
- grad_tokens: bfloat16 [16, 256, 1152], P('dp', 'seq')
- grad_ln1_gain: float32 [1152], P('dp')
- grad_ln1_shift: float32 [1152], P('dp')
- grad_q_weight: float32 [1152, 1152], P('dp')
- grad_q_bias: float32 [1152], P('dp')
- grad_k_weight: float32 [1152, 1152], P('dp')
- grad_v_weight: float32 [1152, 1152], P('dp')
- grad_v_bias: float32 [1152], P('dp')
- grad_o_weight: float32 [1152, 1152], P('dp')
- grad_o_bias: float32 [1152], P('dp')
- grad_ln2_gain: float32 [1152], P('dp')
- grad_ln2_shift: float32 [1152], P('dp')
- grad_in_weight: float32 [1152, 4304], P('dp')
- grad_in_bias: float32 [4304], replicated
- grad_out_weight: float32 [4304, 1152], P(None, 'dp')
- grad_out_bias: float32 [1152], P('dp')
All inputs are finite; a program needn't handle non-finite values.
Results may differ from a plain program's by a relative error of at most 0.019.
Values may be sent and summed in bfloat16 or wider, within the bound.
A program may use at most 256 MiB of HBM per device.

v0:
```python
import math

import jax
import jax.numpy as jnp
from jax import lax
from jax.sharding import PartitionSpec as P

HEADS = 16
HEAD_DIM = 72


eps_norm = 1e-06
gelu_coef = 0.7978845608028654
gelu_cube = 0.044715
group_heads = 4


def project(left_mat, right_mat):
    return jnp.dot(left_mat, right_mat, preferred_element_type=jnp.float32)


def contract_rows(left_mat, right_mat):
    return lax.dot_general(
        left_mat, right_mat, (((0,), (0,)), ((), ())), preferred_element_type=jnp.float32
    )


def contract_cols(left_mat, right_mat):
    return lax.dot_general(
        left_mat, right_mat, (((1,), (1,)), ((), ())), preferred_element_type=jnp.float32
    )


def normalize(values):
    row_mean = jnp.mean(values, axis=-1, keepdims=True)
    centred = values - row_mean
    inverse = lax.rsqrt(jnp.mean(centred * centred, axis=-1, keepdims=True) + eps_norm)
    return (centred * inverse, inverse)


def norm_back(grad_normed, gain_vec, scaled, inverse):
    grad_scaled = grad_normed * gain_vec.astype(jnp.float32)
    centred_grad = grad_scaled - jnp.mean(grad_scaled, axis=-1, keepdims=True)
    return inverse * (
        centred_grad - scaled * jnp.mean(grad_scaled * scaled, axis=-1, keepdims=True)
    )


def gelu_parts(pre_act):
    tanh_val = jnp.tanh(gelu_coef * (pre_act + gelu_cube * pre_act * pre_act * pre_act))
    value_part = 0.5 * pre_act * (1.0 + tanh_val)
    slope_part = 0.5 * (1.0 + tanh_val) + 0.5 * pre_act * (
        1.0 - tanh_val * tanh_val
    ) * gelu_coef * (1.0 + 3.0 * gelu_cube * pre_act * pre_act)
    return (value_part, slope_part)


def score_rows(query_heads, key_heads):
    factor = 1.0 / math.sqrt(query_heads.shape[-1])
    return (
        jnp.einsum("qhd,khd->hqk", query_heads, key_heads, preferred_element_type=jnp.float32)
        * factor
    )


def split_groups(rows):
    count = rows.shape[0]
    return rows.reshape(count, HEADS // group_heads, group_heads, HEAD_DIM).transpose(1, 0, 2, 3)


def join_groups(grouped):
    count = grouped.shape[1]
    return grouped.transpose(1, 0, 2, 3).reshape(count, HEADS * HEAD_DIM)


def attention_back(parts):
    query_group, key_group, value_group, grad_group, lse_group = parts
    factor = 1.0 / math.sqrt(HEAD_DIM)
    probs_full = jnp.exp(score_rows(query_group, key_group) - lse_group)
    grad_probs = jnp.einsum(
        "qhd,khd->hqk", grad_group, value_group, preferred_element_type=jnp.float32
    )
    row_dot = jnp.sum(probs_full * grad_probs, axis=-1, keepdims=True)
    grad_scores = (probs_full * (grad_probs - row_dot)).astype(jnp.bfloat16)
    grad_query = (
        jnp.einsum("hqk,khd->qhd", grad_scores, key_group, preferred_element_type=jnp.float32)
        * factor
    ).astype(jnp.bfloat16)
    key_part = (
        jnp.einsum("hqk,qhd->khd", grad_scores, query_group, preferred_element_type=jnp.float32)
        * factor
    )
    value_part = jnp.einsum(
        "hqk,qhd->khd",
        probs_full.astype(jnp.bfloat16),
        grad_group,
        preferred_element_type=jnp.float32,
    )
    return (grad_query, key_part, value_part)


def fetch_forward(shards):
    return (
        lax.all_gather(shards[0], "dp", axis=0, tiled=True),
        lax.all_gather(shards[1], "dp", axis=0, tiled=True),
        lax.all_gather(shards[2], "dp", axis=0, tiled=True),
        lax.all_gather(shards[3], "dp", axis=0, tiled=True),
        lax.all_gather(shards[4], "dp", axis=0, tiled=True),
        lax.all_gather(shards[5], "dp", axis=0, tiled=True),
        lax.all_gather(shards[6], "dp", axis=0, tiled=True),
        lax.all_gather(shards[7], "dp", axis=0, tiled=True),
        lax.all_gather(shards[8], "dp", axis=0, tiled=True),
        lax.all_gather(shards[9], "dp", axis=0, tiled=True),
        lax.all_gather(shards[10], "dp", axis=0, tiled=True),
        lax.all_gather(shards[11], "dp", axis=0, tiled=True),
        lax.all_gather(shards[12], "dp", axis=1, tiled=True),
        lax.all_gather(shards[13], "dp", axis=0, tiled=True),
    )


def fetch_backward(shards):
    return (
        lax.all_gather(shards[0], "dp", axis=0, tiled=True),
        lax.all_gather(shards[1], "dp", axis=0, tiled=True),
        lax.all_gather(shards[2], "dp", axis=0, tiled=True),
        lax.all_gather(shards[3], "dp", axis=0, tiled=True),
        lax.all_gather(shards[4], "dp", axis=0, tiled=True),
        lax.all_gather(shards[5], "dp", axis=0, tiled=True),
        lax.all_gather(shards[6], "dp", axis=0, tiled=True),
        lax.all_gather(shards[7], "dp", axis=0, tiled=True),
        lax.all_gather(shards[8], "dp", axis=0, tiled=True),
        lax.all_gather(shards[9], "dp", axis=0, tiled=True),
        lax.all_gather(shards[10], "dp", axis=0, tiled=True),
        lax.all_gather(shards[11], "dp", axis=0, tiled=True),
        lax.all_gather(shards[12], "dp", axis=1, tiled=True),
        lax.all_gather(shards[13], "dp", axis=0, tiled=True),
    )


def full_zeros(shards, group_count):
    zero_list = []
    for position, shard_piece in enumerate(shards):
        if position == 12:
            zero_list.append(
                jnp.zeros((shard_piece.shape[0], shard_piece.shape[1] * group_count), jnp.float32)
            )
        else:
            zero_list.append(
                jnp.zeros(
                    (shard_piece.shape[0] * group_count,) + shard_piece.shape[1:], jnp.float32
                )
            )
    return tuple(zero_list)


def forward(image_rows, full_weights, in_bias):
    (
        ln1_gain,
        ln1_shift,
        q_weight,
        q_bias,
        k_weight,
        v_weight,
        v_bias,
        o_weight,
        o_bias,
        ln2_gain,
        ln2_shift,
        in_weight,
        out_weight,
        out_bias,
    ) = full_weights
    row_count = image_rows.shape[0]
    start_rows = image_rows.astype(jnp.float32)
    scaled1, inverse1 = normalize(start_rows)
    normed1 = (scaled1 * ln1_gain.astype(jnp.float32) + ln1_shift.astype(jnp.float32)).astype(
        jnp.bfloat16
    )
    queries = (project(normed1, q_weight) + q_bias).astype(jnp.bfloat16)
    key_rows = project(normed1, k_weight).astype(jnp.bfloat16)
    value_rows = (project(normed1, v_weight) + v_bias).astype(jnp.bfloat16)
    all_keys, all_values = (
        lax.all_gather(key_rows, "seq", axis=0, tiled=True),
        lax.all_gather(value_rows, "seq", axis=0, tiled=True),
    )
    length = all_keys.shape[0]
    query_heads = queries.reshape(row_count, HEADS, HEAD_DIM)
    key_heads = all_keys.reshape(length, HEADS, HEAD_DIM)
    value_heads = all_values.reshape(length, HEADS, HEAD_DIM)
    scores = score_rows(query_heads, key_heads)
    row_top = jnp.max(scores, axis=-1, keepdims=True)
    expo_rows = jnp.exp(scores - row_top)
    row_total = jnp.sum(expo_rows, axis=-1, keepdims=True)
    probs_low = (expo_rows / row_total).astype(jnp.bfloat16)
    logsum = row_top + jnp.log(row_total)
    mixed_rows = jnp.einsum(
        "hqk,khd->qhd", probs_low, value_heads, preferred_element_type=jnp.float32
    )
    mixed_rows = mixed_rows.reshape(row_count, HEADS * HEAD_DIM).astype(jnp.bfloat16)
    hidden = start_rows + project(mixed_rows, o_weight) + o_bias
    scaled2, inverse2 = normalize(hidden)
    normed2 = (scaled2 * ln2_gain.astype(jnp.float32) + ln2_shift.astype(jnp.float32)).astype(
        jnp.bfloat16
    )
    pre_act = project(normed2, in_weight) + in_bias
    act_value, act_slope = gelu_parts(pre_act)
    active = act_value.astype(jnp.bfloat16)
    result = hidden + project(active, out_weight) + out_bias
    stored = (
        scaled1,
        inverse1,
        normed1,
        queries,
        all_keys,
        all_values,
        logsum,
        mixed_rows,
        scaled2,
        inverse2,
        normed2,
        act_slope,
        active,
    )
    return (result.astype(jnp.bfloat16), stored)


def backward(image_cot, stored, full_weights, totals, bias_grad):
    (
        ln1_gain,
        ln1_shift,
        q_weight,
        q_bias,
        k_weight,
        v_weight,
        v_bias,
        o_weight,
        o_bias,
        ln2_gain,
        ln2_shift,
        in_weight,
        out_weight,
        out_bias,
    ) = full_weights
    (
        scaled1,
        inverse1,
        normed1,
        queries,
        all_keys,
        all_values,
        logsum,
        mixed_rows,
        scaled2,
        inverse2,
        normed2,
        act_slope,
        active,
    ) = stored
    row_count = image_cot.shape[0]
    upstream = image_cot.astype(jnp.float32)
    g_out_weight = contract_rows(active, image_cot)
    g_out_bias = jnp.sum(upstream, axis=0)
    grad_pre = (contract_cols(image_cot, out_weight) * act_slope).astype(jnp.bfloat16)
    g_in_weight = contract_rows(normed2, grad_pre)
    g_in_bias = jnp.sum(grad_pre.astype(jnp.float32), axis=0)
    grad_normed2 = contract_cols(grad_pre, in_weight)
    g_ln2_gain = jnp.sum(grad_normed2 * scaled2, axis=0)
    g_ln2_shift = jnp.sum(grad_normed2, axis=0)
    grad_hidden = upstream + norm_back(grad_normed2, ln2_gain, scaled2, inverse2)
    grad_branch = grad_hidden.astype(jnp.bfloat16)
    g_o_weight = contract_rows(mixed_rows, grad_branch)
    g_o_bias = jnp.sum(grad_branch.astype(jnp.float32), axis=0)
    grad_mixed = contract_cols(grad_branch, o_weight).astype(jnp.bfloat16)
    lse_groups = logsum.reshape(HEADS // group_heads, group_heads, row_count, 1)
    grouped = lax.map(
        attention_back,
        (
            split_groups(queries),
            split_groups(all_keys),
            split_groups(all_values),
            split_groups(grad_mixed),
            lse_groups,
        ),
    )
    grad_queries = join_groups(grouped[0])
    key_terms = join_groups(grouped[1])
    value_terms = join_groups(grouped[2])
    grad_keys, grad_values = (
        lax.psum_scatter(
            key_terms.astype(jnp.bfloat16), "seq", scatter_dimension=0, tiled=True
        ).astype(jnp.float32),
        lax.psum_scatter(
            value_terms.astype(jnp.bfloat16), "seq", scatter_dimension=0, tiled=True
        ).astype(jnp.float32),
    )
    grad_keys = grad_keys.astype(jnp.bfloat16)
    grad_values = grad_values.astype(jnp.bfloat16)
    g_q_weight = contract_rows(normed1, grad_queries)
    g_q_bias = jnp.sum(grad_queries.astype(jnp.float32), axis=0)
    g_k_weight = contract_rows(normed1, grad_keys)
    g_v_weight = contract_rows(normed1, grad_values)
    g_v_bias = jnp.sum(grad_values.astype(jnp.float32), axis=0)
    grad_normed1 = (
        contract_cols(grad_queries, q_weight)
        + contract_cols(grad_keys, k_weight)
        + contract_cols(grad_values, v_weight)
    )
    g_ln1_gain = jnp.sum(grad_normed1 * scaled1, axis=0)
    g_ln1_shift = jnp.sum(grad_normed1, axis=0)
    grad_start = grad_hidden + norm_back(grad_normed1, ln1_gain, scaled1, inverse1)
    new_terms = (
        g_ln1_gain,
        g_ln1_shift,
        g_q_weight,
        g_q_bias,
        g_k_weight,
        g_v_weight,
        g_v_bias,
        g_o_weight,
        g_o_bias,
        g_ln2_gain,
        g_ln2_shift,
        g_in_weight,
        g_out_weight,
        g_out_bias,
    )
    totals = tuple((old_sum + new_term for old_sum, new_term in zip(totals, new_terms)))
    return (grad_start.astype(jnp.bfloat16), totals, bias_grad + g_in_bias)


def on_device(
    tokens,
    cotangent,
    ln1_gain,
    ln1_shift,
    q_weight,
    q_bias,
    k_weight,
    v_weight,
    v_bias,
    o_weight,
    o_bias,
    ln2_gain,
    ln2_shift,
    in_weight,
    in_bias,
    out_weight,
    out_bias,
):
    shards = (
        ln1_gain,
        ln1_shift,
        q_weight,
        q_bias,
        k_weight,
        v_weight,
        v_bias,
        o_weight,
        o_bias,
        ln2_gain,
        ln2_shift,
        in_weight,
        out_weight,
        out_bias,
    )
    totals = full_zeros(shards, lax.axis_size("dp"))
    bias_grad = jnp.zeros(in_bias.shape, jnp.float32)
    outputs = []
    grad_list = []
    for image_idx in range(tokens.shape[0]):
        gathered = fetch_forward(shards)
        result, stored = forward(tokens[image_idx], gathered, in_bias)
        gathered_back = fetch_backward(shards)
        grad_start, totals, bias_grad = backward(
            cotangent[image_idx], stored, gathered_back, totals, bias_grad
        )
        outputs.append(result)
        grad_list.append(grad_start)
    seq_part = (
        lax.psum_scatter(
            totals[2].astype(jnp.bfloat16), "seq", scatter_dimension=1, tiled=True
        ).astype(jnp.float32),
        lax.psum_scatter(
            totals[4].astype(jnp.bfloat16), "seq", scatter_dimension=1, tiled=True
        ).astype(jnp.float32),
        lax.psum_scatter(
            totals[5].astype(jnp.bfloat16), "seq", scatter_dimension=1, tiled=True
        ).astype(jnp.float32),
        lax.psum_scatter(
            totals[7].astype(jnp.bfloat16), "seq", scatter_dimension=1, tiled=True
        ).astype(jnp.float32),
        lax.psum_scatter(
            totals[11].astype(jnp.bfloat16), "seq", scatter_dimension=1, tiled=True
        ).astype(jnp.float32),
        lax.psum_scatter(
            totals[12].astype(jnp.bfloat16), "seq", scatter_dimension=0, tiled=True
        ).astype(jnp.float32),
    )
    scattered = (
        lax.psum_scatter(seq_part[0], "dp", scatter_dimension=0, tiled=True),
        lax.psum_scatter(seq_part[1], "dp", scatter_dimension=0, tiled=True),
        lax.psum_scatter(seq_part[2], "dp", scatter_dimension=0, tiled=True),
        lax.psum_scatter(seq_part[3], "dp", scatter_dimension=0, tiled=True),
        lax.psum_scatter(seq_part[4], "dp", scatter_dimension=0, tiled=True),
        lax.psum_scatter(seq_part[5], "dp", scatter_dimension=1, tiled=True),
        lax.psum_scatter(totals[0], "dp", scatter_dimension=0, tiled=True),
        lax.psum_scatter(totals[1], "dp", scatter_dimension=0, tiled=True),
        lax.psum_scatter(totals[3], "dp", scatter_dimension=0, tiled=True),
        lax.psum_scatter(totals[6], "dp", scatter_dimension=0, tiled=True),
        lax.psum_scatter(totals[8], "dp", scatter_dimension=0, tiled=True),
        lax.psum_scatter(totals[9], "dp", scatter_dimension=0, tiled=True),
        lax.psum_scatter(totals[10], "dp", scatter_dimension=0, tiled=True),
        lax.psum_scatter(totals[13], "dp", scatter_dimension=0, tiled=True),
    )
    matrices = (
        lax.all_gather(scattered[0].astype(jnp.bfloat16), "seq", axis=1, tiled=True).astype(
            jnp.float32
        ),
        lax.all_gather(scattered[1].astype(jnp.bfloat16), "seq", axis=1, tiled=True).astype(
            jnp.float32
        ),
        lax.all_gather(scattered[2].astype(jnp.bfloat16), "seq", axis=1, tiled=True).astype(
            jnp.float32
        ),
        lax.all_gather(scattered[3].astype(jnp.bfloat16), "seq", axis=1, tiled=True).astype(
            jnp.float32
        ),
        lax.all_gather(scattered[4].astype(jnp.bfloat16), "seq", axis=1, tiled=True).astype(
            jnp.float32
        ),
        lax.all_gather(scattered[5].astype(jnp.bfloat16), "seq", axis=0, tiled=True).astype(
            jnp.float32
        ),
    )
    vectors = lax.psum(
        (
            scattered[6],
            scattered[7],
            scattered[8],
            scattered[9],
            scattered[10],
            scattered[11],
            scattered[12],
            scattered[13],
        ),
        "seq",
    )
    bias_total = lax.psum(bias_grad, ("dp", "seq"))
    return (
        jnp.stack(outputs),
        jnp.stack(grad_list),
        vectors[0],
        vectors[1],
        matrices[0],
        vectors[2],
        matrices[1],
        matrices[2],
        vectors[3],
        matrices[3],
        vectors[4],
        vectors[5],
        vectors[6],
        matrices[4],
        bias_total,
        matrices[5],
        vectors[7],
    )


def solution(mesh):
    return jax.shard_map(
        on_device,
        mesh=mesh,
        in_specs=(
            P("dp", "seq", None),
            P("dp", "seq", None),
            P("dp"),
            P("dp"),
            P("dp", None),
            P("dp"),
            P("dp", None),
            P("dp", None),
            P("dp"),
            P("dp", None),
            P("dp"),
            P("dp"),
            P("dp"),
            P("dp", None),
            P(),
            P(None, "dp"),
            P("dp"),
        ),
        out_specs=(
            P("dp", "seq", None),
            P("dp", "seq", None),
            P("dp"),
            P("dp"),
            P("dp", None),
            P("dp"),
            P("dp", None),
            P("dp", None),
            P("dp"),
            P("dp", None),
            P("dp"),
            P("dp"),
            P("dp"),
            P("dp", None),
            P(),
            P(None, "dp"),
            P("dp"),
        ),
        check_vma=False,
    )
```

profile of v0, /device:TPU:1, one launch (start us, length us, event | category | flops | bytes accessed | tf_op | source)
XLA Modules:
  0.0 1498.2 jit_solution(15623618965766850240)
XLA Ops:
  14.6 31.5 %all-reduce.22 = (bf16[1152]{0:T(1024)(128)(2,1)S(1)}, bf16[1152]{0:T(1024)(128)(2,1)S(1)}, bf16[1152]{0:T(1024)(128)(2,1)S(1)}, bf16[1152]{0:T(1024)(128)(2,1)S...) all-reduce(bf16[1152]{0:T(1024)(128)(2,1)S(1)} %dynamic-update-slic, ...), channel_id=1, replica_groups=mesh['dp'=8,'seq'=4] {'dp'}, use_global_device_ids=true, to_apply=%add.1 | all-reduce | flops 9216 | bytes 36864
  49.6 16.2 %all-gather.17.cloned.1.call-done = bf16[1152,1152]{1,0:T(8,128)(2,1)} async-done(((bf16[144,1152]{1,0:T(8,128)(2,1)}), bf16[1152,1152]{1,0:T(8,128)(2,1)}) %all-gather.17.cloned.1.call-update) | async-done | bytes 2654224 | tf_op jit(solution)/shard_map/all_gather | solution.py:106
  73.8 47.8 %all-gather.19.cloned.1.call-done = bf16[1152,1152]{1,0:T(8,128)(2,1)} async-done(((bf16[144,1152]{1,0:T(8,128)(2,1)}), bf16[1152,1152]{1,0:T(8,128)(2,1)}) %all-gather.19.cloned.1.call-update) | async-done | bytes 2654224 | tf_op jit(solution)/shard_map/all_gather | solution.py:108
  144.0 33.4 %all-gather.15.cloned.1.call-done = bf16[1152,1152]{1,0:T(8,128)(2,1)} async-done(((bf16[144,1152]{1,0:T(8,128)(2,1)}), bf16[1152,1152]{1,0:T(8,128)(2,1)}) %all-gather.15.cloned.1.call-update) | async-done | bytes 2654224 | tf_op jit(solution)/shard_map/all_gather | solution.py:109
  179.9 10.1 all_gather.52
  209.1 23.9 %all-gather.21.cloned.1.call-done = bf16[1152,1152]{1,0:T(8,128)(2,1)} async-done(((bf16[144,1152]{1,0:T(8,128)(2,1)}), bf16[1152,1152]{1,0:T(8,128)(2,1)}) %all-gather.21.cloned.1.call-update) | async-done | bytes 2654224 | tf_op jit(solution)/shard_map/all_gather | solution.py:111
  240.3 139.1 %all-gather.23.cloned.1.call-done = bf16[1152,4304]{1,0:T(8,128)(2,1)} async-done(((bf16[144,4304]{1,0:T(8,128)(2,1)}), bf16[1152,4304]{1,0:T(8,128)(2,1)}) %all-gather.23.cloned.1.call-update) | async-done | bytes 9916432 | tf_op jit(solution)/shard_map/all_gather | solution.py:115
  389.0 135.4 %all-gather.25.cloned.1.call-done = bf16[4304,1152]{0,1:T(8,128)(2,1)} async-done(((bf16[4304,144]{0,1:T(8,128)(2,1)}), bf16[4304,1152]{0,1:T(8,128)(2,1)}) %all-gather.25.cloned.1.call-update) | async-done | bytes 9916432 | tf_op jit(solution)/shard_map/all_gather | solution.py:116
  555.5 34.3 %while.28 = (s32[]{:T(128)}, bf16[4,64,4,72]{3,1,2,0:T(8,128)(2,1)}, bf16[4,256,4,72]{1,3,2,0:T(8,128)(2,1)}, bf16[4,256,4,72]{1,3,2,0:T(8,128)(2,1)}, bf16[4,25...) while((s32[]{:T(128)}, ...), condition=%wide.region_16.17_spmd, body=%wide.region_14.16_spmd.sunk | while | flops 47820544 | bytes 8054953 | solution.py:275
  596.2 22.2 %while.29 = (s32[]{:T(128)}, bf16[4,64,4,72]{3,1,2,0:T(8,128)(2,1)S(1)}, bf16[4,256,4,72]{1,3,2,0:T(8,128)(2,1)S(1)}, bf16[4,256,4,72]{1,3,2,0:T(8,128)(2,1)S(1)...) while((s32[]{:T(128)}, ...), condition=%wide.region_25.26_spmd, body=%wide.region_23.25_spmd.sunk | while | flops 47820544 | bytes 3336305 | solution.py:275
  663.4 11.1 fusion.63
  674.4 11.3 fusion.62
  695.6 227.4 %fusion.182 = (bf16[1152,1088]{0,1:T(8,128)(2,1)}, bf16[1088,1152]{1,0:T(8,128)(2,1)S(1)}) fusion(bf16[1152,4304]{0,1:T(8,128)(2,1)} %fusion.62, bf16[4304,1152]{1,0:T(8,128)(2,1)} %fusion.63), kind=kCustom, calls=%all-reduce-scatter.2 | all-reduce-scatter fusion | flops 10027009 | bytes 24846848
  929.9 14.1 concatenate
  961.3 12.2 concatenate.1
  1000.1 41.8 %psum.70 = f32[4304]{0:T(1024)} all-reduce(f32[4304]{0:T(1024)S(1)} %add.415), channel_id=1, replica_groups=mesh['dp'=8,'seq'=4] {'dp','seq'}, use_global_device_ids=true, to_apply=%region_70.71 | all-reduce | flops 4304 | bytes 34432 | tf_op jit(solution)/shard_map/psum | solution.py:448
  1071.9 32.5 %all-reduce.20 = (f32[1152]{0:T(1024)S(1)}, f32[1152]{0:T(1024)S(1)}, f32[1152]{0:T(1024)S(1)}, f32[1152]{0:T(1024)S(1)}, f32[1152]{0:T(1024)S(1)}, /*index=5*/f...) all-reduce(f32[1152]{0:T(1024)S(1)} %add.399, ...), channel_id=6, replica_groups=mesh['dp'=8,'seq'=4] {'dp'}, use_global_device_ids=true, to_apply=%region_32.33.clone | all-reduce | flops 9216 | bytes 73728
  1105.0 13.8 all-reduce.21
  1118.8 51.6 %reduce-scatter.65.cloned.1.call-done = f32[144,1076]{1,0:T(8,128)} async-done(((f32[1152,1076]{1,0:T(8,128)}), f32[144,1076]{1,0:T(8,128)}) %reduce-scatter.65.cloned.1.call-update) | async-done | bytes 619792
  1173.7 65.3 %reduce-scatter.61.cloned.1.call-done = f32[144,288]{1,0:T(8,128)} async-done(((f32[1152,288]{1,0:T(8,128)}), f32[144,288]{1,0:T(8,128)}) %reduce-scatter.61.cloned.1.call-update) | async-done | bytes 165904
  1250.1 58.2 %reduce-scatter.55.cloned.1.call-done = f32[144,288]{1,0:T(8,128)} async-done(((f32[1152,288]{1,0:T(8,128)}), f32[144,288]{1,0:T(8,128)}) %reduce-scatter.55.cloned.1.call-update) | async-done | bytes 165904
  1319.4 57.6 %reduce-scatter.59.cloned.1.call-done = f32[144,288]{1,0:T(8,128)} async-done(((f32[1152,288]{1,0:T(8,128)}), f32[144,288]{1,0:T(8,128)}) %reduce-scatter.59.cloned.1.call-update) | async-done | bytes 165904
  1388.3 58.1 %reduce-scatter.57.cloned.1.call-done = f32[144,288]{1,0:T(8,128)} async-done(((f32[1152,288]{1,0:T(8,128)}), f32[144,288]{1,0:T(8,128)}) %reduce-scatter.57.cloned.1.call-update) | async-done | bytes 165904
  1471.1 15.6 %all-gather.29.cloned.1.call-done = bf16[4,1076,144]{1,2,0:T(8,128)(2,1)} async-done(((bf16[1,1076,144]{1,2,0:T(8,128)(2,1)}), bf16[4,1076,144]{1,2,0:T(8,128)(2,1)}) %all-gather.29.cloned.1.call-update) | async-done | bytes 1239568 | tf_op jit(solution)/shard_map/all_gather | solution.py:431
  (555 shorter events, 371.7 us)
Async XLA Ops:
  7.3 58.5 %all-gather.17.cloned.1.call-start = ((), (), s32[]{:S(2)}) async-start(), calls=%async_computation.15 | async-start | bytes 2985984 | tf_op jit(solution)/shard_map/all_gather | solution.py:106
  8.0 113.6 %all-gather.19.cloned.1.call-start = ((), (), s32[]{:S(2)}) async-start(), calls=%async_computation.16 | async-start | bytes 2985984 | tf_op jit(solution)/shard_map/all_gather | solution.py:108
  8.8 168.6 %all-gather.15.cloned.1.call-start = ((), (), s32[]{:S(2)}) async-start(), calls=%async_computation.14 | async-start | bytes 2985984 | tf_op jit(solution)/shard_map/all_gather | solution.py:109
  9.5 223.5 %all-gather.21.cloned.1.call-start = ((), (), s32[]{:S(2)}) async-start(), calls=%async_computation.17 | async-start | bytes 2985984 | tf_op jit(solution)/shard_map/all_gather | solution.py:111
  10.1 369.2 %all-gather.23.cloned.1.call-start = ((), (), s32[]{:S(2)}) async-start(), calls=%async_computation.18 | async-start | bytes 11280384 | tf_op jit(solution)/shard_map/all_gather | solution.py:115
  10.7 513.7 %all-gather.25.cloned.1.call-start = ((), (), s32[]{:S(2)}) async-start(), calls=%async_computation.19 | async-start | bytes 11280384 | tf_op jit(solution)/shard_map/all_gather | solution.py:116
  11.3 619.2 %reduce-scatter.49.cloned.1.call-start = ((), (), s32[]{:S(2)}) async-start(), calls=%async_computation.27 | async-start | bytes 737280
  591.9 48.5 %reduce-scatter.53.cloned.1.call-start = ((), (), s32[]{:S(2)}) async-start(), calls=%async_computation.29 | async-start | bytes 737280
  619.5 66.3 %reduce-scatter.47.cloned.1.call-start = ((), (), s32[]{:S(2)}) async-start(), calls=%async_computation.26 | async-start | bytes 737280
  620.6 69.9 %reduce-scatter.51.cloned.1.call-start = ((), (), s32[]{:S(2)}) async-start(), calls=%async_computation.28 | async-start | bytes 737280
  621.8 363.1 %reduce-scatter.45.cloned.1.call-start = ((), (), s32[]{:S(2)}) async-start(), calls=%async_computation.23 | async-start | bytes 3317760 | tf_op jit(solution)/shard_map/reduce_scatter | solution.py:389
  625.3 362.4 %reduce-scatter.39.cloned.1.call-start = ((), (), s32[]{:S(2)}) async-start(), calls=%async_computation.20 | async-start | bytes 3317760 | tf_op jit(solution)/shard_map/reduce_scatter | solution.py:380
  630.2 360.2 %reduce-scatter.43.cloned.1.call-start = ((), (), s32[]{:S(2)}) async-start(), calls=%async_computation.22 | async-start | bytes 3317760 | tf_op jit(solution)/shard_map/reduce_scatter | solution.py:386
  645.5 347.7 %reduce-scatter.41.cloned.1.call-start = ((), (), s32[]{:S(2)}) async-start(), calls=%async_computation.21 | async-start | bytes 3317760 | tf_op jit(solution)/shard_map/reduce_scatter | solution.py:383
  695.6 365.9 %reduce-scatter.63.cloned.1.call-start = ((), (), s32[]{:S(2)}) async-start(), calls=%async_computation.34 | async-start | bytes 5971968
  923.9 6.0 collective-permute-start
  955.2 215.1 %reduce-scatter.65.cloned.1.call-start = ((), (), s32[]{:S(2)}) async-start(), calls=%async_computation.35 | async-start | bytes 5971968
  955.3 6.0 collective-permute-start.1
  984.8 254.2 %reduce-scatter.61.cloned.1.call-start = ((), (), s32[]{:S(2)}) async-start(), calls=%async_computation.33 | async-start | bytes 1990656
  987.6 320.7 %reduce-scatter.55.cloned.1.call-start = ((), (), s32[]{:S(2)}) async-start(), calls=%async_computation.30 | async-start | bytes 1990656
  990.3 386.7 %reduce-scatter.59.cloned.1.call-start = ((), (), s32[]{:S(2)}) async-start(), calls=%async_computation.32 | async-start | bytes 1990656
  993.2 453.1 %reduce-scatter.57.cloned.1.call-start = ((), (), s32[]{:S(2)}) async-start(), calls=%async_computation.31 | async-start | bytes 1990656
  996.0 470.8 %all-gather.27.cloned.1.call-start = ((), (), s32[]{:S(2)}) async-start(), calls=%async_computation.24 | async-start | bytes 1658880 | tf_op jit(solution)/shard_map/all_gather | solution.py:428
  1063.8 422.9 %all-gather.29.cloned.1.call-start = ((), (), s32[]{:S(2)}) async-start(), calls=%async_computation.25 | async-start | bytes 1658880 | tf_op jit(solution)/shard_map/all_gather | solution.py:431
  (125 other events, 1653.9 us)
Sparse Core Ops, SparseCore 0:
  10.3 55.4 all-gather.16
  67.9 53.6 all-gather.18
  123.8 53.5 all-gather.14
  179.4 53.5 all-gather.20
  235.0 144.2 all-gather.22
  381.4 142.9 all-gather.24
  592.0 20.7 reduce-scatter.48
  619.6 20.7 reduce-scatter.52
  643.5 22.0 reduce-scatter.46
  668.5 22.0 reduce-scatter.50
  693.1 49.3 reduce-scatter.44
  744.8 49.0 reduce-scatter.38
  796.5 49.0 reduce-scatter.42
  848.0 42.1 reduce-scatter.40
  955.3 106.0 reduce-scatter.62
  1064.9 105.4 reduce-scatter.64
  1173.7 65.2 reduce-scatter.60
  1242.9 65.3 reduce-scatter.54
  1311.8 65.2 reduce-scatter.58
  1380.9 65.3 reduce-scatter.56
  1447.9 18.9 all-gather.26
  1468.4 18.2 all-gather.28
where the time goes:
time: 1510 us; the launch traced here: 1500 us
  waiting for transfers between devices  724 us (48%)
  blocking collectives  416 us (28%)
  matrix products  187 us (12%)
  local copies, waits for them, and re-layouts  118 us (8%)
  other arithmetic  24 us (2%)
  between operations  18.4 us (1%)
    unnamed x34, waiting for transfers between devices  303 us
    unnamed x3, blocking collectives  291 us
    all_gather x1, waiting for transfers between devices, fetch_forward(): lax.all_gather(shards[11], 'dp', axis=0, tiled=True)  139 us
    all_gather x1, waiting for transfers between devices, fetch_forward(): lax.all_gather(shards[12], 'dp', axis=1, tiled=True)  135 us
    unnamed x288, local copies, waits for them, and re-layouts  74.4 us
    dot_general x12, matrix products, contract_rows(): lax.dot_general(left_mat, right_mat, (((0,), (0,)), ((), ())), preferred_...  64.4 us
    all_gather x1, waiting for transfers between devices, fetch_forward(): lax.all_gather(shards[4], 'dp', axis=0, tiled=True)  47.8 us
    psum x1, blocking collectives, on_device(): bias_total = lax.psum(bias_grad, ('dp', 'seq'))  41.8 us
  transfers between devices with their start and end apart: 24, of which 18 were waited for; matrix products, arithmetic and copies ran while one was open for 32% of the time, Pallas kernels for 0%

commit v1 on v0

v1 whole, which is shorter than its diff:
```python
import math

import jax
import jax.numpy as jnp
from jax import lax
from jax.sharding import PartitionSpec as P

HEADS = 16
HEAD_DIM = 72

eps_norm = 1e-06
gelu_coef = 0.7978845608028654
gelu_cube = 0.044715
F32 = jnp.float32
BF16 = jnp.bfloat16


def mm(a, b, ca, cb):
    return lax.dot_general(a, b, (((ca,), (cb,)), ((), ())), preferred_element_type=F32)


def normalize(values):
    row_mean = jnp.mean(values, axis=-1, keepdims=True)
    centred = values - row_mean
    inverse = lax.rsqrt(jnp.mean(centred * centred, axis=-1, keepdims=True) + eps_norm)
    return centred * inverse, inverse


def norm_back(grad_normed, gain_vec, scaled, inverse):
    grad_scaled = grad_normed * gain_vec
    centred_grad = grad_scaled - jnp.mean(grad_scaled, axis=-1, keepdims=True)
    return inverse * (
        centred_grad - scaled * jnp.mean(grad_scaled * scaled, axis=-1, keepdims=True)
    )


def gelu_parts(pre_act):
    tanh_val = jnp.tanh(gelu_coef * (pre_act + gelu_cube * pre_act * pre_act * pre_act))
    value_part = 0.5 * pre_act * (1.0 + tanh_val)
    slope_part = 0.5 * (1.0 + tanh_val) + 0.5 * pre_act * (
        1.0 - tanh_val * tanh_val
    ) * gelu_coef * (1.0 + 3.0 * gelu_cube * pre_act * pre_act)
    return value_part, slope_part


def on_device(
    tokens, cotangent, ln1_gain, ln1_shift, q_weight, q_bias, k_weight, v_weight, v_bias,
    o_weight, o_bias, ln2_gain, ln2_shift, in_weight, in_bias, out_weight, out_bias,
):
    part = lax.axis_index("seq")
    parts = lax.axis_size("seq")
    groups = lax.axis_size("dp")
    images, own_len, width = tokens.shape
    ff = in_weight.shape[1]
    hid = width // parts
    ffp = ff // parts
    heads = HEADS // parts
    length = own_len * parts
    rows = images * length

    def cols(w, n):
        return lax.dynamic_slice_in_dim(w, part * n, n, axis=1)

    vecs = jnp.stack(
        [ln1_gain, ln1_shift, q_bias, v_bias, o_bias, ln2_gain, ln2_shift, out_bias]
    )
    vecs = lax.all_gather(vecs, "dp", axis=1, tiled=True).astype(F32)
    g1, s1, qb, vb, ob, g2, s2, outb = [vecs[i] for i in range(8)]
    x = lax.all_gather(tokens, "seq", axis=1, tiled=True).reshape(rows, width)
    cot = lax.all_gather(cotangent, "seq", axis=1, tiled=True).reshape(rows, width)
    qkv = jnp.concatenate([cols(q_weight, hid), cols(k_weight, hid), cols(v_weight, hid)], axis=1)
    qkv = lax.all_gather(qkv, "dp", axis=0, tiled=True)
    o_w = lax.all_gather(o_weight, "dp", axis=0, tiled=True)
    o_w = lax.dynamic_slice_in_dim(o_w, part * hid, hid, axis=0)
    in_w = lax.all_gather(cols(in_weight, ffp), "dp", axis=0, tiled=True)
    out_w = lax.dynamic_slice_in_dim(out_weight, part * ffp, ffp, axis=0)
    out_w = lax.all_gather(out_w.T, "dp", axis=0, tiled=True)
    qb_own = lax.dynamic_slice_in_dim(qb, part * hid, hid)
    vb_own = lax.dynamic_slice_in_dim(vb, part * hid, hid)
    inb_own = lax.dynamic_slice_in_dim(in_bias, part * ffp, ffp).astype(F32)

    def scatter_tokens(partial):
        return lax.psum_scatter(
            partial.astype(BF16).reshape(images, length, width),
            "seq", scatter_dimension=1, tiled=True,
        ).astype(F32)

    hat1, _ = normalize(x.astype(F32))
    normed1 = (hat1 * g1 + s1).astype(BF16)
    proj = mm(normed1, qkv, 1, 0)
    queries = (proj[:, :hid] + qb_own).astype(BF16).reshape(images, length, heads, HEAD_DIM)
    keys = proj[:, hid : 2 * hid].astype(BF16).reshape(images, length, heads, HEAD_DIM)
    values = (proj[:, 2 * hid :] + vb_own).astype(BF16).reshape(images, length, heads, HEAD_DIM)
    factor = 1.0 / math.sqrt(HEAD_DIM)
    ein = lambda s, a, b: jnp.einsum(s, a, b, preferred_element_type=F32)
    scores = ein("iqhd,ikhd->ihqk", queries, keys) * factor
    top = jnp.max(scores, axis=-1, keepdims=True)
    expo = jnp.exp(scores - top)
    probs = expo / jnp.sum(expo, axis=-1, keepdims=True)
    probs_low = probs.astype(BF16)
    mixed = ein("ihqk,ikhd->iqhd", probs_low, values).astype(BF16).reshape(rows, hid)
    start = tokens.astype(F32)
    hidden = start + scatter_tokens(mm(mixed, o_w, 1, 0)) + ob
    hat2, r2 = normalize(hidden)
    normed2 = (hat2 * g2 + s2).astype(BF16)
    normed2 = lax.all_gather(normed2, "seq", axis=1, tiled=True).reshape(rows, width)
    pre = mm(normed2, in_w, 1, 0) + inb_own
    act, slope = gelu_parts(pre)
    act = act.astype(BF16)
    out = hidden + scatter_tokens(mm(act, out_w, 1, 1)) + outb
    d_out_w = mm(cot, act, 0, 0)
    cot_own = cotangent.astype(F32)
    grad_pre = (mm(cot, out_w, 1, 0) * slope).astype(BF16)
    d_in_w = mm(normed2, grad_pre, 0, 0)
    d_in_b = jnp.sum(grad_pre.astype(F32), axis=0)
    grad_n2 = scatter_tokens(mm(grad_pre, in_w, 1, 1))
    grad_hidden = cot_own + norm_back(grad_n2, g2, hat2, r2)
    branch_own = grad_hidden.astype(BF16)
    branch = lax.all_gather(branch_own, "seq", axis=1, tiled=True).reshape(rows, width)
    d_o_w = mm(mixed, branch, 0, 0)
    grad_mixed = mm(branch, o_w, 1, 1).astype(BF16).reshape(images, length, heads, HEAD_DIM)
    grad_probs = ein("iqhd,ikhd->ihqk", grad_mixed, values)
    row_dot = jnp.sum(probs * grad_probs, axis=-1, keepdims=True)
    grad_scores = (probs * (grad_probs - row_dot)).astype(BF16)
    grad_q = (ein("ihqk,ikhd->iqhd", grad_scores, keys) * factor).astype(BF16).reshape(rows, hid)
    grad_k = (ein("ihqk,iqhd->ikhd", grad_scores, queries) * factor).astype(BF16).reshape(rows, hid)
    grad_v = ein("ihqk,iqhd->ikhd", probs_low, grad_mixed).astype(BF16).reshape(rows, hid)
    grad_qkv = jnp.concatenate([grad_q, grad_k, grad_v], axis=1)
    d_qkv = mm(normed1, grad_qkv, 0, 0)
    d_qb = jnp.sum(grad_q.astype(F32), axis=0)
    d_vb = jnp.sum(grad_v.astype(F32), axis=0)
    grad_n1 = scatter_tokens(mm(grad_qkv, qkv, 1, 1))
    hat1o, r1o = normalize(start)
    grad_tokens = grad_hidden + norm_back(grad_n1, g1, hat1o, r1o)
    wide = jnp.concatenate([d_qkv, d_in_w, d_out_w], axis=1).astype(BF16)
    wide = lax.psum_scatter(wide, "dp", scatter_dimension=0, tiled=True)
    wide = lax.all_gather(wide, "seq", axis=0, tiled=False).astype(F32)

    def spread(lo, n):
        return wide[:, :, lo : lo + n].transpose(1, 0, 2).reshape(width // groups, n * parts)

    gq, gk, gv = [spread(i * hid, hid) for i in range(3)]
    gin = spread(3 * hid, ffp)
    gout = wide[:, :, 3 * hid + ffp :].transpose(0, 2, 1).reshape(ff, width // groups)
    o_full = lax.all_gather(
        lax.psum_scatter(d_o_w.astype(BF16), "dp", scatter_dimension=1, tiled=True),
        "seq", axis=0, tiled=True,
    )
    go = lax.all_to_all(o_full, "dp", split_axis=0, concat_axis=1, tiled=True).astype(F32)
    own_sums = jnp.stack([
        jnp.sum(grad_n1 * hat1o, axis=(0, 1)), jnp.sum(grad_n1, axis=(0, 1)),
        jnp.sum(grad_n2 * hat2, axis=(0, 1)), jnp.sum(grad_n2, axis=(0, 1)),
        jnp.sum(branch_own.astype(F32), axis=(0, 1)), jnp.sum(cot_own, axis=(0, 1)),
        lax.dynamic_update_slice_in_dim(jnp.zeros(width, F32), d_qb, part * hid, 0),
        lax.dynamic_update_slice_in_dim(jnp.zeros(width, F32), d_vb, part * hid, 0),
    ])
    bias_in = lax.dynamic_update_slice_in_dim(jnp.zeros(ff, F32), d_in_b, part * ffp, 0)
    total = lax.psum(jnp.concatenate([own_sums.reshape(-1), bias_in]), ("dp", "seq"))
    vec_part = total[: 8 * width].reshape(8, groups, width // groups)
    vec_part = lax.dynamic_index_in_dim(vec_part, lax.axis_index("dp"), axis=1, keepdims=False)
    bias_total = total[8 * width :]
    return (
        out.astype(BF16), grad_tokens.astype(BF16), vec_part[0], vec_part[1], gq, vec_part[6],
        gk, gv, vec_part[7], go, vec_part[4], vec_part[2], vec_part[3], gin, bias_total, gout,
        vec_part[5],
    )


def solution(mesh):
    rows, vec = P("dp", None), P("dp")
    tok = P("dp", "seq", None)
    return jax.shard_map(
        on_device,
        mesh=mesh,
        in_specs=(tok, tok, vec, vec, rows, vec, rows, rows, vec, rows, vec, vec, vec, rows,
                  P(), P(None, "dp"), vec),
        out_specs=(tok, tok, vec, vec, rows, vec, rows, rows, vec, rows, vec, vec, vec, rows,
                   P(), P(None, "dp"), vec),
        check_vma=False,
    )
```

time: 1510 us -> 761 us (0.50)
  blocking collectives: 416 us -> 74.6 us
  waiting for transfers between devices: 724 us -> 491 us
  matrix products: 187 us -> 53.9 us
  local copies, waits for them, and re-layouts: 118 us -> 89.6 us
    unnamed x34 -> x15, waiting for transfers between devices: 303 us -> 2.25 us
    unnamed x3 -> x0, blocking collectives: 291 us -> none
    reduce_scatter x4 -> x6, waiting for transfers between devices: 0.07 us -> 253 us  [the longest x1 114 us: on_device(): wide = lax.psum_scatter(wide, 'dp', scatter_dimension=0, tiled=True)]
    all_gather x8 -> x9, waiting for transfers between devices: 420 us -> 221 us  [the longest x1 55.8 us: on_device(): out_w = lax.all_gather(out_w.T, 'dp', axis=0, tiled=True)]
    dot_general x80 -> x17, matrix products: 187 us -> 51.7 us  [the longest x12 44.9 us: mm(): lax.dot_general(a, b, (((ca,), (cb,)), ((), ())), preferred_element_type=...]
    unnamed x288 -> x67, local copies, waits for them, and re-layouts: 74.4 us -> 13.1 us
    all_gather x8 -> x2, blocking collectives: 69.5 us -> 34.9 us  [the longest x1 25.4 us: on_device(): vecs = lax.all_gather(vecs, 'dp', axis=1, tiled=True).astype(F32)]
    concatenate x0 -> x2, local copies, waits for them, and re-layouts: none -> 29.5 us  [the longest x1 29.5 us: on_device(): wide = jnp.concatenate([d_qkv, d_in_w, d_out_w], axis=1).astype(BF16)]
  transfers between devices with their start and end apart: 24 -> 16, of which waited for: 18 -> 13; matrix products, arithmetic and copies ran while one was open for 32% -> 9% of each run, Pallas kernels for 0% -> 0%
where the time goes in v1:
time: 761 us; the launch traced here: 752 us
  waiting for transfers between devices  491 us (65%)
  local copies, waits for them, and re-layouts  89.6 us (12%)
  blocking collectives  74.6 us (10%)
  matrix products  53.9 us (7%)
  other arithmetic  23 us (3%)
  between operations  15.1 us (2%)
    reduce_scatter x1, waiting for transfers between devices, on_device(): wide = lax.psum_scatter(wide, 'dp', scatter_dimension=0, tiled=True)  114 us
    reduce_scatter x4, waiting for transfers between devices, scatter_tokens(): lax.psum_scatter(partial.astype(BF16).reshape(images, length, width), 'se...  75.5 us
    reduce_scatter x1, waiting for transfers between devices, on_device(): lax.psum_scatter(d_o_w.astype(BF16), 'dp', scatter_dimension=1, tiled=True)  63.3 us
    all_gather x1, waiting for transfers between devices, on_device(): out_w = lax.all_gather(out_w.T, 'dp', axis=0, tiled=True)  55.8 us
    all_gather x1, waiting for transfers between devices, on_device(): in_w = lax.all_gather(cols(in_weight, ffp), 'dp', axis=0, tiled=True)  48.2 us
    dot_general x12, matrix products, mm(): lax.dot_general(a, b, (((ca,), (cb,)), ((), ())), preferred_element_type=...  44.9 us
    all_gather x1, waiting for transfers between devices, on_device(): o_w = lax.all_gather(o_weight, 'dp', axis=0, tiled=True)  43.3 us
    psum x1, blocking collectives, on_device(): lax.psum(jnp.concatenate([own_sums.reshape(-1), bias_in]), ('dp', 'seq'))  39.8 us
  transfers between devices with their start and end apart: 16, of which 13 were waited for; matrix products, arithmetic and copies ran while one was open for 9% of the time, Pallas kernels for 0%

profile of v1, /device:TPU:1, one launch (start us, length us, event | category | flops | bytes accessed | tf_op | source)
XLA Modules:
  0.0 751.8 jit_solution(17912709824997006762)
XLA Ops:
  17.1 25.4 %all-gather.1 = bf16[8,144,8]{1,2,0:T(8,128)(2,1)S(1)} all-gather(bf16[1,144,8]{1,2,0:T(8,128)(2,1)S(1)} %bitcast.143), channel_id=1, replica_groups=mesh['dp'=8,'seq'=4] {'dp'}, dimensions={0}, use_global_device_ids=true | all-gather | bytes 20736 | tf_op jit(solution)/shard_map/all_gather | solution.py:67
  48.3 30.4 %all-gather.15.cloned.1.call-done = bf16[1152,864]{1,0:T(8,128)(2,1)} async-done(((bf16[144,864]{1,0:T(8,128)(2,1)}), bf16[1152,864]{1,0:T(8,128)(2,1)}) %all-gather.15.cloned.1.call-update) | async-done | bytes 1990672 | tf_op jit(solution)/shard_map/all_gather | solution.py:72
  91.5 43.3 %all-gather.17.cloned.1.call-done = bf16[1152,1152]{1,0:T(8,128)(2,1)} async-done(((bf16[144,1152]{1,0:T(8,128)(2,1)}), bf16[1152,1152]{1,0:T(8,128)(2,1)}) %all-gather.17.cloned.1.call-update) | async-done | bytes 2654224 | tf_op jit(solution)/shard_map/all_gather | solution.py:73
  138.9 24.7 %reduce-scatter.9.cloned.1.call-done = bf16[2,64,1152]{2,1,0:T(8,128)(2,1)} async-done(((bf16[2,256,1152]{2,1,0:T(8,128)(2,1)}), bf16[2,64,1152]{2,1,0:T(8,128)(2,1)}) %reduce-scatter.9.cloned.1.call-update) | async-done | bytes 294928 | tf_op jit(solution)/shard_map/reduce_scatter | solution.py:83
  171.6 48.2 %all-gather.21.cloned.1.call-done = bf16[1152,1076]{1,0:T(8,128)(2,1)} async-done(((bf16[144,1076]{1,0:T(8,128)(2,1)}), bf16[1152,1076]{1,0:T(8,128)(2,1)}) %all-gather.21.cloned.1.call-update) | async-done | bytes 2479120 | tf_op jit(solution)/shard_map/all_gather | solution.py:75
  219.8 20.0 %all-gather.19.cloned.1.call-done = bf16[2,256,1152]{2,1,0:T(8,128)(2,1)} async-done(((bf16[2,64,1152]{2,1,0:T(8,128)(2,1)}), bf16[2,256,1152]{2,1,0:T(8,128)(2,1)}) %all-gather.19.cloned.1.call-update) | async-done | bytes 1179664 | tf_op jit(solution)/shard_map/all_gather | solution.py:106
  239.8 5.1 convolution_add_fusion
  244.9 13.9 %all-gather.25.cloned.1.call-done = bf16[2,256,1152]{2,1,0:T(8,128)(2,1)} async-done(((bf16[2,64,1152]{2,1,0:T(8,128)(2,1)}), bf16[2,256,1152]{2,1,0:T(8,128)(2,1)}) %all-gather.25.cloned.1.call-update) | async-done | bytes 1179664 | tf_op jit(solution)/shard_map/all_gather | solution.py:70
  258.8 55.8 %all-gather.23.cloned.1.call-done = bf16[1152,1076]{1,0:T(8,128)(2,1)} async-done(((bf16[144,1076]{1,0:T(8,128)(2,1)}), bf16[1152,1076]{1,0:T(8,128)(2,1)}) %all-gather.23.cloned.1.call-update) | async-done | bytes 2479120 | tf_op jit(solution)/shard_map/all_gather | solution.py:77
  314.6 5.8 convert_reduce_fusion
  323.5 25.7 %reduce-scatter.13.cloned.1.call-done = bf16[2,64,1152]{2,1,0:T(8,128)(2,1)} async-done(((bf16[2,256,1152]{2,1,0:T(8,128)(2,1)}), bf16[2,64,1152]{2,1,0:T(8,128)(2,1)}) %reduce-scatter.13.cloned.1.call-update) | async-done | bytes 294928 | tf_op jit(solution)/shard_map/reduce_scatter | solution.py:83
  353.7 4.8 convolution_convert_fusion.1
  362.0 9.6 %all-gather.27.cloned.1.call-done = bf16[2,256,1152]{2,1,0:T(8,128)(2,1)} async-done(((bf16[2,64,1152]{2,1,0:T(8,128)(2,1)}), bf16[2,256,1152]{2,1,0:T(8,128)(2,1)}) %all-gather.27.cloned.1.call-update) | async-done | bytes 1179664 | tf_op jit(solution)/shard_map/all_gather | solution.py:119
  382.9 29.5 %concatenate.16 = bf16[1152,3016]{0,1:T(8,128)(2,1)} concatenate(bf16[1152,864]{0,1:T(8,128)(2,1)S(1)} %convolution_convert_fusion.2, bf16[1152,1076]{0,1:T(8,128)(2,1)} %convolution_convert_fusion.1, bf16[1152,1076]{0,1:T(8,128)(2,1)} %fusion.1), dimensions={1} | concatenate | bytes 13897728 | tf_op jit(solution)/shard_map/concatenate | solution.py:135
  412.4 10.4 %copy.125 = bf16[1152,3016]{1,0:T(8,128)(2,1)} copy(bf16[1152,3016]{0,1:T(8,128)(2,1)} %concatenate.16) | data formatting | bytes 13897728
  431.4 5.7 convolution_convert_fusion.5
  437.2 113.9 %reduce-scatter.19.cloned.1.call-done = bf16[144,3016]{1,0:T(8,128)(2,1)} async-done(((bf16[1152,3016]{1,0:T(8,128)(2,1)}), bf16[144,3016]{1,0:T(8,128)(2,1)}) %reduce-scatter.19.cloned.1.call-update) | async-done | bytes 868624 | tf_op jit(solution)/shard_map/reduce_scatter | solution.py:136
  551.2 63.3 %reduce-scatter.17.cloned.1.call-done = bf16[288,144]{0,1:T(8,128)(2,1)} async-done(((bf16[288,1152]{0,1:T(8,128)(2,1)}), bf16[288,144]{0,1:T(8,128)(2,1)}) %reduce-scatter.17.cloned.1.call-update) | async-done | bytes 82960 | tf_op jit(solution)/shard_map/reduce_scatter | solution.py:146
  614.5 9.5 %all-gather.2 = bf16[4,288,144]{1,2,0:T(8,128)(2,1)S(1)} all-gather(bf16[1,288,144]{1,2,0:T(8,128)(2,1)} %bitcast.142), channel_id=1, replica_groups=mesh['dp'=8,'seq'=4] {'seq'}, dimensions={0}, use_global_device_ids=true | all-gather | bytes 414720 | tf_op jit(solution)/shard_map/all_gather | solution.py:145
  630.4 14.5 %all-to-all-done = bf16[8,144,144]{1,2,0:T(8,128)(2,1)S(1)} async-done(((bf16[8,144,144]{1,2,0:T(8,128)(2,1)}), bf16[8,144,144]{1,2,0:T(8,128)(2,1)S(1)}, u32[]{:S(2)}, u32[]{:S(2)}) %all-to-all-start) | async-done | bytes 331808 | tf_op jit(solution)/shard_map/all_to_all | solution.py:149
  647.6 25.0 %reduce-scatter.11.cloned.1.call-done = bf16[2,64,1152]{2,1,0:T(8,128)(2,1)} async-done(((bf16[2,256,1152]{2,1,0:T(8,128)(2,1)}), bf16[2,64,1152]{2,1,0:T(8,128)(2,1)}) %reduce-scatter.11.cloned.1.call-update) | async-done | bytes 294928 | tf_op jit(solution)/shard_map/reduce_scatter | solution.py:83
  675.2 39.8 %psum.7 = f32[13520]{0:T(1024)S(1)} all-reduce(f32[13520]{0:T(1024)S(1)} %pad_maximum_fusion.1), channel_id=1, replica_groups=mesh['dp'=8,'seq'=4] {'dp','seq'}, use_global_device_ids=true, to_apply=%region_26.0 | all-reduce | flops 13520 | bytes 108160 | tf_op jit(solution)/shard_map/psum | solution.py:158
  728.4 4.3 copy.118
  736.6 4.4 copy.119
  (202 shorter events, 103.7 us)
Async XLA Ops:
  7.2 130.7 %copy-start = (bf16[144,4304]{1,0:T(8,128)(2,1)S(1)}, bf16[144,4304]{1,0:T(8,128)(2,1)}, u32[]{:S(2)}) copy-start(bf16[144,4304]{1,0:T(8,128)(2,1)} %param.30) | copy-start | bytes 3718660
  7.2 36.2 %all-gather.13.cloned.1.call-start = ((), (), s32[]{:S(2)}) async-start(), calls=%async_computation.7 | async-start | bytes 1474560 | tf_op jit(solution)/shard_map/all_gather | solution.py:69
  7.9 70.8 %all-gather.15.cloned.1.call-start = ((), (), s32[]{:S(2)}) async-start(), calls=%async_computation.8 | async-start | bytes 2322432 | tf_op jit(solution)/shard_map/all_gather | solution.py:72
  11.0 123.8 %all-gather.17.cloned.1.call-start = ((), (), s32[]{:S(2)}) async-start(), calls=%async_computation.9 | async-start | bytes 2985984 | tf_op jit(solution)/shard_map/all_gather | solution.py:73
  11.7 151.9 %reduce-scatter.9.cloned.1.call-start = ((), (), s32[]{:S(2)}) async-start(), calls=%async_computation.10 | async-start | bytes 1474560 | tf_op jit(solution)/shard_map/reduce_scatter | solution.py:83
  91.5 47.4 %copy-start.11 = (bf16[36,8,2,256]{3,1,2,0:T(8,128)(2,1)}, bf16[36,8,2,256]{3,1,2,0:T(8,128)(2,1)S(1)}, u32[]{:S(2)}) copy-start(bf16[36,8,2,256]{3,1,2,0:T(8,128)(2,1)S(1)} %copy.129) | copy-start | bytes 884740
  134.8 28.8 %copy-start.2 = (bf16[2,64,1152]{2,1,0:T(8,128)(2,1)S(1)}, bf16[2,64,1152]{2,1,0:T(8,128)(2,1)}, u32[]{:S(2)}) copy-start(bf16[2,64,1152]{2,1,0:T(8,128)(2,1)} %param.17) | copy-start | bytes 884740
  137.9 81.9 %all-gather.21.cloned.1.call-start = ((), (), s32[]{:S(2)}) async-start(), calls=%async_computation.12 | async-start | bytes 2985984 | tf_op jit(solution)/shard_map/all_gather | solution.py:75
  138.8 100.9 %all-gather.19.cloned.1.call-start = ((), (), s32[]{:S(2)}) async-start(), calls=%async_computation.11 | async-start | bytes 1474560 | tf_op jit(solution)/shard_map/all_gather | solution.py:106
  167.9 91.0 %all-gather.25.cloned.1.call-start = ((), (), s32[]{:S(2)}) async-start(), calls=%async_computation.15 | async-start | bytes 1474560 | tf_op jit(solution)/shard_map/all_gather | solution.py:70
  168.6 146.0 %all-gather.23.cloned.1.call-start = ((), (), s32[]{:S(2)}) async-start(), calls=%async_computation.13 | async-start | bytes 2985984 | tf_op jit(solution)/shard_map/all_gather | solution.py:77
  170.6 178.7 %reduce-scatter.13.cloned.1.call-start = ((), (), s32[]{:S(2)}) async-start(), calls=%async_computation.16 | async-start | bytes 1474560 | tf_op jit(solution)/shard_map/reduce_scatter | solution.py:83
  320.5 28.8 %copy-start.3 = (bf16[2,64,1152]{2,1,0:T(8,128)(2,1)S(1)}, bf16[2,64,1152]{2,1,0:T(8,128)(2,1)}, u32[]{:S(2)}) copy-start(bf16[2,64,1152]{2,1,0:T(8,128)(2,1)} %reduce-scatter.9.cloned.1.call-done) | copy-start | bytes 884740
  323.5 48.1 %all-gather.27.cloned.1.call-start = ((), (), s32[]{:S(2)}) async-start(), calls=%async_computation.17 | async-start | bytes 1474560 | tf_op jit(solution)/shard_map/all_gather | solution.py:119
  353.4 197.8 %reduce-scatter.19.cloned.1.call-start = ((), (), s32[]{:S(2)}) async-start(), calls=%async_computation.21 | async-start | bytes 7962624 | tf_op jit(solution)/shard_map/reduce_scatter | solution.py:136
  422.8 191.7 %reduce-scatter.17.cloned.1.call-start = ((), (), s32[]{:S(2)}) async-start(), calls=%async_computation.19 | async-start | bytes 995328 | tf_op jit(solution)/shard_map/reduce_scatter | solution.py:146
  426.9 219.3 %reduce-scatter.15.cloned.1.call-start = ((), (), s32[]{:S(2)}) async-start(), calls=%async_computation.18 | async-start | bytes 1474560 | tf_op jit(solution)/shard_map/reduce_scatter | solution.py:83
  431.1 241.5 %reduce-scatter.11.cloned.1.call-start = ((), (), s32[]{:S(2)}) async-start(), calls=%async_computation.14 | async-start | bytes 1474560 | tf_op jit(solution)/shard_map/reduce_scatter | solution.py:83
  437.2 279.1 %all-gather.29.cloned.1.call-start = ((), (), s32[]{:S(2)}) async-start(), calls=%async_computation.20 | async-start | bytes 4423680 | tf_op jit(solution)/shard_map/all_gather | solution.py:137
  625.5 19.5 %all-to-all-start = ((bf16[8,144,144]{1,2,0:T(8,128)(2,1)}), bf16[8,144,144]{1,2,0:T(8,128)(2,1)S(1)}, u32[]{:S(2)}, u32[]{:S(2)}) async-start(bf16[8,144,144]{1,2,0:T(8,128)(2,1)} %copy.116), calls=%async_computation.5 | async-start | bytes 1179648 | tf_op jit(solution)/shard_map/all_to_all | solution.py:149
  629.2 43.4 %copy-start.6 = (bf16[2,64,1152]{2,1,0:T(8,128)(2,1)S(1)}, bf16[2,64,1152]{2,1,0:T(8,128)(2,1)}, u32[]{:S(2)}) copy-start(bf16[2,64,1152]{2,1,0:T(8,128)(2,1)} %reduce-scatter.13.cloned.1.call-done) | copy-start | bytes 884740
  629.2 43.4 %copy-start.17 = (f32[1152]{0:T(1024)S(1)}, f32[1152]{0:T(1024)}, u32[]{:S(2)}) copy-start(f32[1152]{0:T(1024)} %get-tuple-element.60) | copy-start | bytes 13828
  629.2 43.4 %copy-start.19 = (f32[2,64]{1,0:T(2,128)S(1)}, f32[2,64]{1,0:T(2,128)}, u32[]{:S(2)}) copy-start(f32[2,64]{1,0:T(2,128)} %copy-done.18) | copy-start | bytes 1540
  629.2 43.4 %copy-start.21 = (f32[2,64]{1,0:T(2,128)S(1)}, f32[2,64]{1,0:T(2,128)}, u32[]{:S(2)}) copy-start(f32[2,64]{1,0:T(2,128)} %copy-done.20) | copy-start | bytes 1540
  (21 other events, 132.2 us)
Sparse Core Ops, SparseCore 0:
  9.6 19.8 all-gather.12
  32.2 46.4 all-gather.14
  81.0 53.8 all-gather.16
  138.0 25.5 reduce-scatter.8
  166.2 53.5 all-gather.20
  221.8 17.9 all-gather.18
  241.4 17.4 all-gather.24
  261.6 52.9 all-gather.22
  323.6 25.6 reduce-scatter.12
  353.5 17.9 all-gather.26
  422.9 128.2 reduce-scatter.18
  554.4 60.0 reduce-scatter.16
  617.6 26.2 reduce-scatter.14
  647.0 25.6 reduce-scatter.10
  674.0 31.6 all-gather.28

commit v2 on v1

--- a/solution.py
+++ b/solution.py
@@ -1,22 +1,20 @@
+import functools
 import math
 
 import jax
 import jax.numpy as jnp
 from jax import lax
+from jax.experimental import pallas as pl
+from jax.experimental.pallas import tpu as pltpu
 from jax.sharding import PartitionSpec as P
 
-HEADS = 16
-HEAD_DIM = 72
-
+BF16, F32 = jnp.bfloat16, jnp.float32
+HEADS, HEAD_DIM = 16, 72
 eps_norm = 1e-06
 gelu_coef = 0.7978845608028654
 gelu_cube = 0.044715
-F32 = jnp.float32
-BF16 = jnp.bfloat16
-
-
-def mm(a, b, ca, cb):
-    return lax.dot_general(a, b, (((ca,), (cb,)), ((), ())), preferred_element_type=F32)
+MESH = pl.DeviceIdType.MESH
+VEC = 8
 
 
 def normalize(values):
@@ -41,6 +39,785 @@
         1.0 - tanh_val * tanh_val
     ) * gelu_coef * (1.0 + 3.0 * gelu_cube * pre_act * pre_act)
     return value_part, slope_part
+
+
+def dot(a, b, ca, cb):
+    return lax.dot_general(a, b, (((ca,), (cb,)), ((), ())), preferred_element_type=F32)
+
+
+def layer_kernel(
+    nz, hid, ffp,
+    wp, ow_own, tok, cot_in, inb,
+    out_ref, gtok_ref, fgrad, ograd, ibgrad,
+    w, ow, xall, call, n1, n2, gb, qkv, probs, mix, act, slope, gp, part, part2, r1, r1b,
+    dx, dy, rx, ry, dxb, dyb, rxb, ryb, hid_s, hat2_s, inv2_s, gh_s, n2own, gbown, vecs, g, rb, rbo, gin_tail,
+    gout_tail, dqkv, vsum, ibx, isb, og,
+    gy_s, gzr_s, gzl_s, g_r, o_s, o_r, ag_s, ag_r, rs_s, rs_r, z_s, z_r, zo_s, zo_r, f_s, f_r,
+    ib_s, ib_r,
+):
+    d, s = lax.axis_index("dp"), lax.axis_index("seq")
+    z, y = d // 2, d % 2
+    x, c = s // 2, s % 2
+    rank = 2 * s + y
+    own_len = tok.shape[1]
+    nimg, length, width = xall.shape
+    rows8 = wp.shape[1]
+    plane = 2 * rows8
+    cols = 512
+    qw = hid
+    in_at = VEC + 3 * qw
+    in_win = in_at // 128 * 128
+    out_at = in_at + ffp
+    out_win = out_at // 128 * 128
+    win = (ffp + 127) // 128 * 128
+    off_in, off_out = in_at - in_win, out_at - out_win
+    shift = off_out - off_in
+    core_n, x_n, y_n = (d, s + 1 - 2 * c), (d, (s + 2) % 4), (d + 1 - 2 * y, s)
+    right, left = (d + 2, s), (d - 2, s)
+    has_r, has_l = z < nz - 1, z > 0
+    factor = 1.0 / math.sqrt(HEAD_DIM)
+
+    def rc(src, dst, ss, rs, dev):
+        return pltpu.make_async_remote_copy(
+            src_ref=src, dst_ref=dst, send_sem=ss, recv_sem=rs, device_id=dev, device_id_type=MESH
+        )
+
+    barrier = pltpu.get_barrier_semaphore()
+    for dev in (core_n, x_n, y_n):
+        pl.semaphore_signal(barrier, inc=1, device_id=dev, device_id_type=MESH)
+    pl.when(has_r)(lambda: pl.semaphore_signal(barrier, inc=1, device_id=right, device_id_type=MESH))
+    pl.when(has_l)(lambda: pl.semaphore_signal(barrier, inc=1, device_id=left, device_id_type=MESH))
+    beside = (z + nz - 2) // (nz - 1) + (2 * nz - 3 - z) // (nz - 1)
+    pl.semaphore_wait(barrier, 3 + beside)
+
+    def wrows(origin, sub):
+        return pl.ds(pl.multiple_of(origin * plane + sub * rows8, 16), rows8)
+
+    def wslab(ch, origin, sub):
+        return w.at[wrows(origin, sub), pl.ds(ch * cols, cols)]
+
+    def wsend(ch, origin, sub, src, to_right):
+        sems = gzr_s if to_right else gzl_s
+        return rc(src, wslab(ch, origin, sub), sems.at[ch, origin, sub], g_r.at[ch, origin, sub],
+                  right if to_right else left)
+
+    def wrecv(ch, origin, sub):
+        slab = wslab(ch, origin, sub)
+        rc(slab, slab, g_r.at[ch, origin, sub], g_r.at[ch, origin, sub], core_n).wait_recv()
+
+    def gather_own(ch):
+        src = wp.at[y, :, pl.ds(ch * cols, cols)]
+        pl.when(has_r)(lambda: wsend(ch, z, y, src, True).start())
+        pl.when(has_l)(lambda: wsend(ch, z, y, src, False).start())
+        w[wrows(z, y), ch * cols : (ch + 1) * cols] = wp[y, :, ch * cols : (ch + 1) * cols]
+
+    def gather_swap(ch):
+        rc(wp.at[1 - y, :, pl.ds(ch * cols, cols)], wslab(ch, z, y), gy_s.at[ch], g_r.at[ch, z, y],
+           y_n).start()
+
+    def gather_other(ch):
+        wrecv(ch, z, 1 - y)
+        src = wslab(ch, z, 1 - y)
+        pl.when(has_r)(lambda: wsend(ch, z, 1 - y, src, True).start())
+        pl.when(has_l)(lambda: wsend(ch, z, 1 - y, src, False).start())
+
+    def gather_hop(ch, k):
+        def from_left():
+            for sub in range(2):
+                wrecv(ch, z - k, sub)
+                pl.when(has_r)(lambda: wsend(ch, z - k, sub, wslab(ch, z - k, sub), True).start())
+
+        def from_right():
+            for sub in range(2):
+                wrecv(ch, z + k, sub)
+                pl.when(has_l)(lambda: wsend(ch, z + k, sub, wslab(ch, z + k, sub), False).start())
+
+        pl.when(z - k >= 0)(from_left)
+        pl.when(z + k < nz)(from_right)
+
+    def gather_drain(ch):
+        for k in range(nz):
+            for sub in range(2):
+                pl.when((z - k >= 0) & has_r)(
+                    lambda: wsend(ch, z - k, sub, wslab(ch, z - k, sub), True).wait_send())
+                pl.when((z + k < nz) & has_l)(
+                    lambda: wsend(ch, z + k, sub, wslab(ch, z + k, sub), False).wait_send())
+        rc(wp.at[1 - y, :, pl.ds(ch * cols, cols)], wslab(ch, z, y), gy_s.at[ch], g_r.at[ch, z, y],
+           y_n).wait_send()
+
+    def osend(to_right):
+        return rc(ow, ow, o_s.at[0 if to_right else 1], o_r.at[0], right if to_right else left)
+
+    def o_own():
+        def go():
+            ow[...] = ow_own[...]
+            pl.when(has_r)(lambda: rc(ow_own, ow, o_s.at[0], o_r.at[0], right).start())
+            pl.when(has_l)(lambda: rc(ow_own, ow, o_s.at[1], o_r.at[0], left).start())
+        pl.when(z == s)(go)
+
+    def o_pass():
+        def go():
+            rc(ow, ow, o_r.at[0], o_r.at[0], core_n).wait_recv()
+            pl.when((z > s) & has_r)(lambda: osend(True).start())
+            pl.when((z < s) & has_l)(lambda: osend(False).start())
+        pl.when(z != s)(go)
+
+    def o_drain():
+        pl.when((z >= s) & has_r)(lambda: osend(True).wait_send())
+        pl.when((z <= s) & has_l)(lambda: osend(False).wait_send())
+
+    def agather(inst, dst):
+        ss, rr = ag_s.at[inst], ag_r.at[inst]
+
+        def blk(yy, sq, i):
+            return dst.at[2 * yy + i, pl.ds(pl.multiple_of(sq * own_len, 16), own_len)]
+
+        sx, sp = (s + 2) % 4, s + 1 - 2 * c
+        spx = (sp + 2) % 4
+
+        def msg(n, block, dev):
+            return rc(block, block, ss.at[n], rr.at[n], dev)
+
+        mine = [blk(y, s, i) for i in range(2)]
+        xs = [blk(y, sx, i) for i in range(2)]
+        ys = [blk(1 - y, s, i) for i in range(2)]
+        dg = [blk(1 - y, sx, i) for i in range(2)]
+        sends = [msg(0, mine[0], x_n), msg(1, mine[1], x_n), msg(2, ys[1], x_n),
+                 msg(3, mine[0], y_n), msg(4, mine[1], y_n), msg(5, xs[0], y_n)]
+        sends += [msg(6 + i, mine[i], core_n) for i in range(2)]
+        sends += [msg(8 + i, xs[i], core_n) for i in range(2)]
+        sends += [msg(10 + i, ys[i], core_n) for i in range(2)]
+        sends += [msg(12 + i, dg[i], core_n) for i in range(2)]
+        recvs = [msg(0, xs[0], x_n), msg(1, xs[1], x_n), msg(2, dg[1], x_n),
+                 msg(3, ys[0], y_n), msg(4, ys[1], y_n), msg(5, dg[0], y_n)]
+        recvs += [msg(6 + i, blk(y, sp, i), core_n) for i in range(2)]
+        recvs += [msg(8 + i, blk(y, spx, i), core_n) for i in range(2)]
+        recvs += [msg(10 + i, blk(1 - y, sp, i), core_n) for i in range(2)]
+        recvs += [msg(12 + i, blk(1 - y, spx, i), core_n) for i in range(2)]
+
+        def begin():
+            for n in (0, 4, 1, 3, 6, 7):
+                sends[n].start()
+
+        def relay():
+            recvs[0].wait_recv()
+            sends[5].start()
+            recvs[4].wait_recv()
+            sends[2].start()
+            sends[8].start()
+            sends[11].start()
+            recvs[1].wait_recv()
+            sends[9].start()
+            recvs[3].wait_recv()
+            sends[10].start()
+
+        def finish():
+            recvs[2].wait_recv()
+            sends[13].start()
+            recvs[5].wait_recv()
+            sends[12].start()
+            for n in range(6, 14):
+                recvs[n].wait_recv()
+
+        def drain():
+            for m in sends:
+                m.wait_send()
+
+        return begin, relay, finish, drain
+
+    def rscatter(inst, pt, ra, bufs, produce):
+        bdx, bdy, brx, bry = bufs
+        ss, rr = rs_s.at[inst], rs_r.at[inst]
+        xo = 1 - x
+
+        def image(it):
+            return (2 * (1 - y) + it) % 4
+
+        def rows(xx, cc):
+            return pl.ds(pl.multiple_of((2 * xx + cc) * own_len, 16), own_len)
+
+        def swap(it, xx):
+            img = image(it)
+            return rc(pt.at[img, rows(xx, 1 - c)], ra.at[img, xx], ss.at[2 * it + xx],
+                      rr.at[2 * it + xx], core_n)
+
+        def run():
+            def step(it, carry):
+                produce(image(it))
+                swap(it, xo).start()
+                swap(it, x).start()
+                return carry
+            lax.fori_loop(0, nimg, step, 0)
+
+            def add(it, xx):
+                swap(it, xx).wait_recv()
+                img = image(it)
+                ra[img, xx] = (ra[img, xx].astype(F32) + pt[img, rows(xx, c)].astype(F32)).astype(BF16)
+                return ra.at[img, xx]
+
+            msgs = [
+                (8, lambda: rc(ra.at[image(0), xo], bdx, ss.at[8], rr.at[8], x_n)),
+                (9, lambda: rc(ra.at[image(1), xo], bdy, ss.at[9], rr.at[9], y_n)),
+                (10, lambda: rc(ra.at[image(1), x], bry.at[1], ss.at[10], rr.at[10], y_n)),
+                (11, lambda: rc(ra.at[image(2), xo], brx.at[0], ss.at[11], rr.at[11], x_n)),
+                (12, lambda: rc(ra.at[image(0), x], bry.at[0], ss.at[12], rr.at[12], y_n)),
+                (13, lambda: rc(ra.at[image(3), xo], brx.at[1], ss.at[13], rr.at[13], x_n)),
+            ]
+            m = [f() for _, f in msgs]
+            add(0, xo)
+            m[0].start()
+            add(1, xo)
+            m[1].start()
+            add(1, x)
+            m[2].start()
+            add(2, xo)
+            m[3].start()
+            add(0, x)
+            add(3, xo)
+            m[0].wait_recv()
+            ra[image(0), x] = (ra[image(0), x].astype(F32) + bdx[...].astype(F32)).astype(BF16)
+            m[4].start()
+            m[1].wait_recv()
+            ra[image(3), xo] = (ra[image(3), xo].astype(F32) + bdy[...].astype(F32)).astype(BF16)
+            m[5].start()
+            add(2, x)
+            add(3, x)
+
+        def result(i):
+            rc(brx.at[i], brx.at[i], ss.at[11 + 2 * i], rr.at[11 + 2 * i], x_n).wait_recv()
+            rc(bry.at[i], bry.at[i], ss.at[12 - 2 * i], rr.at[12 - 2 * i], y_n).wait_recv()
+            return (ra[image(2 + i), x].astype(F32) + brx[i].astype(F32)) + bry[i].astype(F32)
+
+        def drain():
+            for it in range(nimg):
+                swap(it, 0).wait_send()
+                swap(it, 1).wait_send()
+            for n in range(8, 14):
+                rc(bdx, bdx, ss.at[n], rr.at[n], x_n).wait_send()
+
+        return run, result, drain
+
+    gather_swap(0)
+    gather_own(0)
+    o_own()
+    ag_x = agather(0, xall)
+    ag_c = agather(1, call)
+    for i in range(2):
+        xall[2 * y + i, pl.ds(pl.multiple_of(s * own_len, 16), own_len)] = tok[i]
+        call[2 * y + i, pl.ds(pl.multiple_of(s * own_len, 16), own_len)] = cot_in[i]
+    ag_x[0]()
+    gather_other(0)
+    ag_x[1]()
+    gather_hop(0, 1)
+    gather_swap(1)
+    gather_swap(2)
+    ag_c[0]()
+    ag_x[2]()
+    gather_hop(0, 2)
+    o_pass()
+    gather_own(1)
+    gather_other(1)
+    ag_c[1]()
+    ag_c[2]()
+    gather_hop(0, 3)
+
+    lane = lax.broadcasted_iota(jnp.int32, (1, cols), 1)
+    vt = jnp.transpose(w[:, 0:128].astype(F32), (1, 0))
+    vecs[...] = vt[0:8]
+    qb = pltpu.roll(vecs[...], (VEC - rank * qw + width) % width, 1)[2:3, :cols]
+    vb = pltpu.roll(vecs[...], (VEC + 2 * qw - rank * qw + width) % width, 1)[3:4, :cols]
+    qkv_bias = jnp.where((lane >= VEC) & (lane < VEC + qw), qb, 0.0) + jnp.where(
+        (lane >= VEC + 2 * qw) & (lane < VEC + 3 * qw), vb, 0.0)
+    g1, s1 = vecs[0:1], vecs[1:2]
+    o_b, g2, s2, out_b = vecs[4:5], vecs[5:6], vecs[6:7], vecs[7:8]
+
+    def ln1_step(b, carry):
+        img, r = b // 4, pl.ds(pl.multiple_of((b % 4) * 64, 64), 64)
+        hat, _ = normalize(xall[img, r].astype(F32))
+        n1[img, r] = (hat * g1 + s1).astype(BF16)
+        return carry
+    lax.fori_loop(0, 4 * nimg, ln1_step, 0)
+
+    def att_step(img, carry):
+        proj = dot(n1[img], w[:, 0:cols], 1, 0) + qkv_bias
+        proj = proj.astype(BF16)
+        qkv[img] = proj
+        outs = []
+        for h in range(2):
+            at = VEC + h * HEAD_DIM
+            q = proj[:, at : at + HEAD_DIM]
+            k = proj[:, qw + at : qw + at + HEAD_DIM]
+            v = proj[:, 2 * qw + at : 2 * qw + at + HEAD_DIM]
+            sc = dot(q, k, 1, 1) * factor
+            e = jnp.exp(sc - jnp.max(sc, axis=-1, keepdims=True))
+            p = e / jnp.sum(e, axis=-1, keepdims=True)
+            probs[img, h] = p
+            outs.append(dot(p.astype(BF16), v, 1, 0).astype(BF16))
+        mix[img] = jnp.concatenate(outs, axis=1)
+        return carry
+    lax.fori_loop(0, nimg, att_step, 0)
+
+    gather_hop(1, 1)
+    gather_own(2)
+    gather_other(2)
+    gather_hop(1, 2)
+
+    def o_part(img):
+        part[img] = dot(mix[img], ow[...], 1, 0).astype(BF16)
+
+    rs_h = rscatter(0, part, r1, (dx, dy, rx, ry), o_part)
+    rs_h[0]()
+    rs_h[2]()
+    ag_n = agather(2, n2)
+    for i in range(2):
+        hidden = tok[i].astype(F32) + rs_h[1](i) + o_b
+        hid_s[i] = hidden
+        hat, inv = normalize(hidden)
+        hat2_s[i] = hat
+        inv2_s[i] = jnp.broadcast_to(inv, (own_len, 128))
+        n2[2 * y + i, pl.ds(pl.multiple_of(s * own_len, 16), own_len)] = (hat * g2 + s2).astype(BF16)
+    ag_n[0]()
+    gather_hop(1, 3)
+    gather_hop(2, 1)
+    ag_n[1]()
+    ag_n[2]()
+    gather_hop(2, 2)
+
+    wlane = lax.broadcasted_iota(jnp.int32, (1, win), 1)
+    valid = (wlane >= off_out) & (wlane < off_out + ffp)
+
+    def in_step(img, carry):
+        pre = dot(n2[img], w[:, in_win : in_win + win], 1, 0) + inb[0:1]
+        a, sl = gelu_parts(pre)
+        act[img] = jnp.where(valid, pltpu.roll(a, shift, 1), 0.0).astype(BF16)
+        slope[img] = jnp.where(valid, pltpu.roll(sl, shift, 1), 0.0)
+        return carry
+    lax.fori_loop(0, nimg, in_step, 0)
+
+    def rb_at(ch, slot, sub):
+        return rb.at[ch, slot, sub]
+
+    def gslab(ch, dest, sub):
+        return g.at[wrows(dest, sub), pl.ds(ch * cols, cols)]
+
+    def zsend(ch, k, sub, to_right):
+        dest = z + k if to_right else z - k
+        slot = nz if k == 1 and not to_right else dest
+        return rc(gslab(ch, dest, sub), rb_at(ch, slot, sub), z_s.at[ch, dest, sub], z_r.at[ch, slot, sub],
+                  right if to_right else left)
+
+    def zadd(ch, dest, slot, sub):
+        rc(rb_at(ch, slot, sub), rb_at(ch, slot, sub), z_r.at[ch, slot, sub], z_r.at[ch, slot, sub],
+           core_n).wait_recv()
+        r, cs = wrows(dest, sub), slice(ch * cols, (ch + 1) * cols)
+        g[r, cs] = (g[r, cs].astype(F32) + rb[ch, slot, sub].astype(F32)).astype(BF16)
+
+    def zreduce_hop(ch, k):
+        def to_right():
+            for sub in range(2):
+                pl.when(has_l)(lambda: zadd(ch, z + k, z + k, sub))
+                zsend(ch, k, sub, True).start()
+
+        def to_left():
+            for sub in range(2):
+                pl.when(has_r)(lambda: zadd(ch, z - k, z - k, sub))
+                zsend(ch, k, sub, False).start()
+
+        pl.when(z + k < nz)(to_right)
+        pl.when(z - k >= 0)(to_left)
+
+    def zreduce_own(ch):
+        for sub in range(2):
+            pl.when(has_l)(lambda: zadd(ch, z, z, sub))
+            pl.when(has_r)(lambda: zadd(ch, z, nz, sub))
+
+    def zdrain(ch):
+        for k in range(1, nz):
+            for sub in range(2):
+                pl.when(z + k < nz)(lambda: zsend(ch, k, sub, True).wait_send())
+                pl.when(z - k >= 0)(lambda: zsend(ch, k, sub, False).wait_send())
+
+    def fslot(ch, first, n):
+        return fgrad.at[pl.ds(first, n), :, pl.ds(ch * cols, cols)]
+
+    def f_swap(ch):
+        src = g.at[wrows(z, 1 - y), pl.ds(ch * cols, cols)]
+        return rc(src, fgrad.at[rank, :, pl.ds(ch * cols, cols)], f_s.at[ch, 0], f_r.at[ch, 0], y_n)
+
+    def f_msg(ch, n, first, dev):
+        return rc(fslot(ch, first, 2), fslot(ch, first, 2), f_s.at[ch, n], f_r.at[ch, n], dev)
+
+    def f_begin(ch):
+        f_swap(ch).start()
+        fgrad[rank, :, ch * cols : (ch + 1) * cols] = g[wrows(z, y), ch * cols : (ch + 1) * cols]
+
+    def f_spread(ch):
+        other = fgrad.at[2 * s + 1 - y, :, pl.ds(ch * cols, cols)]
+        rc(other, other, f_s.at[ch, 0], f_r.at[ch, 0], y_n).wait_recv()
+        f_msg(ch, 1, 2 * s, x_n).start()
+        f_msg(ch, 2, 2 * s, core_n).start()
+
+    def f_relay(ch):
+        sx = (s + 2) % 4
+        f_msg(ch, 1, 2 * sx, x_n).wait_recv()
+        f_msg(ch, 3, 2 * sx, core_n).start()
+
+    def f_end(ch):
+        sp = s + 1 - 2 * c
+        f_msg(ch, 2, 2 * sp, core_n).wait_recv()
+        f_msg(ch, 3, 2 * ((sp + 2) % 4), core_n).wait_recv()
+        f_swap(ch).wait_send()
+        for n in (1, 2, 3):
+            f_msg(ch, n, 0, core_n).wait_send()
+
+    rtile = width // 3
+
+    def gout_step(t, carry):
+        r = pl.ds(pl.multiple_of(t * rtile, rtile), rtile)
+        acc = jnp.zeros((rtile, win), F32)
+        for img in range(nimg):
+            acc = acc + dot(call[img, :, r], act[img], 0, 0)
+        gout_tail[r] = acc[:, 0 : 2 * cols - out_win].astype(BF16)
+        g[r, 2 * cols : 3 * cols] = acc[:, 2 * cols - out_win :].astype(BF16)
+        return carry
+    lax.fori_loop(0, 3, gout_step, 0)
+    for k in range(nz - 1, 0, -1):
+        pl.when(z == 0)(lambda: zreduce_hop(2, k))
+        pl.when(z == nz - 1)(lambda: zreduce_hop(2, k))
+    gather_hop(2, 3)
+
+    def out_part(img):
+        part2[img] = dot(act[img], w[:, out_win : out_win + win], 1, 1).astype(BF16)
+
+    rs_o = rscatter(1, part2, r1b, (dxb, dyb, rxb, ryb), out_part)
+
+    def gp_step(img, carry):
+        ga = dot(call[img], w[:, out_win : out_win + win], 1, 0) * slope[img]
+        ga = pltpu.roll(ga, win - shift, 1)
+        gp[img] = ga.astype(BF16)
+        return carry
+    lax.fori_loop(0, nimg, gp_step, 0)
+
+    ib = jnp.zeros((1, win), F32)
+    for img in range(nimg):
+        ib = ib + jnp.sum(gp[img].astype(F32), axis=0, keepdims=True)
+    isb[0] = jnp.broadcast_to(ib, (8, win))
+
+    def gn2_part(img):
+        part[img] = dot(gp[img], w[:, in_win : in_win + win], 1, 1).astype(BF16)
+
+    rs_g2 = rscatter(2, part, r1, (dx, dy, rx, ry), gn2_part)
+    rs_g2[0]()
+
+    def gin_step(t, carry):
+        r = pl.ds(pl.multiple_of(t * rtile, rtile), rtile)
+        acc = jnp.zeros((rtile, win), F32)
+        for img in range(nimg):
+            acc = acc + dot(n2[img, :, r], gp[img], 0, 0)
+        lo = cols - in_win
+        gin_tail[r] = acc[:, 0:lo].astype(BF16)
+        g[r, cols : 2 * cols - 128] = acc[:, lo : win - 128].astype(BF16)
+        g[r, 2 * cols - 128 : 2 * cols] = (acc[:, win - 128 :] + gout_tail[r].astype(F32)).astype(BF16)
+        return carry
+    lax.fori_loop(0, 3, gin_step, 0)
+
+    def z_middle(ch, k):
+        pl.when((z > 0) & (z < nz - 1))(lambda: zreduce_hop(ch, k))
+
+    def z_ends(ch):
+        for k in range(nz - 1, 0, -1):
+            pl.when((z == 0) | (z == nz - 1))(lambda: zreduce_hop(ch, k))
+
+    z_ends(1)
+    sums = [jnp.zeros((1, width), F32) for _ in range(6)]
+    ag_g = agather(3, gb)
+    for i in range(2):
+        gn2 = rs_g2[1](i)
+        hat = hat2_s[i]
+        sums[2] = sums[2] + jnp.sum(gn2 * hat, axis=0, keepdims=True)
+        sums[3] = sums[3] + jnp.sum(gn2, axis=0, keepdims=True)
+        up = cot_in[i].astype(F32)
+        gh = up + norm_back(gn2, g2, hat, inv2_s[i][:, 0:1])
+        gh_s[i] = gh
+        low = gh.astype(BF16)
+        gb[2 * y + i, pl.ds(pl.multiple_of(s * own_len, 16), own_len)] = low
+        sums[4] = sums[4] + jnp.sum(low.astype(F32), axis=0, keepdims=True)
+        sums[5] = sums[5] + jnp.sum(up, axis=0, keepdims=True)
+    rs_g2[2]()
+    ag_g[0]()
+    z_middle(2, 2)
+    z_middle(2, 1)
+    ag_g[1]()
+    rs_o[0]()
+    ag_g[2]()
+    zreduce_own(2)
+    f_begin(2)
+    z_middle(1, 2)
+    z_middle(1, 1)
+
+    def attb_step(img, carry):
+        proj, gbi = qkv[img], gb[img]
+        gmix = dot(gbi, ow[...], 1, 1).astype(BF16)
+        zero = jnp.zeros((length, VEC), BF16)
+        dq, dk, dv = [], [], []
+        for h in range(2):
+            at = VEC + h * HEAD_DIM
+            q = proj[:, at : at + HEAD_DIM]
+            k = proj[:, qw + at : qw + at + HEAD_DIM]
+            v = proj[:, 2 * qw + at : 2 * qw + at + HEAD_DIM]
+            gm = gmix[:, h * HEAD_DIM : (h + 1) * HEAD_DIM]
+            p = probs[img, h]
+            gpr = dot(gm, v, 1, 1)
+            gs = (p * (gpr - jnp.sum(p * gpr, axis=-1, keepdims=True))).astype(BF16)
+            dq.append((dot(gs, k, 1, 0) * factor).astype(BF16))
+            dk.append((dot(gs, q, 0, 0) * factor).astype(BF16))
+            dv.append(dot(p.astype(BF16), gm, 0, 0).astype(BF16))
+        pad = jnp.zeros((length, cols - VEC - 3 * qw), BF16)
+        dqkv[img] = jnp.concatenate([zero] + dq + dk + dv + [pad], axis=1)
+        return carry
+    lax.fori_loop(0, nimg, attb_step, 0)
+
+    vsum[0:2] = jnp.zeros((2, width), F32)
+
+    def gn1_part(img):
+        pr = dot(dqkv[img], w[:, 0:cols], 1, 1)
+        hat, _ = normalize(xall[img].astype(F32))
+        vsum[0:1] = vsum[0:1] + jnp.sum(pr * hat, axis=0, keepdims=True)
+        vsum[1:2] = vsum[1:2] + jnp.sum(pr, axis=0, keepdims=True)
+        part[img] = pr.astype(BF16)
+
+    rs_g1 = rscatter(3, part, r1, (dx, dy, rx, ry), gn1_part)
+    rs_g1[0]()
+    for n in range(2, 6):
+        vsum[n : n + 1] = sums[n]
+    vsum[6:8] = jnp.zeros((2, width), F32)
+
+    def gqkv_step(t, carry):
+        r = pl.ds(pl.multiple_of(t * rtile, rtile), rtile)
+        acc = jnp.zeros((rtile, cols), F32)
+        for img in range(nimg):
+            acc = acc + dot(n1[img, :, r], dqkv[img], 0, 0)
+        vcol = jnp.transpose(jnp.concatenate([vsum[:, r], jnp.zeros((120, rtile), F32)], axis=0), (1, 0))
+        g[r, 0:128] = (acc[:, 0:128] + vcol).astype(BF16)
+        g[r, 128 : cols - 128] = acc[:, 128 : cols - 128].astype(BF16)
+        g[r, cols - 128 : cols] = (acc[:, cols - 128 :] + gin_tail[r].astype(F32)).astype(BF16)
+        return carry
+    lax.fori_loop(0, 3, gqkv_step, 0)
+    z_ends(0)
+
+    gacc = jnp.zeros((qw, width), F32)
+    for img in range(nimg):
+        gacc = gacc + dot(mix[img], gb[img], 0, 0)
+    og[0:qw] = gacc.astype(BF16)
+    bsum = jnp.zeros((1, cols), F32)
+    for img in range(nimg):
+        bsum = bsum + jnp.sum(dqkv[img].astype(F32), axis=0, keepdims=True)
+    og[qw:, 0:cols] = jnp.broadcast_to(bsum, (16, cols)).astype(BF16)
+    og[qw:, cols:] = jnp.zeros((16, width - cols), BF16)
+
+    def zo_send(to_right):
+        n = 0 if to_right else 1
+        return rc(og, rbo.at[n], zo_s.at[n], zo_r.at[n], right if to_right else left)
+
+    def zo_add(n):
+        rc(rbo.at[n], rbo.at[n], zo_s.at[n], zo_r.at[n], core_n).wait_recv()
+        og[...] = (og[...].astype(F32) + rbo[n].astype(F32)).astype(BF16)
+
+    pl.when((z == 0) & (z < s))(lambda: zo_send(True).start())
+    pl.when((z == nz - 1) & (z > s))(lambda: zo_send(False).start())
+
+    def ib_send(to_right):
+        n = 0 if to_right else 1
+        return rc(isb.at[1 + n], ibx.at[n], ib_s.at[n], ib_r.at[n], right if to_right else left)
+
+    def ib_recv(n):
+        rc(ibx.at[n], ibx.at[n], ib_s.at[n], ib_r.at[n], core_n).wait_recv()
+
+    def ib_first():
+        isb[1] = isb[0]
+        isb[2] = isb[0]
+    ib_first()
+    pl.when(z == 0)(lambda: ib_send(True).start())
+    pl.when(z == nz - 1)(lambda: ib_send(False).start())
+
+    f_spread(2)
+    zreduce_own(1)
+    f_begin(1)
+    f_relay(2)
+    z_middle(0, 2)
+    z_middle(0, 1)
+
+    def zo_mid_r():
+        zo_add(0)
+        zo_send(True).start()
+
+    def zo_mid_l():
+        zo_add(1)
+        zo_send(False).start()
+    pl.when((z > 0) & (z < s))(zo_mid_r)
+    pl.when((z < nz - 1) & (z > s))(zo_mid_l)
+
+    def ib_mid(n):
+        ib_recv(n)
+        isb[1 + n] = isb[0] + ibx[n]
+        pl.when((has_r if n == 0 else has_l))(lambda: ib_send(n == 0).start())
+    pl.when(has_l)(lambda: ib_mid(0))
+    pl.when(has_r)(lambda: ib_mid(1))
+
+    for i in range(2):
+        gn1 = rs_g1[1](i)
+        hat, inv = normalize(tok[i].astype(F32))
+        gtok_ref[i] = (gh_s[i] + norm_back(gn1, g1, hat, inv)).astype(BF16)
+        out_ref[i] = (hid_s[i] + rs_o[1](i) + out_b).astype(BF16)
+
+    f_spread(1)
+
+    def o_here():
+        pl.when(has_l)(lambda: zo_add(0))
+        pl.when(has_r)(lambda: zo_add(1))
+        ograd[...] = og[...]
+        rc(ograd, ograd, zo_s.at[2], zo_r.at[2], x_n).start()
+        rc(ograd, ograd, zo_s.at[3], zo_r.at[3], core_n).start()
+    pl.when(z == s)(o_here)
+
+    isb[0] = (isb[1] + isb[2]) - isb[0]
+    ibgrad[rank] = isb[0]
+    rc(isb.at[0], ibgrad.at[rank], ib_s.at[2], ib_r.at[2], y_n).start()
+    rc(isb.at[0], ibgrad.at[2 * s + 1 - y], ib_s.at[2], ib_r.at[2], y_n).wait_recv()
+
+    def ib_two(n, first, dev):
+        return rc(ibgrad.at[pl.ds(first, 2)], ibgrad.at[pl.ds(first, 2)], ib_s.at[n], ib_r.at[n], dev)
+    ib_two(3, 2 * s, x_n).start()
+    ib_two(4, 2 * s, core_n).start()
+    ib_two(3, 2 * ((s + 2) % 4), x_n).wait_recv()
+    ib_two(5, 2 * ((s + 2) % 4), core_n).start()
+
+    f_relay(1)
+
+    def o_x():
+        rc(ograd, ograd, zo_s.at[2], zo_r.at[2], x_n).wait_recv()
+        rc(ograd, ograd, zo_s.at[3], zo_r.at[3], core_n).start()
+    pl.when((s + 2) % 4 == z)(o_x)
+    pl.when((s + 1 - 2 * c == z) | ((s + 1 - 2 * c + 2) % 4 == z))(
+        lambda: rc(ograd, ograd, zo_s.at[3], zo_r.at[3], core_n).wait_recv())
+
+    zreduce_own(0)
+    f_begin(0)
+    f_spread(0)
+    f_relay(0)
+
+    for ch in range(3):
+        gather_drain(ch)
+        zdrain(ch)
+        f_end(ch)
+    o_drain()
+    for a in (ag_x, ag_c, ag_n, ag_g):
+        a[3]()
+    rs_o[2]()
+    rs_g1[2]()
+    pl.when(z < s)(lambda: zo_send(True).wait_send())
+    pl.when(z > s)(lambda: zo_send(False).wait_send())
+
+    def o_out_done(n):
+        rc(ograd, ograd, zo_s.at[n], zo_r.at[n], core_n).wait_send()
+    pl.when(z == s)(lambda: o_out_done(2))
+    pl.when((z == s) | ((s + 2) % 4 == z))(lambda: o_out_done(3))
+    pl.when(has_r)(lambda: ib_send(True).wait_send())
+    pl.when(has_l)(lambda: ib_send(False).wait_send())
+    rc(isb.at[0], ibgrad.at[rank], ib_s.at[2], ib_r.at[2], y_n).wait_send()
+    ib_two(4, 2 * (s + 1 - 2 * c), core_n).wait_recv()
+    ib_two(5, 2 * ((s + 1 - 2 * c + 2) % 4), core_n).wait_recv()
+    for n in (3, 4, 5):
+        ib_two(n, 0, core_n).wait_send()
+
+
+def layer_fast(
+    tokens, cotangent, ln1_gain, ln1_shift, q_weight, q_bias, k_weight, v_weight, v_bias,
+    o_weight, o_bias, ln2_gain, ln2_shift, in_weight, in_bias, out_weight, out_bias,
+):
+    sq, ns = lax.axis_index("seq"), lax.axis_size("seq")
+    ndp = lax.axis_size("dp")
+    nz, ranks = ndp // 2, 2 * ns
+    images, own_len, width = tokens.shape
+    ff = in_weight.shape[1]
+    hid, ffp = width // ranks, ff // ranks
+    rows = q_weight.shape[0]
+    y = lax.axis_index("dp") % 2
+
+    def two(mat, n):
+        part = lax.dynamic_slice_in_dim(mat, sq * 2 * n, 2 * n, axis=1)
+        return part.reshape(rows, 2, n).transpose(1, 0, 2)
+
+    vec = jnp.stack([ln1_gain, ln1_shift, q_bias, v_bias, o_bias, ln2_gain, ln2_shift, out_bias], axis=1)
+    out_rows = lax.dynamic_slice_in_dim(out_weight, sq * 2 * ffp, 2 * ffp, axis=0)
+    wp = jnp.concatenate(
+        [jnp.broadcast_to(vec, (2, rows, VEC)), two(q_weight, hid), two(k_weight, hid), two(v_weight, hid),
+         two(in_weight, ffp), out_rows.reshape(2, ffp, rows).transpose(0, 2, 1)], axis=2)
+    total = 3 * 512
+    used = VEC + 3 * hid + 2 * ffp
+    wp = jnp.pad(wp, ((0, 0), (0, 0), (0, total - used)))
+    in_at = VEC + 3 * hid
+    off_in = in_at % 128
+    win = (ffp + 127) // 128 * 128
+    inb = lax.dynamic_slice_in_dim(in_bias, (2 * sq + y) * ffp, ffp).astype(F32)
+    inb = jnp.broadcast_to(jnp.pad(inb, (off_in, win - ffp - off_in)), (8, win))
+    vmem = pl.BlockSpec(memory_space=pltpu.VMEM)
+    nimg, length, cols = 2 * images, own_len * ns, 512
+    tall = (nimg, length, width)
+    half = (own_len, width)
+    D = pltpu.SemaphoreType.DMA
+    V = pltpu.VMEM
+    scratch = dict(
+        w=V((2 * nz * rows, total), BF16), ow=V((hid, width), BF16), xall=V(tall, BF16), call=V(tall, BF16),
+        n1=V(tall, BF16), n2=V(tall, BF16), gb=V(tall, BF16), qkv=V((nimg, length, cols), BF16),
+        probs=V((nimg, 2, length, length), F32), mix=V((nimg, length, hid), BF16),
+        act=V((nimg, length, win), BF16), slope=V((nimg, length, win), F32), gp=V((nimg, length, win), BF16),
+        part=V(tall, BF16), part2=V(tall, BF16), r1=V((nimg, 2) + half, BF16), r1b=V((nimg, 2) + half, BF16),
+        dx=V(half, BF16), dy=V(half, BF16), rx=V((2,) + half, BF16), ry=V((2,) + half, BF16),
+        dxb=V(half, BF16), dyb=V(half, BF16), rxb=V((2,) + half, BF16), ryb=V((2,) + half, BF16),
+        hid_s=V((2,) + half, F32), hat2_s=V((2,) + half, F32), inv2_s=V((2, own_len, 128), F32),
+        gh_s=V((2,) + half, F32), n2own=V((8, 128), BF16), gbown=V((8, 128), BF16), vecs=V((VEC, width), F32),
+        g=V((2 * nz * rows, total), BF16), rb=V((3, nz + 1, 2, rows, cols), BF16),
+        rbo=V((2, hid + 16, width), BF16), gin_tail=V((width, 128), BF16), gout_tail=V((width, 128), BF16),
+        dqkv=V((nimg, length, cols), BF16), vsum=V((8, width), F32), ibx=V((2, 8, win), F32),
+        isb=V((3, 8, win), F32), og=V((hid + 16, width), BF16),
+        gy_s=D((3,)), gzr_s=D((3, nz, 2)), gzl_s=D((3, nz, 2)), g_r=D((3, nz, 2)), o_s=D((2,)), o_r=D((1,)),
+        ag_s=D((4, 14)), ag_r=D((4, 14)), rs_s=D((4, 14)), rs_r=D((4, 14)), z_s=D((3, nz, 2)),
+        z_r=D((3, nz + 1, 2)), zo_s=D((4,)), zo_r=D((4,)), f_s=D((3, 4)), f_r=D((3, 4)), ib_s=D((6,)),
+        ib_r=D((6,)),
+    )
+    out, gtok, fg, og, ib = pl.pallas_call(
+        functools.partial(layer_kernel, nz, hid, ffp),
+        out_shape=(
+            jax.ShapeDtypeStruct(tokens.shape, BF16), jax.ShapeDtypeStruct(tokens.shape, BF16),
+            jax.ShapeDtypeStruct((ranks, rows, total), BF16), jax.ShapeDtypeStruct((hid + 16, width), BF16),
+            jax.ShapeDtypeStruct((ranks, 8, win), F32),
+        ),
+        in_specs=[vmem] * 5,
+        out_specs=[vmem] * 5,
+        scratch_shapes=list(scratch.values()),
+        compiler_params=pltpu.CompilerParams(
+            collective_id=0, has_side_effects=True, vmem_limit_bytes=64000 * 1024),
+    )(wp, o_weight, tokens, cotangent, inb)
+    f = fg.astype(F32)
+
+    def spread(lo, n):
+        return f[:, :, lo : lo + n].transpose(1, 0, 2).reshape(rows, ranks * n)
+
+    gq, gk, gv = [spread(VEC + i * hid, hid) for i in range(3)]
+    gin = spread(in_at, ffp)
+    gout = f[:, :, in_at + ffp : used].transpose(0, 2, 1).reshape(ff, rows)
+    vs = jnp.sum(f[:, :, 0:VEC], axis=0)
+    go = og[:hid].astype(F32)
+    gqb = og[hid, VEC : VEC + hid].astype(F32)
+    gvb = og[hid, VEC + 2 * hid : VEC + 3 * hid].astype(F32)
+    gib = ib[:, 0, off_in : off_in + ffp].reshape(ff)
+    return (out, gtok, vs[:, 0], vs[:, 1], gq, gqb, gk, gv, gvb, go, vs[:, 4], vs[:, 2], vs[:, 3], gin, gib,
+            gout, vs[:, 5])
+
+
+def mm(a, b, ca, cb):
+    return lax.dot_general(a, b, (((ca,), (cb,)), ((), ())), preferred_element_type=F32)
 
 
 def on_device(
@@ -167,10 +944,11 @@
 
 
 def solution(mesh):
+    fast = mesh.shape["dp"] == 2 * mesh.shape["seq"]
     rows, vec = P("dp", None), P("dp")
     tok = P("dp", "seq", None)
     return jax.shard_map(
-        on_device,
+        layer_fast if fast else on_device,
         mesh=mesh,
         in_specs=(tok, tok, vec, vec, rows, vec, rows, rows, vec, rows, vec, vec, vec, rows,
                   P(), P(None, "dp"), vec),

time: 761 us -> 289 us (0.38)
  waiting for transfers between devices: 491 us -> 0 us
  Pallas kernels: 0 us -> 224 us
  blocking collectives: 74.6 us -> 0 us
  matrix products: 53.9 us -> 0 us
  local copies, waits for them, and re-layouts: 89.6 us -> 55.4 us
  other arithmetic: 23 us -> 4.64 us
  between operations: 15.1 us -> 0.85 us
    reduce_scatter x6 -> x0, waiting for transfers between devices: 253 us -> none  [the longest x1 114 us: on_device(): wide = lax.psum_scatter(wide, 'dp', scatter_dimension=0, tiled=True)]
    pallas_call x0 -> x1, Pallas kernels: none -> 224 us  [layer_fast(): pl.pallas_call(functools.partial(layer_kernel, nz, hid, ffp), out_shape=(...]
    all_gather x9 -> x0, waiting for transfers between devices: 221 us -> none  [the longest x1 55.8 us: on_device(): out_w = lax.all_gather(out_w.T, 'dp', axis=0, tiled=True)]
    dot_general x17 -> x0, matrix products: 51.7 us -> none  [the longest x12 44.9 us: mm(): lax.dot_general(a, b, (((ca,), (cb,)), ((), ())), preferred_element_type=...]
    psum x1 -> x0, blocking collectives: 39.8 us -> none  [on_device(): lax.psum(jnp.concatenate([own_sums.reshape(-1), bias_in]), ('dp', 'seq'))]
    all_gather x2 -> x0, blocking collectives: 34.9 us -> none  [the longest x1 25.4 us: on_device(): vecs = lax.all_gather(vecs, 'dp', axis=1, tiled=True).astype(F32)]
    concatenate x2 -> x1, local copies, waits for them, and re-layouts: 29.5 us -> 0.82 us  [layer_fast(): jnp.concatenate([jnp.broadcast_to(vec, (2, rows, VEC)), two(q_weight, hid...]
    all_to_all x1 -> x0, waiting for transfers between devices: 14.5 us -> none  [on_device(): lax.all_to_all(o_full, 'dp', split_axis=0, concat_axis=1, tiled=True)]
  transfers between devices with their start and end apart: 16 -> 0, of which waited for: 13 -> 0; matrix products, arithmetic and copies ran while one was open for 9% -> 0% of each run, Pallas kernels for 0% -> 0%
where the time goes in v2:
time: 289 us; the launch traced here: 285 us
  Pallas kernels  224 us (78%)
  local copies, waits for them, and re-layouts  55.4 us (19%)
  other arithmetic  4.64 us (2%)
    pallas_call x1, Pallas kernels, layer_fast(): pl.pallas_call(functools.partial(layer_kernel, nz, hid, ffp), out_shape=(...  224 us
    reshape x4, local copies, waits for them, and re-layouts, spread(): return f[:, :, lo:lo + n].transpose(1, 0, 2).reshape(rows, ranks * n)  11.8 us
    transpose x5, local copies, waits for them, and re-layouts, spread(): return f[:, :, lo:lo + n].transpose(1, 0, 2).reshape(rows, ranks * n)  10.8 us
    transpose x2, local copies, waits for them, and re-layouts, layer_fast(): gout = f[:, :, in_at + ffp:used].transpose(0, 2, 1).reshape(ff, rows)  10.5 us

profile of v2, /device:TPU:1, one launch (start us, length us, event | category | flops | bytes accessed | tf_op | source)
XLA Modules:
  0.0 285.2 jit_solution(10506585966189913346)
XLA Ops:
  0.7 0.8 stack.27
  6.2 1.0 constant_dynamic-slice_fusion.4
  7.4 1.1 constant_dynamic-slice_fusion.2
  9.4 1.2 constant_dynamic-slice_fusion
  11.0 0.8 concatenate.3
  11.8 1.0 pad.11.wp
  12.8 0.8 dynamic_slice.23
  14.2 224.3 %shard_map.296 = (bf16[2,64,1152]{2,1,0:T(8,128)(2,1)}, bf16[2,64,1152]{2,1,0:T(8,128)(2,1)}, bf16[8,144,1536]{2,1,0:T(8,128)(2,1)}, bf16[160,1152]{1,0:T(8,128)(2,1)}, f32[8,8,640]{2,1,0:T(8,128)}) custom-call(bf16[2,144,1536]{2,1,0:T(8,128)(2,1)} %pad.11.wp, bf16[144,1152]{1,0:T(8,128)(2,1)} %ow_own.1, bf16[2,64,1152]{2,1,0:T(8,128)(2,1)} %tok.1, ...), custom_call_target="tpu_custom_call" | custom-call | tf_op jit(solution)/shard_map/pallas_call | solution.py:789
  238.5 3.0 %convert_element_type.23 = f32[8,144,1536]{2,1,0:T(8,128)S(1)} convert(bf16[8,144,1536]{2,1,0:T(8,128)(2,1)} %get-tuple-element.24) | non-fusion elementwise | flops 1769472 | bytes 10616832 | tf_op jit(solution)/shard_map/convert_element_type | solution.py:802
  241.6 1.4 slice_reduce_fusion.1
  243.0 2.0 slice_bitcast_fusion.2
  245.0 1.7 copy.51
  246.7 2.5 reshape.73
  249.8 3.0 %copy.52 = f32[144,8,144]{2,1,0:T(8,128)} copy(f32[144,8,144]{2,0,1:T(8,128)} %get-tuple-element.36) | data formatting | bytes 1327104 | tf_op jit(solution)/shard_map/transpose | solution.py:805
  252.8 2.5 reshape.74
  255.3 1.7 copy.53
  257.0 2.5 reshape.75
  259.6 0.9 slice_convert_fusion
  260.5 6.1 %slice_bitcast_fusion = (f32[8,538,144]{1,2,0:T(8,128)}, f32[144,8,538]{2,0,1:T(8,128)S(1)}) fusion(f32[8,144,1536]{2,1,0:T(8,128)} %copy-done.1), kind=kLoop, calls=%fused_computation | loop fusion | bytes 9916416 | tf_op jit(solution)/shard_map/transpose | solution.py:809
  266.6 2.5 copy.54
  269.1 4.2 %reshape.76 = f32[144,4304]{1,0:T(8,128)} reshape(f32[144,8,538]{2,1,0:T(8,128)} %copy.54) | data formatting | bytes 4958208 | tf_op jit(solution)/shard_map/reshape | solution.py:805
  273.3 1.0 slice_reduce_fusion.7
  275.1 4.4 %copy.55 = f32[8,538,144]{1,0,2:T(8,128)} copy(f32[8,538,144]{1,2,0:T(8,128)} %get-tuple-element.33) | data formatting | bytes 4958208 | tf_op jit(solution)/shard_map/transpose | solution.py:809
  279.5 4.3 %reshape.77 = f32[4304,144]{0,1:T(8,128)} reshape(f32[8,538,144]{1,0,2:T(8,128)} %copy.55) | data formatting | bytes 4958208 | tf_op jit(solution)/shard_map/reshape | solution.py:809
  (38 shorter events, 9.7 us)
Async XLA Ops:
  0.7 8.1 %copy-start = (bf16[144,4304]{1,0:T(8,128)(2,1)S(1)}, bf16[144,4304]{1,0:T(8,128)(2,1)}, u32[]{:S(2)}) copy-start(bf16[144,4304]{1,0:T(8,128)(2,1)} %param.30) | copy-start | bytes 3718660
  241.5 3.4 %copy-start.1 = (f32[8,144,1536]{2,1,0:T(8,128)}, f32[8,144,1536]{2,1,0:T(8,128)S(1)}, u32[]{:S(2)}) copy-start(f32[8,144,1536]{2,1,0:T(8,128)S(1)} %convert_element_type.23) | copy-start | bytes 21233668
  245.0 4.2 %copy-start.2 = (bf16[160,1152]{1,0:T(8,128)(2,1)S(1)}, bf16[160,1152]{1,0:T(8,128)(2,1)}, u32[]{:S(2)}) copy-start(bf16[160,1152]{1,0:T(8,128)(2,1)} %get-tuple-element.25) | copy-start | bytes 1105924
  279.5 4.3 %copy-start.4 = (bf16[2,64,1152]{2,1,0:T(8,128)(2,1)S(1)}, bf16[2,64,1152]{2,1,0:T(8,128)(2,1)}, u32[]{:S(2)}) copy-start(bf16[2,64,1152]{2,1,0:T(8,128)(2,1)} %get-tuple-element.59) | copy-start | bytes 884740
  279.5 5.0 %copy-start.3 = (bf16[2,64,1152]{2,1,0:T(8,128)(2,1)S(1)}, bf16[2,64,1152]{2,1,0:T(8,128)(2,1)}, u32[]{:S(2)}) copy-start(bf16[2,64,1152]{2,1,0:T(8,128)(2,1)} %get-tuple-element.60) | copy-start | bytes 884740

commit v3 on v2

--- a/solution.py
+++ b/solution.py
@@ -47,13 +47,14 @@
 
 def layer_kernel(
     nz, hid, ffp,
-    wp, ow_own, tok, cot_in, inb,
-    out_ref, gtok_ref, fgrad, ograd, ibgrad,
+    wp, vin, ow_own, tok, cot_in, inb,
+    out_ref, gtok_ref, q_out, k_out, v_out, in_out, out_out, o_out, vec_out, ib_out,
+    fgrad, ograd, ibgrad, st_q, st_k, st_v, st_in, st_out, vslab,
     w, ow, xall, call, n1, n2, gb, qkv, probs, mix, act, slope, gp, part, part2, r1, r1b,
-    dx, dy, rx, ry, dxb, dyb, rxb, ryb, hid_s, hat2_s, inv2_s, gh_s, n2own, gbown, vecs, g, rb, rbo, gin_tail,
-    gout_tail, dqkv, vsum, ibx, isb, og,
+    dx, dy, rx, ry, dxb, dyb, rxb, ryb, hid_s, hat2_s, inv2_s, gh_s, vecs, g, rb, rbo, gin_tail,
+    gout_tail, dqkv, vsum, ibx, isb, og, qbs, qbx,
     gy_s, gzr_s, gzl_s, g_r, o_s, o_r, ag_s, ag_r, rs_s, rs_r, z_s, z_r, zo_s, zo_r, f_s, f_r,
-    ib_s, ib_r,
+    ib_s, ib_r, qb_s, qb_r, v_s, v_r, st_s,
 ):
     d, s = lax.axis_index("dp"), lax.axis_index("seq")
     z, y = d // 2, d % 2
@@ -83,12 +84,10 @@
         )
 
     barrier = pltpu.get_barrier_semaphore()
-    for dev in (core_n, x_n, y_n):
+    column = [((d + 2 * k) % (2 * nz), s) for k in range(1, nz)]
+    for dev in [core_n, x_n, y_n] + column:
         pl.semaphore_signal(barrier, inc=1, device_id=dev, device_id_type=MESH)
-    pl.when(has_r)(lambda: pl.semaphore_signal(barrier, inc=1, device_id=right, device_id_type=MESH))
-    pl.when(has_l)(lambda: pl.semaphore_signal(barrier, inc=1, device_id=left, device_id_type=MESH))
-    beside = (z + nz - 2) // (nz - 1) + (2 * nz - 3 - z) // (nz - 1)
-    pl.semaphore_wait(barrier, 3 + beside)
+    pl.semaphore_wait(barrier, 3 + len(column))
 
     def wrows(origin, sub):
         return pl.ds(pl.multiple_of(origin * plane + sub * rows8, 16), rows8)
@@ -131,6 +130,18 @@
             for sub in range(2):
                 wrecv(ch, z + k, sub)
                 pl.when(has_l)(lambda: wsend(ch, z + k, sub, wslab(ch, z + k, sub), False).start())
+
+        pl.when(z - k >= 0)(from_left)
+        pl.when(z + k < nz)(from_right)
+
+    def gather_hop1(ch, k, sub):
+        def from_left():
+            wrecv(ch, z - k, sub)
+            pl.when(has_r)(lambda: wsend(ch, z - k, sub, wslab(ch, z - k, sub), True).start())
+
+        def from_right():
+            wrecv(ch, z + k, sub)
+            pl.when(has_l)(lambda: wsend(ch, z + k, sub, wslab(ch, z + k, sub), False).start())
 
         pl.when(z - k >= 0)(from_left)
         pl.when(z + k < nz)(from_right)
@@ -155,12 +166,12 @@
             pl.when(has_l)(lambda: rc(ow_own, ow, o_s.at[1], o_r.at[0], left).start())
         pl.when(z == s)(go)
 
-    def o_pass():
+    def o_pass(k):
         def go():
             rc(ow, ow, o_r.at[0], o_r.at[0], core_n).wait_recv()
             pl.when((z > s) & has_r)(lambda: osend(True).start())
             pl.when((z < s) & has_l)(lambda: osend(False).start())
-        pl.when(z != s)(go)
+        pl.when((z == s + k) | (z == s - k))(go)
 
     def o_drain():
         pl.when((z >= s) & has_r)(lambda: osend(True).wait_send())
@@ -297,37 +308,263 @@
 
         return run, result, drain
 
+    def rb_at(ch, slot, sub):
+        return rb.at[ch, slot, sub]
+
+    def gslab(ch, dest, sub):
+        return g.at[wrows(dest, sub), pl.ds(ch * cols, cols)]
+
+    def zsend(ch, k, sub, to_right):
+        dest = z + k if to_right else z - k
+        slot = nz if k == 1 and not to_right else dest
+        return rc(gslab(ch, dest, sub), rb_at(ch, slot, sub), z_s.at[ch, dest, sub], z_r.at[ch, slot, sub],
+                  right if to_right else left)
+
+    def zadd(ch, dest, slot, sub):
+        rc(rb_at(ch, slot, sub), rb_at(ch, slot, sub), z_r.at[ch, slot, sub], z_r.at[ch, slot, sub],
+           core_n).wait_recv()
+        r, cs = wrows(dest, sub), slice(ch * cols, (ch + 1) * cols)
+        g[r, cs] = (g[r, cs].astype(F32) + rb[ch, slot, sub].astype(F32)).astype(BF16)
+
+    def zreduce_hop(ch, k):
+        def to_right():
+            for sub in range(2):
+                pl.when(has_l)(lambda: zadd(ch, z + k, z + k, sub))
+                zsend(ch, k, sub, True).start()
+
+        def to_left():
+            for sub in range(2):
+                pl.when(has_r)(lambda: zadd(ch, z - k, z - k, sub))
+                zsend(ch, k, sub, False).start()
+
+        pl.when(z + k < nz)(to_right)
+        pl.when(z - k >= 0)(to_left)
+
+    def zreduce_own(ch):
+        for sub in range(2):
+            pl.when(has_l)(lambda: zadd(ch, z, z, sub))
+            pl.when(has_r)(lambda: zadd(ch, z, nz, sub))
+
+    def zdrain(ch):
+        for k in range(1, nz):
+            for sub in range(2):
+                pl.when(z + k < nz)(lambda: zsend(ch, k, sub, True).wait_send())
+                pl.when(z - k >= 0)(lambda: zsend(ch, k, sub, False).wait_send())
+
+    def f_swap(ch):
+        src = g.at[wrows(z, 1 - y), pl.ds(ch * cols, cols)]
+        return rc(src, fgrad.at[rank, :, pl.ds(ch * cols, cols)], f_s.at[ch, 0], f_r.at[ch, 0], y_n)
+
+    def f_msg(ch, n, slot, dev):
+        piece = fgrad.at[slot, :, pl.ds(ch * cols, cols)]
+        return rc(piece, piece, f_s.at[ch, n], f_r.at[ch, n], dev)
+
+    sx, sp = (s + 2) % 4, s + 1 - 2 * c
+    spx = (sp + 2) % 4
+
+    def f_begin(ch):
+        f_swap(ch).start()
+        fgrad[rank, :, ch * cols : (ch + 1) * cols] = g[wrows(z, y), ch * cols : (ch + 1) * cols]
+        f_msg(ch, 1, rank, x_n).start()
+        f_msg(ch, 3, rank, core_n).start()
+
+    def f_spread(ch):
+        other = 2 * s + 1 - y
+        f_msg(ch, 0, other, y_n).wait_recv()
+        f_msg(ch, 2, other, x_n).start()
+        f_msg(ch, 4, other, core_n).start()
+
+    def f_relay(ch):
+        f_msg(ch, 1, 2 * sx + y, x_n).wait_recv()
+        f_msg(ch, 5, 2 * sx + y, core_n).start()
+        f_msg(ch, 2, 2 * sx + 1 - y, x_n).wait_recv()
+        f_msg(ch, 6, 2 * sx + 1 - y, core_n).start()
+
+    def f_end(ch):
+        f_msg(ch, 3, 2 * sp + y, core_n).wait_recv()
+        f_msg(ch, 4, 2 * sp + 1 - y, core_n).wait_recv()
+        f_msg(ch, 5, 2 * spx + y, core_n).wait_recv()
+        f_msg(ch, 6, 2 * spx + 1 - y, core_n).wait_recv()
+
+    def f_drain(ch):
+        f_swap(ch).wait_send()
+        for n in range(1, 7):
+            f_msg(ch, n, rank, core_n).wait_send()
+
+    def z_middle(ch, k):
+        pl.when((z > 0) & (z < nz - 1))(lambda: zreduce_hop(ch, k))
+
+    def z_ends(ch):
+        for k in range(nz - 1, 0, -1):
+            pl.when((z == 0) | (z == nz - 1))(lambda: zreduce_hop(ch, k))
+
+    def zo_send(to_right):
+        n = 0 if to_right else 1
+        return rc(og, rbo.at[n], zo_s.at[n], zo_r.at[n], right if to_right else left)
+
+    def zo_add(n):
+        rc(rbo.at[n], rbo.at[n], zo_s.at[n], zo_r.at[n], core_n).wait_recv()
+        og[...] = (og[...].astype(F32) + rbo[n].astype(F32)).astype(BF16)
+
+    def zo_mid_r():
+        zo_add(0)
+        zo_send(True).start()
+
+    def zo_mid_l():
+        zo_add(1)
+        zo_send(False).start()
+
+    def qb_send():
+        return rc(qbs, qbx.at[z], qb_s.at[0], qb_r.at[z], (2 * s + y, s))
+
+    def qb_begin():
+        bsum = jnp.zeros((1, cols), F32)
+        for img in range(nimg):
+            bsum = bsum + jnp.sum(dqkv[img].astype(F32), axis=0, keepdims=True)
+        qbs[...] = jnp.broadcast_to(bsum, (8, cols))
+        pl.when(z != s)(lambda: qb_send().start())
+
+    def o_here():
+        pl.when(has_l)(lambda: zo_add(0))
+        pl.when(has_r)(lambda: zo_add(1))
+        total = qbs[...]
+        for k in range(1, nz):
+            zz = (z + k) % nz
+            rc(qbs, qbx.at[zz], qb_s.at[0], qb_r.at[zz], core_n).wait_recv()
+            total = total + qbx[zz]
+        og[qw:, 0:cols] = jnp.concatenate([total, total], axis=0).astype(BF16)
+        ograd[...] = og[...]
+        rc(ograd, ograd, zo_s.at[2], zo_r.at[2], x_n).start()
+        rc(ograd, ograd, zo_s.at[3], zo_r.at[3], core_n).start()
+
+    def o_x():
+        rc(ograd, ograd, zo_s.at[2], zo_r.at[2], x_n).wait_recv()
+        rc(ograd, ograd, zo_s.at[3], zo_r.at[3], core_n).start()
+
+    def o_end():
+        pl.when((sp == z) | (spx == z))(
+            lambda: rc(ograd, ograd, zo_s.at[3], zo_r.at[3], core_n).wait_recv())
+
+    def o_out_done(n):
+        rc(ograd, ograd, zo_s.at[n], zo_r.at[n], core_n).wait_send()
+
+    def ib_send(k):
+        return rc(isb, ibx.at[z], ib_s.at[k - 1], ib_r.at[z], ((d + 2 * k) % (2 * nz), s))
+
+    def ib_begin():
+        ib = jnp.zeros((1, win), F32)
+        for img in range(nimg):
+            ib = ib + jnp.sum(gp[img].astype(F32), axis=0, keepdims=True)
+        isb[...] = jnp.broadcast_to(ib, (8, win))
+        for k in range(1, nz):
+            ib_send(k).start()
+
+    def ib_msg(n, slot, dev):
+        return rc(ibgrad.at[slot], ibgrad.at[slot], ib_s.at[n], ib_r.at[n], dev)
+
+    def ib_pass():
+        ibsum = isb[...]
+        for k in range(1, nz):
+            zz = (z + k) % nz
+            rc(isb, ibx.at[zz], ib_s.at[0], ib_r.at[zz], core_n).wait_recv()
+            ibsum = ibsum + ibx[zz]
+        ibgrad[rank] = ibsum
+        ib_msg(nz, rank, y_n).start()
+        ib_msg(nz + 1, rank, x_n).start()
+        ib_msg(nz + 3, rank, core_n).start()
+
+    def ib_end():
+        other = 2 * s + 1 - y
+        ib_msg(nz, other, y_n).wait_recv()
+        ib_msg(nz + 2, other, x_n).start()
+        ib_msg(nz + 4, other, core_n).start()
+        ib_msg(nz + 1, 2 * sx + y, x_n).wait_recv()
+        ib_msg(nz + 5, 2 * sx + y, core_n).start()
+        ib_msg(nz + 2, 2 * sx + 1 - y, x_n).wait_recv()
+        ib_msg(nz + 6, 2 * sx + 1 - y, core_n).start()
+        ib_msg(nz + 3, 2 * sp + y, core_n).wait_recv()
+        ib_msg(nz + 4, 2 * sp + 1 - y, core_n).wait_recv()
+        ib_msg(nz + 5, 2 * spx + y, core_n).wait_recv()
+        ib_msg(nz + 6, 2 * spx + 1 - y, core_n).wait_recv()
+
+    def vec_send(k):
+        return rc(vin, vslab.at[y, z], v_s.at[k - 1], v_r.at[z], ((d + 2 * k) % (2 * nz), s))
+
+    def vec_cross():
+        return rc(vslab.at[y], vslab.at[y], v_s.at[nz - 1], v_r.at[nz], y_n)
+
+    def vec_begin():
+        for k in range(1, nz):
+            vec_send(k).start()
+        vslab[y, z] = vin[...]
+
+    def vec_pass():
+        for k in range(1, nz):
+            zz = (z + k) % nz
+            rc(vin, vslab.at[y, zz], v_s.at[0], v_r.at[zz], core_n).wait_recv()
+        vec_cross().start()
+
+    def vec_end():
+        rc(vslab.at[1 - y], vslab.at[1 - y], v_s.at[0], v_r.at[nz], y_n).wait_recv()
+        for zz in range(nz):
+            for yy in range(2):
+                at = (2 * zz + yy) * rows8
+                vecs[:, at : at + rows8] = vslab[yy, zz].astype(F32)[0:VEC, 0:rows8]
+
+    def vec_drain():
+        for k in range(1, nz):
+            vec_send(k).wait_send()
+        vec_cross().wait_send()
+
+    nrank = fgrad.shape[0]
+    stores = [(st_q, q_out, 0), (st_k, k_out, 1), (st_v, v_out, 2), (st_in, in_out, 3),
+              (st_out, out_out, 4), (ograd, o_out, 5)]
+
+    def emit_out():
+        for t in range(nrank):
+            piece = fgrad[t, :, out_at : out_at + ffp].astype(F32)
+            st_out[t * ffp : (t + 1) * ffp] = jnp.transpose(piece, (1, 0)).astype(BF16)
+            st_in[:, t * ffp + cols - in_at : (t + 1) * ffp] = fgrad[t, :, cols : in_at + ffp]
+        pltpu.make_async_copy(st_out, out_out, st_s.at[4]).start()
+
+    def emit_rest():
+        pltpu.make_async_copy(ograd, o_out, st_s.at[5]).start()
+        for t in range(nrank):
+            for n, st in enumerate((st_q, st_k, st_v)):
+                st[:, t * qw : (t + 1) * qw] = fgrad[t, :, VEC + n * qw : VEC + (n + 1) * qw]
+            st_in[:, t * ffp : t * ffp + cols - in_at] = fgrad[t, :, in_at:cols]
+        for stage, dst, n in stores[:4]:
+            pltpu.make_async_copy(stage, dst, st_s.at[n]).start()
+        vcols = jnp.zeros((rows8, 128), F32)
+        for t in range(nrank):
+            vcols = vcols + fgrad[t, :, 0:128].astype(F32)
+        vec_out[0:VEC] = jnp.transpose(vcols, (1, 0))[0:VEC]
+        vec_out[6:7] = ograd[qw : qw + 8, VEC : VEC + qw].astype(F32)[0:1]
+        vec_out[7:8] = ograd[qw : qw + 8, VEC + 2 * qw : VEC + 3 * qw].astype(F32)[0:1]
+        for t in range(nrank):
+            ib_out[0:1, t * ffp : (t + 1) * ffp] = ibgrad[t, 0:1, off_in : off_in + ffp]
+
     gather_swap(0)
-    gather_own(0)
-    o_own()
+    own_rows = pl.ds(pl.multiple_of(s * own_len, 16), own_len)
+    for i in range(2):
+        xall[2 * y + i, own_rows] = tok[i]
     ag_x = agather(0, xall)
     ag_c = agather(1, call)
+    ag_x[0]()
+    gather_own(0)
+    vec_begin()
     for i in range(2):
-        xall[2 * y + i, pl.ds(pl.multiple_of(s * own_len, 16), own_len)] = tok[i]
-        call[2 * y + i, pl.ds(pl.multiple_of(s * own_len, 16), own_len)] = cot_in[i]
-    ag_x[0]()
+        call[2 * y + i, own_rows] = cot_in[i]
     gather_other(0)
+    o_own()
+    gather_hop1(0, 1, y)
+    vec_pass()
     ag_x[1]()
-    gather_hop(0, 1)
-    gather_swap(1)
-    gather_swap(2)
-    ag_c[0]()
+    gather_hop1(0, 1, 1 - y)
+    gather_hop1(0, 2, y)
+    o_pass(1)
     ag_x[2]()
-    gather_hop(0, 2)
-    o_pass()
-    gather_own(1)
-    gather_other(1)
-    ag_c[1]()
-    ag_c[2]()
-    gather_hop(0, 3)
-
-    lane = lax.broadcasted_iota(jnp.int32, (1, cols), 1)
-    vt = jnp.transpose(w[:, 0:128].astype(F32), (1, 0))
-    vecs[...] = vt[0:8]
-    qb = pltpu.roll(vecs[...], (VEC - rank * qw + width) % width, 1)[2:3, :cols]
-    vb = pltpu.roll(vecs[...], (VEC + 2 * qw - rank * qw + width) % width, 1)[3:4, :cols]
-    qkv_bias = jnp.where((lane >= VEC) & (lane < VEC + qw), qb, 0.0) + jnp.where(
-        (lane >= VEC + 2 * qw) & (lane < VEC + 3 * qw), vb, 0.0)
+    vec_end()
     g1, s1 = vecs[0:1], vecs[1:2]
     o_b, g2, s2, out_b = vecs[4:5], vecs[5:6], vecs[6:7], vecs[7:8]
 
@@ -336,7 +573,21 @@
         hat, _ = normalize(xall[img, r].astype(F32))
         n1[img, r] = (hat * g1 + s1).astype(BF16)
         return carry
+
+    gather_hop1(0, 2, 1 - y)
+    o_pass(2)
+    gather_own(1)
+    gather_swap(1)
+    ag_c[0]()
     lax.fori_loop(0, 4 * nimg, ln1_step, 0)
+    gather_hop(0, 3)
+    gather_other(1)
+
+    lane = lax.broadcasted_iota(jnp.int32, (1, cols), 1)
+    qb = pltpu.roll(vecs[...], (VEC - rank * qw + width) % width, 1)[2:3, :cols]
+    vb = pltpu.roll(vecs[...], (VEC + 2 * qw - rank * qw + width) % width, 1)[3:4, :cols]
+    qkv_bias = jnp.where((lane >= VEC) & (lane < VEC + qw), qb, 0.0) + jnp.where(
+        (lane >= VEC + 2 * qw) & (lane < VEC + 3 * qw), vb, 0.0)
 
     def att_step(img, carry):
         proj = dot(n1[img], w[:, 0:cols], 1, 0) + qkv_bias
@@ -355,18 +606,23 @@
             outs.append(dot(p.astype(BF16), v, 1, 0).astype(BF16))
         mix[img] = jnp.concatenate(outs, axis=1)
         return carry
-    lax.fori_loop(0, nimg, att_step, 0)
-
+
+    lax.fori_loop(0, 2, att_step, 0)
+    ag_c[1]()
     gather_hop(1, 1)
+    lax.fori_loop(2, nimg, att_step, 0)
+    o_pass(3)
+    ag_c[2]()
+    gather_swap(2)
+
+    def o_part(img):
+        part[img] = dot(mix[img], ow[...], 1, 0).astype(BF16)
+
+    rs_h = rscatter(0, part, r1, (dx, dy, rx, ry), o_part)
+    rs_h[0]()
+    gather_hop(1, 2)
     gather_own(2)
     gather_other(2)
-    gather_hop(1, 2)
-
-    def o_part(img):
-        part[img] = dot(mix[img], ow[...], 1, 0).astype(BF16)
-
-    rs_h = rscatter(0, part, r1, (dx, dy, rx, ry), o_part)
-    rs_h[0]()
     rs_h[2]()
     ag_n = agather(2, n2)
     for i in range(2):
@@ -375,13 +631,12 @@
         hat, inv = normalize(hidden)
         hat2_s[i] = hat
         inv2_s[i] = jnp.broadcast_to(inv, (own_len, 128))
-        n2[2 * y + i, pl.ds(pl.multiple_of(s * own_len, 16), own_len)] = (hat * g2 + s2).astype(BF16)
+        n2[2 * y + i, own_rows] = (hat * g2 + s2).astype(BF16)
     ag_n[0]()
+    ag_n[1]()
     gather_hop(1, 3)
     gather_hop(2, 1)
-    ag_n[1]()
     ag_n[2]()
-    gather_hop(2, 2)
 
     wlane = lax.broadcasted_iota(jnp.int32, (1, win), 1)
     valid = (wlane >= off_out) & (wlane < off_out + ffp)
@@ -392,83 +647,9 @@
         act[img] = jnp.where(valid, pltpu.roll(a, shift, 1), 0.0).astype(BF16)
         slope[img] = jnp.where(valid, pltpu.roll(sl, shift, 1), 0.0)
         return carry
-    lax.fori_loop(0, nimg, in_step, 0)
-
-    def rb_at(ch, slot, sub):
-        return rb.at[ch, slot, sub]
-
-    def gslab(ch, dest, sub):
-        return g.at[wrows(dest, sub), pl.ds(ch * cols, cols)]
-
-    def zsend(ch, k, sub, to_right):
-        dest = z + k if to_right else z - k
-        slot = nz if k == 1 and not to_right else dest
-        return rc(gslab(ch, dest, sub), rb_at(ch, slot, sub), z_s.at[ch, dest, sub], z_r.at[ch, slot, sub],
-                  right if to_right else left)
-
-    def zadd(ch, dest, slot, sub):
-        rc(rb_at(ch, slot, sub), rb_at(ch, slot, sub), z_r.at[ch, slot, sub], z_r.at[ch, slot, sub],
-           core_n).wait_recv()
-        r, cs = wrows(dest, sub), slice(ch * cols, (ch + 1) * cols)
-        g[r, cs] = (g[r, cs].astype(F32) + rb[ch, slot, sub].astype(F32)).astype(BF16)
-
-    def zreduce_hop(ch, k):
-        def to_right():
-            for sub in range(2):
-                pl.when(has_l)(lambda: zadd(ch, z + k, z + k, sub))
-                zsend(ch, k, sub, True).start()
-
-        def to_left():
-            for sub in range(2):
-                pl.when(has_r)(lambda: zadd(ch, z - k, z - k, sub))
-                zsend(ch, k, sub, False).start()
-
-        pl.when(z + k < nz)(to_right)
-        pl.when(z - k >= 0)(to_left)
-
-    def zreduce_own(ch):
-        for sub in range(2):
-            pl.when(has_l)(lambda: zadd(ch, z, z, sub))
-            pl.when(has_r)(lambda: zadd(ch, z, nz, sub))
-
-    def zdrain(ch):
-        for k in range(1, nz):
-            for sub in range(2):
-                pl.when(z + k < nz)(lambda: zsend(ch, k, sub, True).wait_send())
-                pl.when(z - k >= 0)(lambda: zsend(ch, k, sub, False).wait_send())
-
-    def fslot(ch, first, n):
-        return fgrad.at[pl.ds(first, n), :, pl.ds(ch * cols, cols)]
-
-    def f_swap(ch):
-        src = g.at[wrows(z, 1 - y), pl.ds(ch * cols, cols)]
-        return rc(src, fgrad.at[rank, :, pl.ds(ch * cols, cols)], f_s.at[ch, 0], f_r.at[ch, 0], y_n)
-
-    def f_msg(ch, n, first, dev):
-        return rc(fslot(ch, first, 2), fslot(ch, first, 2), f_s.at[ch, n], f_r.at[ch, n], dev)
-
-    def f_begin(ch):
-        f_swap(ch).start()
-        fgrad[rank, :, ch * cols : (ch + 1) * cols] = g[wrows(z, y), ch * cols : (ch + 1) * cols]
-
-    def f_spread(ch):
-        other = fgrad.at[2 * s + 1 - y, :, pl.ds(ch * cols, cols)]
-        rc(other, other, f_s.at[ch, 0], f_r.at[ch, 0], y_n).wait_recv()
-        f_msg(ch, 1, 2 * s, x_n).start()
-        f_msg(ch, 2, 2 * s, core_n).start()
-
-    def f_relay(ch):
-        sx = (s + 2) % 4
-        f_msg(ch, 1, 2 * sx, x_n).wait_recv()
-        f_msg(ch, 3, 2 * sx, core_n).start()
-
-    def f_end(ch):
-        sp = s + 1 - 2 * c
-        f_msg(ch, 2, 2 * sp, core_n).wait_recv()
-        f_msg(ch, 3, 2 * ((sp + 2) % 4), core_n).wait_recv()
-        f_swap(ch).wait_send()
-        for n in (1, 2, 3):
-            f_msg(ch, n, 0, core_n).wait_send()
+    lax.fori_loop(0, 2, in_step, 0)
+    gather_hop(2, 2)
+    lax.fori_loop(2, nimg, in_step, 0)
 
     rtile = width // 3
 
@@ -481,33 +662,21 @@
         g[r, 2 * cols : 3 * cols] = acc[:, 2 * cols - out_win :].astype(BF16)
         return carry
     lax.fori_loop(0, 3, gout_step, 0)
-    for k in range(nz - 1, 0, -1):
-        pl.when(z == 0)(lambda: zreduce_hop(2, k))
-        pl.when(z == nz - 1)(lambda: zreduce_hop(2, k))
+    z_ends(2)
     gather_hop(2, 3)
-
-    def out_part(img):
-        part2[img] = dot(act[img], w[:, out_win : out_win + win], 1, 1).astype(BF16)
-
-    rs_o = rscatter(1, part2, r1b, (dxb, dyb, rxb, ryb), out_part)
 
     def gp_step(img, carry):
         ga = dot(call[img], w[:, out_win : out_win + win], 1, 0) * slope[img]
-        ga = pltpu.roll(ga, win - shift, 1)
-        gp[img] = ga.astype(BF16)
+        gp[img] = pltpu.roll(ga, win - shift, 1).astype(BF16)
         return carry
     lax.fori_loop(0, nimg, gp_step, 0)
 
-    ib = jnp.zeros((1, win), F32)
-    for img in range(nimg):
-        ib = ib + jnp.sum(gp[img].astype(F32), axis=0, keepdims=True)
-    isb[0] = jnp.broadcast_to(ib, (8, win))
-
     def gn2_part(img):
         part[img] = dot(gp[img], w[:, in_win : in_win + win], 1, 1).astype(BF16)
 
     rs_g2 = rscatter(2, part, r1, (dx, dy, rx, ry), gn2_part)
     rs_g2[0]()
+    z_middle(2, 2)
 
     def gin_step(t, carry):
         r = pl.ds(pl.multiple_of(t * rtile, rtile), rtile)
@@ -519,16 +688,7 @@
         g[r, cols : 2 * cols - 128] = acc[:, lo : win - 128].astype(BF16)
         g[r, 2 * cols - 128 : 2 * cols] = (acc[:, win - 128 :] + gout_tail[r].astype(F32)).astype(BF16)
         return carry
-    lax.fori_loop(0, 3, gin_step, 0)
-
-    def z_middle(ch, k):
-        pl.when((z > 0) & (z < nz - 1))(lambda: zreduce_hop(ch, k))
-
-    def z_ends(ch):
-        for k in range(nz - 1, 0, -1):
-            pl.when((z == 0) | (z == nz - 1))(lambda: zreduce_hop(ch, k))
-
-    z_ends(1)
+
     sums = [jnp.zeros((1, width), F32) for _ in range(6)]
     ag_g = agather(3, gb)
     for i in range(2):
@@ -540,20 +700,30 @@
         gh = up + norm_back(gn2, g2, hat, inv2_s[i][:, 0:1])
         gh_s[i] = gh
         low = gh.astype(BF16)
-        gb[2 * y + i, pl.ds(pl.multiple_of(s * own_len, 16), own_len)] = low
+        gb[2 * y + i, own_rows] = low
         sums[4] = sums[4] + jnp.sum(low.astype(F32), axis=0, keepdims=True)
         sums[5] = sums[5] + jnp.sum(up, axis=0, keepdims=True)
     rs_g2[2]()
     ag_g[0]()
-    z_middle(2, 2)
+    for n in range(2, 6):
+        vsum[n : n + 1] = sums[n]
+    vsum[6:8] = jnp.zeros((2, width), F32)
+    vsum[0:2] = jnp.zeros((2, width), F32)
+    lax.fori_loop(0, 3, gin_step, 0)
+    z_ends(1)
+    ib_begin()
+    ag_g[1]()
     z_middle(2, 1)
-    ag_g[1]()
-    rs_o[0]()
     ag_g[2]()
-    zreduce_own(2)
-    f_begin(2)
+
+    gacc = jnp.zeros((qw, width), F32)
+    for img in range(nimg):
+        gacc = gacc + dot(mix[img], gb[img], 0, 0)
+    og[0:qw] = gacc.astype(BF16)
+    og[qw:] = jnp.zeros((16, width), BF16)
+    pl.when((z == 0) & (z < s))(lambda: zo_send(True).start())
+    pl.when((z == nz - 1) & (z > s))(lambda: zo_send(False).start())
     z_middle(1, 2)
-    z_middle(1, 1)
 
     def attb_step(img, carry):
         proj, gbi = qkv[img], gb[img]
@@ -574,23 +744,16 @@
             dv.append(dot(p.astype(BF16), gm, 0, 0).astype(BF16))
         pad = jnp.zeros((length, cols - VEC - 3 * qw), BF16)
         dqkv[img] = jnp.concatenate([zero] + dq + dk + dv + [pad], axis=1)
-        return carry
-    lax.fori_loop(0, nimg, attb_step, 0)
-
-    vsum[0:2] = jnp.zeros((2, width), F32)
-
-    def gn1_part(img):
         pr = dot(dqkv[img], w[:, 0:cols], 1, 1)
         hat, _ = normalize(xall[img].astype(F32))
         vsum[0:1] = vsum[0:1] + jnp.sum(pr * hat, axis=0, keepdims=True)
         vsum[1:2] = vsum[1:2] + jnp.sum(pr, axis=0, keepdims=True)
         part[img] = pr.astype(BF16)
-
+        return carry
+
+    def gn1_part(img):
+        pass
     rs_g1 = rscatter(3, part, r1, (dx, dy, rx, ry), gn1_part)
-    rs_g1[0]()
-    for n in range(2, 6):
-        vsum[n : n + 1] = sums[n]
-    vsum[6:8] = jnp.zeros((2, width), F32)
 
     def gqkv_step(t, carry):
         r = pl.ds(pl.multiple_of(t * rtile, rtile), rtile)
@@ -602,133 +765,76 @@
         g[r, 128 : cols - 128] = acc[:, 128 : cols - 128].astype(BF16)
         g[r, cols - 128 : cols] = (acc[:, cols - 128 :] + gin_tail[r].astype(F32)).astype(BF16)
         return carry
+
+    lax.fori_loop(0, nimg, attb_step, 0)
+    z_middle(1, 1)
+    qb_begin()
     lax.fori_loop(0, 3, gqkv_step, 0)
     z_ends(0)
-
-    gacc = jnp.zeros((qw, width), F32)
-    for img in range(nimg):
-        gacc = gacc + dot(mix[img], gb[img], 0, 0)
-    og[0:qw] = gacc.astype(BF16)
-    bsum = jnp.zeros((1, cols), F32)
-    for img in range(nimg):
-        bsum = bsum + jnp.sum(dqkv[img].astype(F32), axis=0, keepdims=True)
-    og[qw:, 0:cols] = jnp.broadcast_to(bsum, (16, cols)).astype(BF16)
-    og[qw:, cols:] = jnp.zeros((16, width - cols), BF16)
-
-    def zo_send(to_right):
-        n = 0 if to_right else 1
-        return rc(og, rbo.at[n], zo_s.at[n], zo_r.at[n], right if to_right else left)
-
-    def zo_add(n):
-        rc(rbo.at[n], rbo.at[n], zo_s.at[n], zo_r.at[n], core_n).wait_recv()
-        og[...] = (og[...].astype(F32) + rbo[n].astype(F32)).astype(BF16)
-
-    pl.when((z == 0) & (z < s))(lambda: zo_send(True).start())
-    pl.when((z == nz - 1) & (z > s))(lambda: zo_send(False).start())
-
-    def ib_send(to_right):
-        n = 0 if to_right else 1
-        return rc(isb.at[1 + n], ibx.at[n], ib_s.at[n], ib_r.at[n], right if to_right else left)
-
-    def ib_recv(n):
-        rc(ibx.at[n], ibx.at[n], ib_s.at[n], ib_r.at[n], core_n).wait_recv()
-
-    def ib_first():
-        isb[1] = isb[0]
-        isb[2] = isb[0]
-    ib_first()
-    pl.when(z == 0)(lambda: ib_send(True).start())
-    pl.when(z == nz - 1)(lambda: ib_send(False).start())
-
+    zreduce_own(2)
+    f_begin(2)
+    rs_g1[0]()
+    z_middle(0, 2)
+    ib_pass()
     f_spread(2)
+    pl.when((z == 1) & (z < s))(zo_mid_r)
+    pl.when((z == nz - 2) & (z > s))(zo_mid_l)
     zreduce_own(1)
     f_begin(1)
-    f_relay(2)
-    z_middle(0, 2)
-    z_middle(0, 1)
-
-    def zo_mid_r():
-        zo_add(0)
-        zo_send(True).start()
-
-    def zo_mid_l():
-        zo_add(1)
-        zo_send(False).start()
-    pl.when((z > 0) & (z < s))(zo_mid_r)
-    pl.when((z < nz - 1) & (z > s))(zo_mid_l)
-
-    def ib_mid(n):
-        ib_recv(n)
-        isb[1 + n] = isb[0] + ibx[n]
-        pl.when((has_r if n == 0 else has_l))(lambda: ib_send(n == 0).start())
-    pl.when(has_l)(lambda: ib_mid(0))
-    pl.when(has_r)(lambda: ib_mid(1))
 
     for i in range(2):
         gn1 = rs_g1[1](i)
         hat, inv = normalize(tok[i].astype(F32))
         gtok_ref[i] = (gh_s[i] + norm_back(gn1, g1, hat, inv)).astype(BF16)
-        out_ref[i] = (hid_s[i] + rs_o[1](i) + out_b).astype(BF16)
-
+    z_middle(0, 1)
+    pl.when((z > 1) & (z < s))(zo_mid_r)
+    pl.when((z < nz - 2) & (z > s))(zo_mid_l)
+    f_relay(2)
     f_spread(1)
 
-    def o_here():
-        pl.when(has_l)(lambda: zo_add(0))
-        pl.when(has_r)(lambda: zo_add(1))
-        ograd[...] = og[...]
-        rc(ograd, ograd, zo_s.at[2], zo_r.at[2], x_n).start()
-        rc(ograd, ograd, zo_s.at[3], zo_r.at[3], core_n).start()
-    pl.when(z == s)(o_here)
-
-    isb[0] = (isb[1] + isb[2]) - isb[0]
-    ibgrad[rank] = isb[0]
-    rc(isb.at[0], ibgrad.at[rank], ib_s.at[2], ib_r.at[2], y_n).start()
-    rc(isb.at[0], ibgrad.at[2 * s + 1 - y], ib_s.at[2], ib_r.at[2], y_n).wait_recv()
-
-    def ib_two(n, first, dev):
-        return rc(ibgrad.at[pl.ds(first, 2)], ibgrad.at[pl.ds(first, 2)], ib_s.at[n], ib_r.at[n], dev)
-    ib_two(3, 2 * s, x_n).start()
-    ib_two(4, 2 * s, core_n).start()
-    ib_two(3, 2 * ((s + 2) % 4), x_n).wait_recv()
-    ib_two(5, 2 * ((s + 2) % 4), core_n).start()
-
-    f_relay(1)
-
-    def o_x():
-        rc(ograd, ograd, zo_s.at[2], zo_r.at[2], x_n).wait_recv()
-        rc(ograd, ograd, zo_s.at[3], zo_r.at[3], core_n).start()
-    pl.when((s + 2) % 4 == z)(o_x)
-    pl.when((s + 1 - 2 * c == z) | ((s + 1 - 2 * c + 2) % 4 == z))(
-        lambda: rc(ograd, ograd, zo_s.at[3], zo_r.at[3], core_n).wait_recv())
-
+    def out_part(img):
+        part2[img] = dot(act[img], w[:, out_win : out_win + win], 1, 1).astype(BF16)
+
+    rs_o = rscatter(1, part2, r1b, (dxb, dyb, rxb, ryb), out_part)
+    rs_o[0]()
     zreduce_own(0)
     f_begin(0)
+    f_relay(1)
+    pl.when(z == s)(o_here)
     f_spread(0)
+    for i in range(2):
+        out_ref[i] = (hid_s[i] + rs_o[1](i) + out_b).astype(BF16)
+    ib_end()
+    pl.when((s + 2) % 4 == z)(o_x)
+    f_end(2)
+    f_end(1)
+    emit_out()
     f_relay(0)
+    o_end()
+    f_end(0)
+    emit_rest()
 
     for ch in range(3):
         gather_drain(ch)
         zdrain(ch)
-        f_end(ch)
+        f_drain(ch)
     o_drain()
+    vec_drain()
     for a in (ag_x, ag_c, ag_n, ag_g):
         a[3]()
     rs_o[2]()
     rs_g1[2]()
     pl.when(z < s)(lambda: zo_send(True).wait_send())
     pl.when(z > s)(lambda: zo_send(False).wait_send())
-
-    def o_out_done(n):
-        rc(ograd, ograd, zo_s.at[n], zo_r.at[n], core_n).wait_send()
     pl.when(z == s)(lambda: o_out_done(2))
     pl.when((z == s) | ((s + 2) % 4 == z))(lambda: o_out_done(3))
-    pl.when(has_r)(lambda: ib_send(True).wait_send())
-    pl.when(has_l)(lambda: ib_send(False).wait_send())
-    rc(isb.at[0], ibgrad.at[rank], ib_s.at[2], ib_r.at[2], y_n).wait_send()
-    ib_two(4, 2 * (s + 1 - 2 * c), core_n).wait_recv()
-    ib_two(5, 2 * ((s + 1 - 2 * c + 2) % 4), core_n).wait_recv()
-    for n in (3, 4, 5):
-        ib_two(n, 0, core_n).wait_send()
+    pl.when(z != s)(lambda: qb_send().wait_send())
+    for k in range(1, nz):
+        ib_send(k).wait_send()
+    for n in range(7):
+        ib_msg(nz + n, rank, core_n).wait_send()
+    for stage, dst, n in stores:
+        pltpu.make_async_copy(stage, dst, st_s.at[n]).wait()
 
 
 def layer_fast(
@@ -748,10 +854,11 @@
         part = lax.dynamic_slice_in_dim(mat, sq * 2 * n, 2 * n, axis=1)
         return part.reshape(rows, 2, n).transpose(1, 0, 2)
 
-    vec = jnp.stack([ln1_gain, ln1_shift, q_bias, v_bias, o_bias, ln2_gain, ln2_shift, out_bias], axis=1)
+    vec = jnp.concatenate([ln1_gain, ln1_shift, q_bias, v_bias, o_bias, ln2_gain, ln2_shift, out_bias])
+    vec = jnp.pad(vec.reshape(VEC, rows), ((0, 8), (0, -rows % 128)))
     out_rows = lax.dynamic_slice_in_dim(out_weight, sq * 2 * ffp, 2 * ffp, axis=0)
     wp = jnp.concatenate(
-        [jnp.broadcast_to(vec, (2, rows, VEC)), two(q_weight, hid), two(k_weight, hid), two(v_weight, hid),
+        [jnp.zeros((2, rows, VEC), BF16), two(q_weight, hid), two(k_weight, hid), two(v_weight, hid),
          two(in_weight, ffp), out_rows.reshape(2, ffp, rows).transpose(0, 2, 1)], axis=2)
     total = 3 * 512
     used = VEC + 3 * hid + 2 * ffp
@@ -768,6 +875,9 @@
     D = pltpu.SemaphoreType.DMA
     V = pltpu.VMEM
     scratch = dict(
+        fgrad=V((ranks, rows, total), BF16), ograd=V((hid + 16, width), BF16), ibgrad=V((ranks, 8, win), F32),
+        st_q=V((rows, width), BF16), st_k=V((rows, width), BF16), st_v=V((rows, width), BF16),
+        st_in=V((rows, ff), BF16), st_out=V((ff, rows), BF16), vslab=V((2, nz) + vec.shape, BF16),
         w=V((2 * nz * rows, total), BF16), ow=V((hid, width), BF16), xall=V(tall, BF16), call=V(tall, BF16),
         n1=V(tall, BF16), n2=V(tall, BF16), gb=V(tall, BF16), qkv=V((nimg, length, cols), BF16),
         probs=V((nimg, 2, length, length), F32), mix=V((nimg, length, hid), BF16),
@@ -776,44 +886,37 @@
         dx=V(half, BF16), dy=V(half, BF16), rx=V((2,) + half, BF16), ry=V((2,) + half, BF16),
         dxb=V(half, BF16), dyb=V(half, BF16), rxb=V((2,) + half, BF16), ryb=V((2,) + half, BF16),
         hid_s=V((2,) + half, F32), hat2_s=V((2,) + half, F32), inv2_s=V((2, own_len, 128), F32),
-        gh_s=V((2,) + half, F32), n2own=V((8, 128), BF16), gbown=V((8, 128), BF16), vecs=V((VEC, width), F32),
+        gh_s=V((2,) + half, F32), vecs=V((VEC, width), F32),
         g=V((2 * nz * rows, total), BF16), rb=V((3, nz + 1, 2, rows, cols), BF16),
         rbo=V((2, hid + 16, width), BF16), gin_tail=V((width, 128), BF16), gout_tail=V((width, 128), BF16),
-        dqkv=V((nimg, length, cols), BF16), vsum=V((8, width), F32), ibx=V((2, 8, win), F32),
-        isb=V((3, 8, win), F32), og=V((hid + 16, width), BF16),
+        dqkv=V((nimg, length, cols), BF16), vsum=V((8, width), F32), ibx=V((nz, 8, win), F32),
+        isb=V((8, win), F32), og=V((hid + 16, width), BF16),
+        qbs=V((8, cols), F32), qbx=V((nz, 8, cols), F32),
         gy_s=D((3,)), gzr_s=D((3, nz, 2)), gzl_s=D((3, nz, 2)), g_r=D((3, nz, 2)), o_s=D((2,)), o_r=D((1,)),
         ag_s=D((4, 14)), ag_r=D((4, 14)), rs_s=D((4, 14)), rs_r=D((4, 14)), z_s=D((3, nz, 2)),
-        z_r=D((3, nz + 1, 2)), zo_s=D((4,)), zo_r=D((4,)), f_s=D((3, 4)), f_r=D((3, 4)), ib_s=D((6,)),
-        ib_r=D((6,)),
+        z_r=D((3, nz + 1, 2)), zo_s=D((4,)), zo_r=D((4,)), f_s=D((3, 7)), f_r=D((3, 7)), ib_s=D((nz + 7,)),
+        ib_r=D((nz + 7,)), qb_s=D((1,)), qb_r=D((nz,)), v_s=D((nz,)),
+        v_r=D((nz + 1,)), st_s=D((6,)),
     )
-    out, gtok, fg, og, ib = pl.pallas_call(
+    hbm = pl.BlockSpec(memory_space=pl.ANY)
+    out, gtok, gq, gk, gv, gin, gout, go, gvec, gib = pl.pallas_call(
         functools.partial(layer_kernel, nz, hid, ffp),
         out_shape=(
             jax.ShapeDtypeStruct(tokens.shape, BF16), jax.ShapeDtypeStruct(tokens.shape, BF16),
-            jax.ShapeDtypeStruct((ranks, rows, total), BF16), jax.ShapeDtypeStruct((hid + 16, width), BF16),
-            jax.ShapeDtypeStruct((ranks, 8, win), F32),
+            jax.ShapeDtypeStruct((rows, width), BF16), jax.ShapeDtypeStruct((rows, width), BF16),
+            jax.ShapeDtypeStruct((rows, width), BF16), jax.ShapeDtypeStruct((rows, ff), BF16),
+            jax.ShapeDtypeStruct((ff, rows), BF16), jax.ShapeDtypeStruct((hid + 16, width), BF16),
+            jax.ShapeDtypeStruct((VEC, rows), F32), jax.ShapeDtypeStruct((1, ff), F32),
         ),
-        in_specs=[vmem] * 5,
-        out_specs=[vmem] * 5,
+        in_specs=[vmem] * 6,
+        out_specs=[vmem, vmem] + [hbm] * 6 + [vmem, vmem],
         scratch_shapes=list(scratch.values()),
         compiler_params=pltpu.CompilerParams(
-            collective_id=0, has_side_effects=True, vmem_limit_bytes=64000 * 1024),
-    )(wp, o_weight, tokens, cotangent, inb)
-    f = fg.astype(F32)
-
-    def spread(lo, n):
-        return f[:, :, lo : lo + n].transpose(1, 0, 2).reshape(rows, ranks * n)
-
-    gq, gk, gv = [spread(VEC + i * hid, hid) for i in range(3)]
-    gin = spread(in_at, ffp)
-    gout = f[:, :, in_at + ffp : used].transpose(0, 2, 1).reshape(ff, rows)
-    vs = jnp.sum(f[:, :, 0:VEC], axis=0)
-    go = og[:hid].astype(F32)
-    gqb = og[hid, VEC : VEC + hid].astype(F32)
-    gvb = og[hid, VEC + 2 * hid : VEC + 3 * hid].astype(F32)
-    gib = ib[:, 0, off_in : off_in + ffp].reshape(ff)
-    return (out, gtok, vs[:, 0], vs[:, 1], gq, gqb, gk, gv, gvb, go, vs[:, 4], vs[:, 2], vs[:, 3], gin, gib,
-            gout, vs[:, 5])
+            collective_id=0, has_side_effects=True, vmem_limit_bytes=65000 * 1024),
+    )(wp, vec, o_weight, tokens, cotangent, inb)
+    gq, gk, gv, gin, gout, go = [a.astype(F32) for a in (gq, gk, gv, gin, gout, go[:hid])]
+    return (out, gtok, gvec[0], gvec[1], gq, gvec[6], gk, gv, gvec[7], go, gvec[4], gvec[2], gvec[3], gin,
+            gib.reshape(ff), gout, gvec[5])
 
 
 def mm(a, b, ca, cb):

time: 289 us -> 211 us (0.73)
  the two profiles are of different devices: /device:TPU:1 before, /device:TPU:11 now
where the time goes in v3:
time: 211 us; the launch traced here: 210 us
  Pallas kernels  189 us (90%)
  local copies, waits for them, and re-layouts  13.3 us (6%)
  other arithmetic  7.32 us (3%)
    pallas_call x1, Pallas kernels, layer_fast(): pl.pallas_call(functools.partial(layer_kernel, nz, hid, ffp), out_shape=(...  189 us
    convert_element_type x5, other arithmetic, layer_fast(): a.astype(F32)  6.6 us

profile of v3, /device:TPU:11, one launch (start us, length us, event | category | flops | bytes accessed | tf_op | source)
XLA Modules:
  0.0 210.3 jit_solution(16744140646507085449)
XLA Ops:
  0.7 0.8 dynamic_slice.23
  1.6 0.6 broadcast_in_dim.7.inb
  2.2 1.1 constant_dynamic-slice_fusion.2
  3.3 0.1 reshape.57
  3.4 0.1 reshape.56
  3.6 1.1 constant_dynamic-slice_fusion
  4.7 0.4 reshape.59
  5.1 1.1 constant_dynamic-slice_fusion.1
  6.3 0.4 reshape.58
  6.7 0.1 constant_dynamic-slice_fusion.4
  7.0 0.8 concatenate.6
  7.9 1.0 pad.15.wp
  9.2 0.6 pad.16.vin
  9.8 188.7 %shard_map.296 = (bf16[2,64,1152]{2,1,0:T(8,128)(2,1)}, bf16[2,64,1152]{2,1,0:T(8,128)(2,1)}, bf16[144,1152]{1,0:T(8,128)(2,1)}, bf16[144,1152]{1,0:T(8,128)(2,1...) custom-call(bf16[2,144,1536]{2,1,0:T(8,128)(2,1)} %pad.15.wp, ...), custom_call_target="tpu_custom_call" | custom-call | tf_op jit(solution)/shard_map/pallas_call | solution.py:902
  198.5 3.1 %convert_element_type.29 = f32[144,4304]{1,0:T(8,128)} convert(bf16[144,4304]{1,0:T(8,128)(2,1)} %get-tuple-element.34) | non-fusion elementwise | flops 619776 | bytes 3718656 | tf_op jit(solution)/shard_map/convert_element_type | solution.py:917
  201.6 2.4 %copy.40 = f32[4304,144]{0,1:T(8,128)} copy(bf16[4304,144]{1,0:T(8,128)(2,1)S(1)} %copy-done.1) | data formatting | bytes 3718656
  204.0 0.9 convert_element_type.25
  204.9 0.9 convert_element_type.26
  205.8 0.9 convert_element_type.27
  206.7 0.9 slice_convert_fusion
  207.6 0.7 reduce
  208.2 0.6 fusion
  208.8 0.7 copy.53
  209.6 0.7 copy.54
  (46 shorter events, 0.6 us)
Async XLA Ops:
  0.7 6.1 %copy-start = (bf16[144,1152]{1,0:T(8,128)(2,1)S(1)}, bf16[144,1152]{1,0:T(8,128)(2,1)}, u32[]{:S(2)}) copy-start(bf16[144,1152]{1,0:T(8,128)(2,1)} %param.21) | copy-start | bytes 995332
  7.8 1.1 copy-start.10
  7.8 1.1 copy-start.11
  7.9 1.1 copy-start.12
  7.9 1.1 copy-start.13
  7.9 1.0 copy-start.14
  7.9 1.0 copy-start.15
  7.9 1.0 copy-start.16
  7.9 1.0 copy-start.17
  198.5 3.1 %copy-start.1 = (bf16[4304,144]{1,0:T(8,128)(2,1)S(1)}, bf16[4304,144]{1,0:T(8,128)(2,1)}, u32[]{:S(2)}) copy-start(bf16[4304,144]{1,0:T(8,128)(2,1)} %get-tuple-element.36) | copy-start | bytes 3718660
  201.6 2.4 %copy-start.4 = (bf16[144,1152]{1,0:T(8,128)(2,1)S(1)}, bf16[144,1152]{1,0:T(8,128)(2,1)}, u32[]{:S(2)}) copy-start(bf16[144,1152]{1,0:T(8,128)(2,1)} %get-tuple-element.30) | copy-start | bytes 995332
  201.6 3.3 %copy-start.3 = (bf16[144,1152]{1,0:T(8,128)(2,1)S(1)}, bf16[144,1152]{1,0:T(8,128)(2,1)}, u32[]{:S(2)}) copy-start(bf16[144,1152]{1,0:T(8,128)(2,1)} %get-tuple-element.31) | copy-start | bytes 995332
  204.0 1.8 copy-start.2
  204.0 2.7 %copy-start.5 = (bf16[160,1152]{1,0:T(8,128)(2,1)S(1)}, bf16[160,1152]{1,0:T(8,128)(2,1)}, u32[]{:S(2)}) copy-start(bf16[160,1152]{1,0:T(8,128)(2,1)} %get-tuple-element.33) | copy-start | bytes 1105924
  204.9 2.7 %copy-start.8 = (f32[1,4304]{1,0:T(1,128)S(1)}, f32[1,4304]{1,0:T(1,128)}, u32[]{:S(2)}) copy-start(f32[1,4304]{1,0:T(1,128)} %get-tuple-element.35) | copy-start | bytes 51652
  205.8 2.4 %copy-start.9 = (f32[8,144]{1,0:T(8,128)S(1)}, f32[8,144]{1,0:T(8,128)}, u32[]{:S(2)}) copy-start(f32[8,144]{1,0:T(8,128)} %get-tuple-element.29) | copy-start | bytes 13828
  205.8 3.0 %copy-start.7 = (bf16[2,64,1152]{2,1,0:T(8,128)(2,1)S(1)}, bf16[2,64,1152]{2,1,0:T(8,128)(2,1)}, u32[]{:S(2)}) copy-start(bf16[2,64,1152]{2,1,0:T(8,128)(2,1)} %get-tuple-element.98) | copy-start | bytes 884740
  205.8 3.7 %copy-start.6 = (bf16[2,64,1152]{2,1,0:T(8,128)(2,1)S(1)}, bf16[2,64,1152]{2,1,0:T(8,128)(2,1)}, u32[]{:S(2)}) copy-start(bf16[2,64,1152]{2,1,0:T(8,128)(2,1)} %get-tuple-element.99) | copy-start | bytes 884740

commit v4 on v3

--- a/solution.py
+++ b/solution.py
@@ -47,21 +47,21 @@
 
 def layer_kernel(
     nz, hid, ffp,
-    wp, vin, ow_own, tok, cot_in, inb,
+    tok, cot_in, q_in, k_in, v_in, in_in, out_in, ow_in, inb_in, vin0, vin1, vin2, vin3, vin4, vin5, vin6, vin7,
     out_ref, gtok_ref, q_out, k_out, v_out, in_out, out_out, o_out, vec_out, ib_out,
-    fgrad, ograd, ibgrad, st_q, st_k, st_v, st_in, st_out, vslab,
+    wp, fgrad, ograd, ibgrad, st_q, st_k, st_v, st_in, st_out, vslab, inb, inflat, inrow, vflat0, vflat1, vflat2, vflat3, vflat4, vflat5, vflat6, vflat7, vrows, st_o, st_g, st_vec, st_ib,
     w, ow, xall, call, n1, n2, gb, qkv, probs, mix, act, slope, gp, part, part2, r1, r1b,
-    dx, dy, rx, ry, dxb, dyb, rxb, ryb, hid_s, hat2_s, inv2_s, gh_s, vecs, g, rb, rbo, gin_tail,
+    dx, dy, rx, ry, dxb, dyb, rxb, ryb, hid_s, hat2_s, inv2_s, gh_s, vecs, g, rb, rbh, rbo, gin_tail,
     gout_tail, dqkv, vsum, ibx, isb, og, qbs, qbx,
-    gy_s, gzr_s, gzl_s, g_r, o_s, o_r, ag_s, ag_r, rs_s, rs_r, z_s, z_r, zo_s, zo_r, f_s, f_r,
-    ib_s, ib_r, qb_s, qb_r, v_s, v_r, st_s,
+    gy_s, gz_s, gzl_s, g_r, o_s, o_r, ag_s, ag_r, rs_s, rs_r, z_s, z_r, zo_s, zo_r, f_s, f_r,
+    ib_s, ib_r, qb_s, qb_r, v_s, v_r, st_s, ld_s,
 ):
     d, s = lax.axis_index("dp"), lax.axis_index("seq")
     z, y = d // 2, d % 2
     x, c = s // 2, s % 2
     rank = 2 * s + y
-    own_len = tok.shape[1]
     nimg, length, width = xall.shape
+    own_len = dx.shape[0]
     rows8 = wp.shape[1]
     plane = 2 * rows8
     cols = 512
@@ -76,7 +76,16 @@
     core_n, x_n, y_n = (d, s + 1 - 2 * c), (d, (s + 2) % 4), (d + 1 - 2 * y, s)
     right, left = (d + 2, s), (d - 2, s)
     has_r, has_l = z < nz - 1, z > 0
+    sg = 1 - 2 * (z // 2)
+    is_end = (z == 0) | (z == nz - 1)
+    middle = (z > 0) & (z < nz - 1)
     factor = 1.0 / math.sqrt(HEAD_DIM)
+
+    def plane_at(k):
+        return z + sg * k
+
+    def away(k):
+        return (d + 2 * sg * k, s)
 
     def rc(src, dst, ss, rs, dev):
         return pltpu.make_async_remote_copy(
@@ -87,6 +96,55 @@
     column = [((d + 2 * k) % (2 * nz), s) for k in range(1, nz)]
     for dev in [core_n, x_n, y_n] + column:
         pl.semaphore_signal(barrier, inc=1, device_id=dev, device_id_type=MESH)
+
+    own_rows = pl.ds(pl.multiple_of(s * own_len, 16), own_len)
+    vflat = (vflat0, vflat1, vflat2, vflat3, vflat4, vflat5, vflat6, vflat7)
+    vec_loads = list(zip((vin0, vin1, vin2, vin3, vin4, vin5, vin6, vin7), vflat))
+    loads = [pltpu.make_async_copy(a, b, ld_s.at[n]) for n, (a, b) in enumerate(
+        vec_loads + [(q_in, st_q), (k_in, st_k), (v_in, st_v), (in_in, st_in),
+         (tok.at[0], xall.at[2 * y, own_rows]), (tok.at[1], xall.at[2 * y + 1, own_rows]), (out_in, st_out),
+         (cot_in.at[0], call.at[2 * y, own_rows]), (cot_in.at[1], call.at[2 * y + 1, own_rows]),
+         (inb_in, inflat)])]
+    for cp in loads:
+        cp.start()
+    load_o = pltpu.make_async_copy(ow_in, ow, ld_s.at[len(loads)])
+    pl.when(z == s)(lambda: load_o.start())
+
+    def build_first():
+        def go(k):
+            for j in range(2):
+                t = 2 * k + j
+                wp[j, :, 0:128] = jnp.zeros((rows8, 128), BF16)
+                for n, st in enumerate((st_q, st_k, st_v)):
+                    wp[j, :, VEC + n * qw : VEC + (n + 1) * qw] = st[:, t * qw : (t + 1) * qw]
+                wp[j, :, in_at:cols] = st_in[:, t * ffp : t * ffp + cols - in_at]
+        for k in range(4):
+            pl.when(s == k)(functools.partial(go, k))
+
+    def build_rest():
+        def go(k):
+            for j in range(2):
+                t = 2 * k + j
+                wp[j, :, 3 * cols - 128 :] = jnp.zeros((rows8, 128), BF16)
+                wp[j, :, cols : in_at + ffp] = st_in[:, t * ffp + cols - in_at : (t + 1) * ffp]
+                wp[j, :, out_at : out_at + ffp] = st_out[:, t * ffp : (t + 1) * ffp]
+        for k in range(4):
+            pl.when(s == k)(functools.partial(go, k))
+
+    def build_bias():
+        def go(t):
+            inb[...] = jnp.zeros_like(inb)
+            inb[0:1, off_in : off_in + ffp] = inrow[0:1, t * ffp : (t + 1) * ffp]
+        for t in range(8):
+            pl.when(rank == t)(functools.partial(go, t))
+
+    for cp in loads[: VEC + 6]:
+        cp.wait()
+    vrows[...] = jnp.zeros_like(vrows)
+    for n in range(VEC):
+        vrows[n : n + 1, 0:rows8] = vflat[n][...].astype(F32).reshape(1, rows8)
+    vslab[y, z] = vrows[...].astype(BF16)
+    build_first()
     pl.semaphore_wait(barrier, 3 + len(column))
 
     def wrows(origin, sub):
@@ -95,9 +153,9 @@
     def wslab(ch, origin, sub):
         return w.at[wrows(origin, sub), pl.ds(ch * cols, cols)]
 
-    def wsend(ch, origin, sub, src, to_right):
-        sems = gzr_s if to_right else gzl_s
-        return rc(src, wslab(ch, origin, sub), sems.at[ch, origin, sub], g_r.at[ch, origin, sub],
+    def wsend(ch, origin, sub, src, to_right, own=False):
+        sems = gz_s.at[ch % 2, origin, sub] if to_right or not own else gzl_s.at[ch % 2, sub]
+        return rc(src, wslab(ch, origin, sub), sems, g_r.at[ch, origin, sub],
                   right if to_right else left)
 
     def wrecv(ch, origin, sub):
@@ -107,7 +165,7 @@
     def gather_own(ch):
         src = wp.at[y, :, pl.ds(ch * cols, cols)]
         pl.when(has_r)(lambda: wsend(ch, z, y, src, True).start())
-        pl.when(has_l)(lambda: wsend(ch, z, y, src, False).start())
+        pl.when(has_l)(lambda: wsend(ch, z, y, src, False, True).start())
         w[wrows(z, y), ch * cols : (ch + 1) * cols] = wp[y, :, ch * cols : (ch + 1) * cols]
 
     def gather_swap(ch):
@@ -118,7 +176,7 @@
         wrecv(ch, z, 1 - y)
         src = wslab(ch, z, 1 - y)
         pl.when(has_r)(lambda: wsend(ch, z, 1 - y, src, True).start())
-        pl.when(has_l)(lambda: wsend(ch, z, 1 - y, src, False).start())
+        pl.when(has_l)(lambda: wsend(ch, z, 1 - y, src, False, True).start())
 
     def gather_hop(ch, k):
         def from_left():
@@ -152,23 +210,23 @@
                 pl.when((z - k >= 0) & has_r)(
                     lambda: wsend(ch, z - k, sub, wslab(ch, z - k, sub), True).wait_send())
                 pl.when((z + k < nz) & has_l)(
-                    lambda: wsend(ch, z + k, sub, wslab(ch, z + k, sub), False).wait_send())
+                    lambda: wsend(ch, z + k, sub, wslab(ch, z + k, sub), False, k == 0).wait_send())
         rc(wp.at[1 - y, :, pl.ds(ch * cols, cols)], wslab(ch, z, y), gy_s.at[ch], g_r.at[ch, z, y],
            y_n).wait_send()
 
     def osend(to_right):
         return rc(ow, ow, o_s.at[0 if to_right else 1], o_r.at[0], right if to_right else left)
 
-    def o_own():
+    def o_own(outer):
         def go():
-            ow[...] = ow_own[...]
-            pl.when(has_r)(lambda: rc(ow_own, ow, o_s.at[0], o_r.at[0], right).start())
-            pl.when(has_l)(lambda: rc(ow_own, ow, o_s.at[1], o_r.at[0], left).start())
-        pl.when(z == s)(go)
+            load_o.wait()
+            pl.when(has_r)(lambda: osend(True).start())
+            pl.when(has_l)(lambda: osend(False).start())
+        pl.when((z == s) & (is_end if outer else middle))(go)
 
     def o_pass(k):
         def go():
-            rc(ow, ow, o_r.at[0], o_r.at[0], core_n).wait_recv()
+            osend(True).wait_recv()
             pl.when((z > s) & has_r)(lambda: osend(True).start())
             pl.when((z < s) & has_l)(lambda: osend(False).start())
         pl.when((z == s + k) | (z == s - k))(go)
@@ -178,7 +236,7 @@
         pl.when((z <= s) & has_l)(lambda: osend(False).wait_send())
 
     def agather(inst, dst):
-        ss, rr = ag_s.at[inst], ag_r.at[inst]
+        ss, rr = ag_s.at[inst % 2], ag_r.at[inst % 2]
 
         def blk(yy, sq, i):
             return dst.at[2 * yy + i, pl.ds(pl.multiple_of(sq * own_len, 16), own_len)]
@@ -210,25 +268,31 @@
             for n in (0, 4, 1, 3, 6, 7):
                 sends[n].start()
 
-        def relay():
-            recvs[0].wait_recv()
-            sends[5].start()
-            recvs[4].wait_recv()
-            sends[2].start()
-            sends[8].start()
-            sends[11].start()
-            recvs[1].wait_recv()
-            sends[9].start()
-            recvs[3].wait_recv()
-            sends[10].start()
-
-        def finish():
-            recvs[2].wait_recv()
-            sends[13].start()
-            recvs[5].wait_recv()
-            sends[12].start()
-            for n in range(6, 14):
-                recvs[n].wait_recv()
+        def relay(parts=(0, 1, 2, 3)):
+            if 0 in parts:
+                recvs[0].wait_recv()
+                sends[5].start()
+                sends[8].start()
+            if 1 in parts:
+                recvs[4].wait_recv()
+                sends[2].start()
+                sends[11].start()
+            if 2 in parts:
+                recvs[1].wait_recv()
+                sends[9].start()
+            if 3 in parts:
+                recvs[3].wait_recv()
+                sends[10].start()
+
+        def finish(parts=(0, 1)):
+            if 0 in parts:
+                recvs[2].wait_recv()
+                sends[13].start()
+                recvs[5].wait_recv()
+                sends[12].start()
+            if 1 in parts:
+                for n in range(6, 14):
+                    recvs[n].wait_recv()
 
         def drain():
             for m in sends:
@@ -238,7 +302,7 @@
 
     def rscatter(inst, pt, ra, bufs, produce):
         bdx, bdy, brx, bry = bufs
-        ss, rr = rs_s.at[inst], rs_r.at[inst]
+        ss, rr = rs_s.at[inst % 2], rs_r.at[inst % 2]
         xo = 1 - x
 
         def image(it):
@@ -252,7 +316,21 @@
             return rc(pt.at[img, rows(xx, 1 - c)], ra.at[img, xx], ss.at[2 * it + xx],
                       rr.at[2 * it + xx], core_n)
 
-        def run():
+        def add(it, xx):
+            swap(it, xx).wait_recv()
+            img = image(it)
+            ra[img, xx] = (ra[img, xx].astype(F32) + pt[img, rows(xx, c)].astype(F32)).astype(BF16)
+
+        m = [
+            rc(ra.at[image(0), xo], bdx, ss.at[8], rr.at[8], x_n),
+            rc(ra.at[image(1), xo], bdy, ss.at[9], rr.at[9], y_n),
+            rc(ra.at[image(1), x], bry.at[1], ss.at[10], rr.at[10], y_n),
+            rc(ra.at[image(2), xo], brx.at[0], ss.at[11], rr.at[11], x_n),
+            rc(ra.at[image(0), x], bry.at[0], ss.at[12], rr.at[12], y_n),
+            rc(ra.at[image(3), xo], brx.at[1], ss.at[13], rr.at[13], x_n),
+        ]
+
+        def run_a():
             def step(it, carry):
                 produce(image(it))
                 swap(it, xo).start()
@@ -260,21 +338,6 @@
                 return carry
             lax.fori_loop(0, nimg, step, 0)
 
-            def add(it, xx):
-                swap(it, xx).wait_recv()
-                img = image(it)
-                ra[img, xx] = (ra[img, xx].astype(F32) + pt[img, rows(xx, c)].astype(F32)).astype(BF16)
-                return ra.at[img, xx]
-
-            msgs = [
-                (8, lambda: rc(ra.at[image(0), xo], bdx, ss.at[8], rr.at[8], x_n)),
-                (9, lambda: rc(ra.at[image(1), xo], bdy, ss.at[9], rr.at[9], y_n)),
-                (10, lambda: rc(ra.at[image(1), x], bry.at[1], ss.at[10], rr.at[10], y_n)),
-                (11, lambda: rc(ra.at[image(2), xo], brx.at[0], ss.at[11], rr.at[11], x_n)),
-                (12, lambda: rc(ra.at[image(0), x], bry.at[0], ss.at[12], rr.at[12], y_n)),
-                (13, lambda: rc(ra.at[image(3), xo], brx.at[1], ss.at[13], rr.at[13], x_n)),
-            ]
-            m = [f() for _, f in msgs]
             add(0, xo)
             m[0].start()
             add(1, xo)
@@ -285,6 +348,8 @@
             m[3].start()
             add(0, x)
             add(3, xo)
+
+        def run_b():
             m[0].wait_recv()
             ra[image(0), x] = (ra[image(0), x].astype(F32) + bdx[...].astype(F32)).astype(BF16)
             m[4].start()
@@ -306,65 +371,83 @@
             for n in range(8, 14):
                 rc(bdx, bdx, ss.at[n], rr.at[n], x_n).wait_send()
 
-        return run, result, drain
+        return run_a, run_b, result, drain
+
+    zch = [(2 * cols, cols), (cols, cols), (cols // 2, cols // 2), (0, cols // 2)]
+    order = (1 - y, y)
 
     def rb_at(ch, slot, sub):
-        return rb.at[ch, slot, sub]
+        return (rb if ch < 2 else rbh).at[ch % 2, slot, sub]
 
     def gslab(ch, dest, sub):
-        return g.at[wrows(dest, sub), pl.ds(ch * cols, cols)]
-
-    def zsend(ch, k, sub, to_right):
-        dest = z + k if to_right else z - k
-        slot = nz if k == 1 and not to_right else dest
-        return rc(gslab(ch, dest, sub), rb_at(ch, slot, sub), z_s.at[ch, dest, sub], z_r.at[ch, slot, sub],
-                  right if to_right else left)
+        return g.at[wrows(dest, sub), pl.ds(*zch[ch])]
+
+    def zsend(ch, where, sub):
+        k = (1, 2, 3, -1)[where]
+        to, slot = (1, nz) if k == 3 else (k, z)
+        return rc(gslab(ch, plane_at(k), sub), rb_at(ch, slot, sub), z_s.at[ch % 2, where, sub],
+                  z_r.at[ch, slot, sub], away(to))
 
     def zadd(ch, dest, slot, sub):
-        rc(rb_at(ch, slot, sub), rb_at(ch, slot, sub), z_r.at[ch, slot, sub], z_r.at[ch, slot, sub],
-           core_n).wait_recv()
-        r, cs = wrows(dest, sub), slice(ch * cols, (ch + 1) * cols)
-        g[r, cs] = (g[r, cs].astype(F32) + rb[ch, slot, sub].astype(F32)).astype(BF16)
-
-    def zreduce_hop(ch, k):
-        def to_right():
-            for sub in range(2):
-                pl.when(has_l)(lambda: zadd(ch, z + k, z + k, sub))
-                zsend(ch, k, sub, True).start()
-
-        def to_left():
-            for sub in range(2):
-                pl.when(has_r)(lambda: zadd(ch, z - k, z - k, sub))
-                zsend(ch, k, sub, False).start()
-
-        pl.when(z + k < nz)(to_right)
-        pl.when(z - k >= 0)(to_left)
+        ref = rb_at(ch, slot, sub)
+        rc(ref, ref, z_r.at[ch, slot, sub], z_r.at[ch, slot, sub], core_n).wait_recv()
+        r, cs = wrows(dest, sub), slice(zch[ch][0], sum(zch[ch]))
+        g[r, cs] = (g[r, cs].astype(F32) + ref[...].astype(F32)).astype(BF16)
+
+    def z_first(ch):
+        def outer():
+            for where in (2, 1, 0):
+                for sub in order:
+                    zsend(ch, where, sub).start()
+
+        def inner():
+            for where in (3, 0):
+                for sub in order:
+                    zsend(ch, where, sub).start()
+        pl.when(is_end)(outer)
+        pl.when(middle)(inner)
+
+    def z_merge(ch):
+        def inner():
+            for sub in order:
+                zadd(ch, plane_at(2), nz, sub)
+                zsend(ch, 1, sub).start()
+        pl.when(middle)(inner)
 
     def zreduce_own(ch):
+        def outer(sub):
+            zadd(ch, z, plane_at(1), sub)
+            zadd(ch, z, plane_at(2), sub)
+
+        def inner(sub):
+            for k in (-1, 1, 2):
+                zadd(ch, z, plane_at(k), sub)
+        for sub in order:
+            pl.when(is_end)(functools.partial(outer, sub))
+            pl.when(middle)(functools.partial(inner, sub))
+
+    def zdrain(ch):
         for sub in range(2):
-            pl.when(has_l)(lambda: zadd(ch, z, z, sub))
-            pl.when(has_r)(lambda: zadd(ch, z, nz, sub))
-
-    def zdrain(ch):
-        for k in range(1, nz):
-            for sub in range(2):
-                pl.when(z + k < nz)(lambda: zsend(ch, k, sub, True).wait_send())
-                pl.when(z - k >= 0)(lambda: zsend(ch, k, sub, False).wait_send())
+            zsend(ch, 0, sub).wait_send()
+            zsend(ch, 1, sub).wait_send()
+            pl.when(is_end)(lambda: zsend(ch, 2, sub).wait_send())
+            pl.when(middle)(lambda: zsend(ch, 3, sub).wait_send())
 
     def f_swap(ch):
-        src = g.at[wrows(z, 1 - y), pl.ds(ch * cols, cols)]
-        return rc(src, fgrad.at[rank, :, pl.ds(ch * cols, cols)], f_s.at[ch, 0], f_r.at[ch, 0], y_n)
+        src = g.at[wrows(z, 1 - y), pl.ds(*zch[ch])]
+        return rc(src, fgrad.at[rank, :, pl.ds(*zch[ch])], f_s.at[ch % 2, 0], f_r.at[ch, 0], y_n)
 
     def f_msg(ch, n, slot, dev):
-        piece = fgrad.at[slot, :, pl.ds(ch * cols, cols)]
-        return rc(piece, piece, f_s.at[ch, n], f_r.at[ch, n], dev)
+        piece = fgrad.at[slot, :, pl.ds(*zch[ch])]
+        return rc(piece, piece, f_s.at[ch % 2, n], f_r.at[ch, n], dev)
 
     sx, sp = (s + 2) % 4, s + 1 - 2 * c
     spx = (sp + 2) % 4
 
     def f_begin(ch):
         f_swap(ch).start()
-        fgrad[rank, :, ch * cols : (ch + 1) * cols] = g[wrows(z, y), ch * cols : (ch + 1) * cols]
+        cs = slice(zch[ch][0], sum(zch[ch]))
+        fgrad[rank, :, cs] = g[wrows(z, y), cs]
         f_msg(ch, 1, rank, x_n).start()
         f_msg(ch, 3, rank, core_n).start()
 
@@ -391,28 +474,34 @@
         for n in range(1, 7):
             f_msg(ch, n, rank, core_n).wait_send()
 
-    def z_middle(ch, k):
-        pl.when((z > 0) & (z < nz - 1))(lambda: zreduce_hop(ch, k))
-
-    def z_ends(ch):
-        for k in range(nz - 1, 0, -1):
-            pl.when((z == 0) | (z == nz - 1))(lambda: zreduce_hop(ch, k))
-
-    def zo_send(to_right):
-        n = 0 if to_right else 1
-        return rc(og, rbo.at[n], zo_s.at[n], zo_r.at[n], right if to_right else left)
-
-    def zo_add(n):
-        rc(rbo.at[n], rbo.at[n], zo_s.at[n], zo_r.at[n], core_n).wait_recv()
-        og[...] = (og[...].astype(F32) + rbo[n].astype(F32)).astype(BF16)
-
-    def zo_mid_r():
-        zo_add(0)
-        zo_send(True).start()
-
-    def zo_mid_l():
-        zo_add(1)
-        zo_send(False).start()
+    far_out = ((z == 0) & (s == nz - 1)) | ((z == nz - 1) & (s == 0))
+    adds = middle & (plane_at(2) == s)
+
+    def zo_send(far):
+        if far:
+            return rc(og, rbo.at[nz], zo_s.at[0], zo_r.at[nz], away(1))
+        return rc(og, rbo.at[z], zo_s.at[0], zo_r.at[z], (2 * s + y, s))
+
+    def zo_add(slot):
+        rc(rbo.at[slot], rbo.at[slot], zo_s.at[0], zo_r.at[slot], core_n).wait_recv()
+        og[...] = (og[...].astype(F32) + rbo[slot].astype(F32)).astype(BF16)
+
+    def zo_first():
+        pl.when(far_out)(lambda: zo_send(True).start())
+        pl.when(jnp.logical_not(far_out | adds) & (z != s))(lambda: zo_send(False).start())
+
+    def zo_merge():
+        def go():
+            zo_add(nz)
+            zo_send(False).start()
+        pl.when(adds)(go)
+
+    def zo_last():
+        def inner():
+            for k in (-1, 1, 2):
+                zo_add(plane_at(k))
+        pl.when(is_end)(lambda: [zo_add(plane_at(k)) for k in (1, 2)] and None)
+        pl.when(middle)(inner)
 
     def qb_send():
         return rc(qbs, qbx.at[z], qb_s.at[0], qb_r.at[z], (2 * s + y, s))
@@ -425,8 +514,7 @@
         pl.when(z != s)(lambda: qb_send().start())
 
     def o_here():
-        pl.when(has_l)(lambda: zo_add(0))
-        pl.when(has_r)(lambda: zo_add(1))
+        zo_last()
         total = qbs[...]
         for k in range(1, nz):
             zz = (z + k) % nz
@@ -434,19 +522,19 @@
             total = total + qbx[zz]
         og[qw:, 0:cols] = jnp.concatenate([total, total], axis=0).astype(BF16)
         ograd[...] = og[...]
-        rc(ograd, ograd, zo_s.at[2], zo_r.at[2], x_n).start()
-        rc(ograd, ograd, zo_s.at[3], zo_r.at[3], core_n).start()
+        rc(ograd, ograd, zo_s.at[2], zo_r.at[nz + 1], x_n).start()
+        rc(ograd, ograd, zo_s.at[3], zo_r.at[nz + 2], core_n).start()
 
     def o_x():
-        rc(ograd, ograd, zo_s.at[2], zo_r.at[2], x_n).wait_recv()
-        rc(ograd, ograd, zo_s.at[3], zo_r.at[3], core_n).start()
+        rc(ograd, ograd, zo_s.at[2], zo_r.at[nz + 1], x_n).wait_recv()
+        rc(ograd, ograd, zo_s.at[3], zo_r.at[nz + 2], core_n).start()
 
     def o_end():
         pl.when((sp == z) | (spx == z))(
-            lambda: rc(ograd, ograd, zo_s.at[3], zo_r.at[3], core_n).wait_recv())
+            lambda: rc(ograd, ograd, zo_s.at[3], zo_r.at[nz + 2], core_n).wait_recv())
 
     def o_out_done(n):
-        rc(ograd, ograd, zo_s.at[n], zo_r.at[n], core_n).wait_send()
+        rc(ograd, ograd, zo_s.at[n], zo_r.at[0], core_n).wait_send()
 
     def ib_send(k):
         return rc(isb, ibx.at[z], ib_s.at[k - 1], ib_r.at[z], ((d + 2 * k) % (2 * nz), s))
@@ -473,22 +561,26 @@
         ib_msg(nz + 1, rank, x_n).start()
         ib_msg(nz + 3, rank, core_n).start()
 
-    def ib_end():
+    def ib_mid():
         other = 2 * s + 1 - y
         ib_msg(nz, other, y_n).wait_recv()
         ib_msg(nz + 2, other, x_n).start()
         ib_msg(nz + 4, other, core_n).start()
         ib_msg(nz + 1, 2 * sx + y, x_n).wait_recv()
         ib_msg(nz + 5, 2 * sx + y, core_n).start()
+
+    def ib_last():
         ib_msg(nz + 2, 2 * sx + 1 - y, x_n).wait_recv()
         ib_msg(nz + 6, 2 * sx + 1 - y, core_n).start()
+
+    def ib_end():
         ib_msg(nz + 3, 2 * sp + y, core_n).wait_recv()
         ib_msg(nz + 4, 2 * sp + 1 - y, core_n).wait_recv()
         ib_msg(nz + 5, 2 * spx + y, core_n).wait_recv()
         ib_msg(nz + 6, 2 * spx + 1 - y, core_n).wait_recv()
 
     def vec_send(k):
-        return rc(vin, vslab.at[y, z], v_s.at[k - 1], v_r.at[z], ((d + 2 * k) % (2 * nz), s))
+        return rc(vslab.at[y, z], vslab.at[y, z], v_s.at[k - 1], v_r.at[z], ((d + 2 * k) % (2 * nz), s))
 
     def vec_cross():
         return rc(vslab.at[y], vslab.at[y], v_s.at[nz - 1], v_r.at[nz], y_n)
@@ -496,12 +588,11 @@
     def vec_begin():
         for k in range(1, nz):
             vec_send(k).start()
-        vslab[y, z] = vin[...]
 
     def vec_pass():
         for k in range(1, nz):
             zz = (z + k) % nz
-            rc(vin, vslab.at[y, zz], v_s.at[0], v_r.at[zz], core_n).wait_recv()
+            rc(vslab.at[y, zz], vslab.at[y, zz], v_s.at[0], v_r.at[zz], core_n).wait_recv()
         vec_cross().start()
 
     def vec_end():
@@ -517,53 +608,72 @@
         vec_cross().wait_send()
 
     nrank = fgrad.shape[0]
-    stores = [(st_q, q_out, 0), (st_k, k_out, 1), (st_v, v_out, 2), (st_in, in_out, 3),
-              (st_out, out_out, 4), (ograd, o_out, 5)]
+    stores = [pltpu.make_async_copy(a, b, st_s.at[n]) for n, (a, b) in enumerate(
+        [(st_q, q_out), (st_k, k_out), (st_v, v_out), (st_in, in_out), (st_out, out_out), (ograd, o_out),
+         (st_o, out_ref), (st_g, gtok_ref), (st_vec, vec_out), (st_ib, ib_out)])]
 
     def emit_out():
         for t in range(nrank):
-            piece = fgrad[t, :, out_at : out_at + ffp].astype(F32)
-            st_out[t * ffp : (t + 1) * ffp] = jnp.transpose(piece, (1, 0)).astype(BF16)
+            st_out[:, t * ffp : (t + 1) * ffp] = fgrad[t, :, out_at : out_at + ffp]
             st_in[:, t * ffp + cols - in_at : (t + 1) * ffp] = fgrad[t, :, cols : in_at + ffp]
-        pltpu.make_async_copy(st_out, out_out, st_s.at[4]).start()
-
-    def emit_rest():
-        pltpu.make_async_copy(ograd, o_out, st_s.at[5]).start()
+        stores[4].start()
+
+    def emit_ib():
         for t in range(nrank):
-            for n, st in enumerate((st_q, st_k, st_v)):
-                st[:, t * qw : (t + 1) * qw] = fgrad[t, :, VEC + n * qw : VEC + (n + 1) * qw]
+            st_ib[0:1, t * ffp : (t + 1) * ffp] = ibgrad[t, 0:1, off_in : off_in + ffp]
+        stores[9].start()
+
+    def emit_upper():
+        h = cols // 2
+        k_from = h - VEC - qw
+        for t in range(nrank):
+            st_k[:, t * qw + k_from : (t + 1) * qw] = fgrad[t, :, h : VEC + 2 * qw]
+            st_v[:, t * qw : (t + 1) * qw] = fgrad[t, :, VEC + 2 * qw : VEC + 3 * qw]
             st_in[:, t * ffp : t * ffp + cols - in_at] = fgrad[t, :, in_at:cols]
-        for stage, dst, n in stores[:4]:
-            pltpu.make_async_copy(stage, dst, st_s.at[n]).start()
+        stores[2].start()
+        stores[3].start()
+
+    def emit_lower():
+        h = cols // 2
+        k_from = h - VEC - qw
+        for t in range(nrank):
+            st_q[:, t * qw : (t + 1) * qw] = fgrad[t, :, VEC : VEC + qw]
+            st_k[:, t * qw : t * qw + k_from] = fgrad[t, :, VEC + qw : h]
+        stores[0].start()
+        stores[1].start()
         vcols = jnp.zeros((rows8, 128), F32)
         for t in range(nrank):
             vcols = vcols + fgrad[t, :, 0:128].astype(F32)
-        vec_out[0:VEC] = jnp.transpose(vcols, (1, 0))[0:VEC]
-        vec_out[6:7] = ograd[qw : qw + 8, VEC : VEC + qw].astype(F32)[0:1]
-        vec_out[7:8] = ograd[qw : qw + 8, VEC + 2 * qw : VEC + 3 * qw].astype(F32)[0:1]
-        for t in range(nrank):
-            ib_out[0:1, t * ffp : (t + 1) * ffp] = ibgrad[t, 0:1, off_in : off_in + ffp]
+        st_vec[0:VEC] = jnp.transpose(vcols, (1, 0))[0:VEC]
+        st_vec[6:7] = ograd[qw : qw + 8, VEC : VEC + qw].astype(F32)[0:1]
+        st_vec[7:8] = ograd[qw : qw + 8, VEC + 2 * qw : VEC + 3 * qw].astype(F32)[0:1]
+        stores[8].start()
 
     gather_swap(0)
-    own_rows = pl.ds(pl.multiple_of(s * own_len, 16), own_len)
-    for i in range(2):
-        xall[2 * y + i, own_rows] = tok[i]
     ag_x = agather(0, xall)
     ag_c = agather(1, call)
     ag_x[0]()
+    vec_begin()
     gather_own(0)
-    vec_begin()
-    for i in range(2):
-        call[2 * y + i, own_rows] = cot_in[i]
+    for cp in loads[VEC + 6 :]:
+        cp.wait()
+    build_rest()
+    inrow[...] = inflat[...].astype(F32).reshape(inrow.shape)
+    build_bias()
     gather_other(0)
-    o_own()
+    o_own(True)
     gather_hop1(0, 1, y)
-    vec_pass()
-    ag_x[1]()
+    ag_x[1]((0, 1))
     gather_hop1(0, 1, 1 - y)
     gather_hop1(0, 2, y)
-    o_pass(1)
-    ag_x[2]()
+    vec_pass()
+    ag_x[1]((2, 3))
+    gather_swap(1)
+    ag_c[0]()
+    ag_x[2]((0,))
+    gather_hop1(0, 2, 1 - y)
+    o_own(False)
+    ag_x[2]((1,))
     vec_end()
     g1, s1 = vecs[0:1], vecs[1:2]
     o_b, g2, s2, out_b = vecs[4:5], vecs[5:6], vecs[6:7], vecs[7:8]
@@ -574,14 +684,12 @@
         n1[img, r] = (hat * g1 + s1).astype(BF16)
         return carry
 
-    gather_hop1(0, 2, 1 - y)
-    o_pass(2)
+    lax.fori_loop(0, 2 * nimg, ln1_step, 0)
+    o_pass(1)
     gather_own(1)
-    gather_swap(1)
-    ag_c[0]()
-    lax.fori_loop(0, 4 * nimg, ln1_step, 0)
+    lax.fori_loop(2 * nimg, 4 * nimg, ln1_step, 0)
+    gather_other(1)
     gather_hop(0, 3)
-    gather_other(1)
 
     lane = lax.broadcasted_iota(jnp.int32, (1, cols), 1)
     qb = pltpu.roll(vecs[...], (VEC - rank * qw + width) % width, 1)[2:3, :cols]
@@ -608,12 +716,12 @@
         return carry
 
     lax.fori_loop(0, 2, att_step, 0)
+    o_pass(2)
     ag_c[1]()
+    gather_swap(2)
     gather_hop(1, 1)
     lax.fori_loop(2, nimg, att_step, 0)
     o_pass(3)
-    ag_c[2]()
-    gather_swap(2)
 
     def o_part(img):
         part[img] = dot(mix[img], ow[...], 1, 0).astype(BF16)
@@ -621,12 +729,17 @@
     rs_h = rscatter(0, part, r1, (dx, dy, rx, ry), o_part)
     rs_h[0]()
     gather_hop(1, 2)
+    gather_drain(0)
     gather_own(2)
     gather_other(2)
-    rs_h[2]()
+    rs_h[1]()
+    ag_c[2]()
+    gather_hop(2, 1)
+    rs_h[3]()
+    ag_x[3]()
     ag_n = agather(2, n2)
     for i in range(2):
-        hidden = tok[i].astype(F32) + rs_h[1](i) + o_b
+        hidden = xall[2 * y + i, own_rows].astype(F32) + rs_h[2](i) + o_b
         hid_s[i] = hidden
         hat, inv = normalize(hidden)
         hat2_s[i] = hat
@@ -635,7 +748,7 @@
     ag_n[0]()
     ag_n[1]()
     gather_hop(1, 3)
-    gather_hop(2, 1)
+    gather_hop(2, 2)
     ag_n[2]()
 
     wlane = lax.broadcasted_iota(jnp.int32, (1, win), 1)
@@ -647,9 +760,7 @@
         act[img] = jnp.where(valid, pltpu.roll(a, shift, 1), 0.0).astype(BF16)
         slope[img] = jnp.where(valid, pltpu.roll(sl, shift, 1), 0.0)
         return carry
-    lax.fori_loop(0, 2, in_step, 0)
-    gather_hop(2, 2)
-    lax.fori_loop(2, nimg, in_step, 0)
+    lax.fori_loop(0, nimg, in_step, 0)
 
     rtile = width // 3
 
@@ -662,7 +773,7 @@
         g[r, 2 * cols : 3 * cols] = acc[:, 2 * cols - out_win :].astype(BF16)
         return carry
     lax.fori_loop(0, 3, gout_step, 0)
-    z_ends(2)
+    z_first(0)
     gather_hop(2, 3)
 
     def gp_step(img, carry):
@@ -670,13 +781,13 @@
         gp[img] = pltpu.roll(ga, win - shift, 1).astype(BF16)
         return carry
     lax.fori_loop(0, nimg, gp_step, 0)
+    ib_begin()
 
     def gn2_part(img):
         part[img] = dot(gp[img], w[:, in_win : in_win + win], 1, 1).astype(BF16)
 
     rs_g2 = rscatter(2, part, r1, (dx, dy, rx, ry), gn2_part)
     rs_g2[0]()
-    z_middle(2, 2)
 
     def gin_step(t, carry):
         r = pl.ds(pl.multiple_of(t * rtile, rtile), rtile)
@@ -689,31 +800,33 @@
         g[r, 2 * cols - 128 : 2 * cols] = (acc[:, win - 128 :] + gout_tail[r].astype(F32)).astype(BF16)
         return carry
 
+    lax.fori_loop(0, 3, gin_step, 0)
+    z_first(1)
+    z_merge(0)
+    rs_g2[1]()
+
     sums = [jnp.zeros((1, width), F32) for _ in range(6)]
     ag_g = agather(3, gb)
     for i in range(2):
-        gn2 = rs_g2[1](i)
+        gn2 = rs_g2[2](i)
         hat = hat2_s[i]
         sums[2] = sums[2] + jnp.sum(gn2 * hat, axis=0, keepdims=True)
         sums[3] = sums[3] + jnp.sum(gn2, axis=0, keepdims=True)
-        up = cot_in[i].astype(F32)
+        up = call[2 * y + i, own_rows].astype(F32)
         gh = up + norm_back(gn2, g2, hat, inv2_s[i][:, 0:1])
         gh_s[i] = gh
         low = gh.astype(BF16)
         gb[2 * y + i, own_rows] = low
         sums[4] = sums[4] + jnp.sum(low.astype(F32), axis=0, keepdims=True)
         sums[5] = sums[5] + jnp.sum(up, axis=0, keepdims=True)
-    rs_g2[2]()
+    rs_g2[3]()
+    ag_c[3]()
     ag_g[0]()
     for n in range(2, 6):
         vsum[n : n + 1] = sums[n]
     vsum[6:8] = jnp.zeros((2, width), F32)
     vsum[0:2] = jnp.zeros((2, width), F32)
-    lax.fori_loop(0, 3, gin_step, 0)
-    z_ends(1)
-    ib_begin()
     ag_g[1]()
-    z_middle(2, 1)
     ag_g[2]()
 
     gacc = jnp.zeros((qw, width), F32)
@@ -721,9 +834,10 @@
         gacc = gacc + dot(mix[img], gb[img], 0, 0)
     og[0:qw] = gacc.astype(BF16)
     og[qw:] = jnp.zeros((16, width), BF16)
-    pl.when((z == 0) & (z < s))(lambda: zo_send(True).start())
-    pl.when((z == nz - 1) & (z > s))(lambda: zo_send(False).start())
-    z_middle(1, 2)
+    zo_first()
+    z_merge(1)
+    zreduce_own(0)
+    f_begin(0)
 
     def attb_step(img, carry):
         proj, gbi = qkv[img], gb[img]
@@ -753,7 +867,7 @@
 
     def gn1_part(img):
         pass
-    rs_g1 = rscatter(3, part, r1, (dx, dy, rx, ry), gn1_part)
+    rs_g1 = rscatter(4, part, r1, (dx, dy, rx, ry), gn1_part)
 
     def gqkv_step(t, carry):
         r = pl.ds(pl.multiple_of(t * rtile, rtile), rtile)
@@ -766,66 +880,80 @@
         g[r, cols - 128 : cols] = (acc[:, cols - 128 :] + gin_tail[r].astype(F32)).astype(BF16)
         return carry
 
-    lax.fori_loop(0, nimg, attb_step, 0)
-    z_middle(1, 1)
+    lax.fori_loop(0, 2, attb_step, 0)
+    f_spread(0)
+    ib_pass()
+    lax.fori_loop(2, nimg, attb_step, 0)
+    ib_mid()
     qb_begin()
     lax.fori_loop(0, 3, gqkv_step, 0)
-    z_ends(0)
+    zo_merge()
+    zdrain(0)
+    zdrain(1)
+    z_first(2)
+    z_first(3)
+    ib_last()
+    rs_g1[0]()
+    f_relay(0)
+    rs_g1[1]()
+    z_merge(2)
+    zreduce_own(1)
+    f_begin(1)
+
+    for i in range(2):
+        gn1 = rs_g1[2](i)
+        hat, inv = normalize(xall[2 * y + i, own_rows].astype(F32))
+        st_g[i] = (gh_s[i] + norm_back(gn1, g1, hat, inv)).astype(BF16)
+    stores[7].start()
+    z_merge(3)
+
+    def out_part(img):
+        part2[img] = dot(act[img], w[:, out_win : out_win + win], 1, 1).astype(BF16)
+
+    rs_o = rscatter(1, part2, r1b, (dxb, dyb, rxb, ryb), out_part)
+    rs_o[0]()
+    f_spread(1)
+    f_drain(0)
     zreduce_own(2)
     f_begin(2)
-    rs_g1[0]()
-    z_middle(0, 2)
-    ib_pass()
+    rs_o[1]()
+    f_relay(1)
     f_spread(2)
-    pl.when((z == 1) & (z < s))(zo_mid_r)
-    pl.when((z == nz - 2) & (z > s))(zo_mid_l)
-    zreduce_own(1)
-    f_begin(1)
-
-    for i in range(2):
-        gn1 = rs_g1[1](i)
-        hat, inv = normalize(tok[i].astype(F32))
-        gtok_ref[i] = (gh_s[i] + norm_back(gn1, g1, hat, inv)).astype(BF16)
-    z_middle(0, 1)
-    pl.when((z > 1) & (z < s))(zo_mid_r)
-    pl.when((z < nz - 2) & (z > s))(zo_mid_l)
-    f_relay(2)
-    f_spread(1)
-
-    def out_part(img):
-        part2[img] = dot(act[img], w[:, out_win : out_win + win], 1, 1).astype(BF16)
-
-    rs_o = rscatter(1, part2, r1b, (dxb, dyb, rxb, ryb), out_part)
-    rs_o[0]()
-    zreduce_own(0)
-    f_begin(0)
-    f_relay(1)
+    f_drain(1)
+    zreduce_own(3)
+    f_begin(3)
     pl.when(z == s)(o_here)
-    f_spread(0)
-    for i in range(2):
-        out_ref[i] = (hid_s[i] + rs_o[1](i) + out_b).astype(BF16)
-    ib_end()
-    pl.when((s + 2) % 4 == z)(o_x)
-    f_end(2)
+    f_end(0)
     f_end(1)
     emit_out()
-    f_relay(0)
+    f_relay(2)
+    f_spread(3)
+    for i in range(2):
+        st_o[i] = (hid_s[i] + rs_o[2](i) + out_b).astype(BF16)
+    stores[6].start()
+    pl.when((s + 2) % 4 == z)(o_x)
+    ib_end()
+    emit_ib()
+    f_end(2)
+    emit_upper()
     o_end()
-    f_end(0)
-    emit_rest()
-
-    for ch in range(3):
+    stores[5].start()
+    f_relay(3)
+    f_end(3)
+    emit_lower()
+
+    for ch in (1, 2):
         gather_drain(ch)
+    for ch in (2, 3):
         zdrain(ch)
         f_drain(ch)
     o_drain()
     vec_drain()
-    for a in (ag_x, ag_c, ag_n, ag_g):
+    for a in (ag_n, ag_g):
         a[3]()
-    rs_o[2]()
-    rs_g1[2]()
-    pl.when(z < s)(lambda: zo_send(True).wait_send())
-    pl.when(z > s)(lambda: zo_send(False).wait_send())
+    rs_o[3]()
+    rs_g1[3]()
+    pl.when(z != s)(lambda: zo_send(False).wait_send())
     pl.when(z == s)(lambda: o_out_done(2))
     pl.when((z == s) | ((s + 2) % 4 == z))(lambda: o_out_done(3))
     pl.when(z != s)(lambda: qb_send().wait_send())
@@ -833,51 +961,88 @@
         ib_send(k).wait_send()
     for n in range(7):
         ib_msg(nz + n, rank, core_n).wait_send()
-    for stage, dst, n in stores:
-        pltpu.make_async_copy(stage, dst, st_s.at[n]).wait()
+    for cp in stores:
+        cp.wait()
+
+
+def widen_kernel(n_mat, n_copy, n_row, *refs):
+    n = n_mat + n_copy + n_row
+    src, refs = refs[:n], refs[n:]
+    big, refs = refs[: n_mat + n_copy], refs[n_mat + n_copy :]
+    n_flat = (len(refs) - 2 - n - n_mat) // 2
+    flat_out, refs = refs[:n_flat], refs[n_flat:]
+    held, refs = refs[:n], refs[n:]
+    wide, refs = refs[:n_mat], refs[n_mat:]
+    flat, (in_s, out_s) = refs[:n_flat], refs[n_flat:]
+    got = [pltpu.make_async_copy(src[i], held[i], in_s.at[i]) for i in range(n)]
+    put = [pltpu.make_async_copy(wide[i] if i < n_mat else held[i], big[i], out_s.at[i])
+           for i in range(n_mat + n_copy)]
+    put_flat = [pltpu.make_async_copy(flat[i], flat_out[i], out_s.at[n_mat + n_copy + i]) for i in range(n_flat)]
+    for cp in got:
+        cp.start()
+    for i in range(n_mat + n_copy):
+        got[i].wait()
+        if i < n_mat:
+            rows = wide[i].shape[0]
+            for r in range(0, rows, 48):
+                wide[i][r : r + 48] = held[i][r : r + 48].astype(F32)
+        put[i].start()
+    at = 0
+    for i in range(n_mat + n_copy, n):
+        got[i].wait()
+        for r in range(held[i].shape[0]):
+            flat[at][...] = held[i][r : r + 1].reshape(held[i].shape[1])
+            put_flat[at].start()
+            at += 1
+    for cp in put + put_flat:
+        cp.wait()
+
+
+def widen(mats, rows, others, tables):
+    hbm = pl.BlockSpec(memory_space=pl.ANY)
+    arrays = list(mats) + list(others) + list(tables)
+    n = len(arrays)
+    flat = [jax.ShapeDtypeStruct((t.shape[1],), F32) for t in tables for _ in range(t.shape[0])]
+    shapes = [jax.ShapeDtypeStruct((rows, m.shape[1]), F32) for m in mats]
+    shapes += [jax.ShapeDtypeStruct(o.shape, o.dtype) for o in others] + flat
+    return pl.pallas_call(
+        functools.partial(widen_kernel, len(mats), len(others), len(tables)),
+        out_shape=tuple(shapes),
+        in_specs=[hbm] * n,
+        out_specs=[hbm] * len(shapes),
+        scratch_shapes=[pltpu.VMEM(a.shape, a.dtype) for a in arrays]
+        + [pltpu.VMEM((rows, m.shape[1]), F32) for m in mats]
+        + [pltpu.VMEM(f.shape, F32) for f in flat]
+        + [pltpu.SemaphoreType.DMA((n,)), pltpu.SemaphoreType.DMA((len(shapes),))],
+    )(*arrays)
 
 
 def layer_fast(
     tokens, cotangent, ln1_gain, ln1_shift, q_weight, q_bias, k_weight, v_weight, v_bias,
     o_weight, o_bias, ln2_gain, ln2_shift, in_weight, in_bias, out_weight, out_bias,
 ):
-    sq, ns = lax.axis_index("seq"), lax.axis_size("seq")
-    ndp = lax.axis_size("dp")
+    ns, ndp = lax.axis_size("seq"), lax.axis_size("dp")
     nz, ranks = ndp // 2, 2 * ns
     images, own_len, width = tokens.shape
     ff = in_weight.shape[1]
     hid, ffp = width // ranks, ff // ranks
     rows = q_weight.shape[0]
-    y = lax.axis_index("dp") % 2
-
-    def two(mat, n):
-        part = lax.dynamic_slice_in_dim(mat, sq * 2 * n, 2 * n, axis=1)
-        return part.reshape(rows, 2, n).transpose(1, 0, 2)
-
-    vec = jnp.concatenate([ln1_gain, ln1_shift, q_bias, v_bias, o_bias, ln2_gain, ln2_shift, out_bias])
-    vec = jnp.pad(vec.reshape(VEC, rows), ((0, 8), (0, -rows % 128)))
-    out_rows = lax.dynamic_slice_in_dim(out_weight, sq * 2 * ffp, 2 * ffp, axis=0)
-    wp = jnp.concatenate(
-        [jnp.zeros((2, rows, VEC), BF16), two(q_weight, hid), two(k_weight, hid), two(v_weight, hid),
-         two(in_weight, ffp), out_rows.reshape(2, ffp, rows).transpose(0, 2, 1)], axis=2)
+    vec = [ln1_gain, ln1_shift, q_bias, v_bias, o_bias, ln2_gain, ln2_shift, out_bias]
+    slab = (2 * VEC, (rows + 127) // 128 * 128)
     total = 3 * 512
-    used = VEC + 3 * hid + 2 * ffp
-    wp = jnp.pad(wp, ((0, 0), (0, 0), (0, total - used)))
-    in_at = VEC + 3 * hid
-    off_in = in_at % 128
     win = (ffp + 127) // 128 * 128
-    inb = lax.dynamic_slice_in_dim(in_bias, (2 * sq + y) * ffp, ffp).astype(F32)
-    inb = jnp.broadcast_to(jnp.pad(inb, (off_in, win - ffp - off_in)), (8, win))
-    vmem = pl.BlockSpec(memory_space=pltpu.VMEM)
     nimg, length, cols = 2 * images, own_len * ns, 512
     tall = (nimg, length, width)
     half = (own_len, width)
     D = pltpu.SemaphoreType.DMA
     V = pltpu.VMEM
     scratch = dict(
-        fgrad=V((ranks, rows, total), BF16), ograd=V((hid + 16, width), BF16), ibgrad=V((ranks, 8, win), F32),
-        st_q=V((rows, width), BF16), st_k=V((rows, width), BF16), st_v=V((rows, width), BF16),
-        st_in=V((rows, ff), BF16), st_out=V((ff, rows), BF16), vslab=V((2, nz) + vec.shape, BF16),
+        wp=V((2, rows, total), BF16), fgrad=V((ranks, rows, total), BF16), ograd=V((hid + 16, width), BF16),
+        ibgrad=V((ranks, 8, win), F32), st_q=V((rows, width), BF16), st_k=V((rows, width), BF16),
+        st_v=V((rows, width), BF16), st_in=V((rows, ff), BF16), st_out=V((rows, ff), BF16),
+        vslab=V((2, nz) + slab, BF16), inb=V((8, win), F32), inflat=V((ff,), BF16), inrow=V((1, ff), F32),
+        **{f"vflat{n}": V((rows,), BF16) for n in range(VEC)}, vrows=V(slab, F32),
+        st_o=V((2,) + half, BF16), st_g=V((2,) + half, BF16), st_vec=V((VEC, rows), F32), st_ib=V((1, ff), F32),
         w=V((2 * nz * rows, total), BF16), ow=V((hid, width), BF16), xall=V(tall, BF16), call=V(tall, BF16),
         n1=V(tall, BF16), n2=V(tall, BF16), gb=V(tall, BF16), qkv=V((nimg, length, cols), BF16),
         probs=V((nimg, 2, length, length), F32), mix=V((nimg, length, hid), BF16),
@@ -887,16 +1052,17 @@
         dxb=V(half, BF16), dyb=V(half, BF16), rxb=V((2,) + half, BF16), ryb=V((2,) + half, BF16),
         hid_s=V((2,) + half, F32), hat2_s=V((2,) + half, F32), inv2_s=V((2, own_len, 128), F32),
         gh_s=V((2,) + half, F32), vecs=V((VEC, width), F32),
-        g=V((2 * nz * rows, total), BF16), rb=V((3, nz + 1, 2, rows, cols), BF16),
-        rbo=V((2, hid + 16, width), BF16), gin_tail=V((width, 128), BF16), gout_tail=V((width, 128), BF16),
+        g=V((2 * nz * rows, total), BF16), rb=V((2, nz + 1, 2, rows, cols), BF16),
+        rbh=V((2, nz + 1, 2, rows, cols // 2), BF16),
+        rbo=V((nz + 1, hid + 16, width), BF16), gin_tail=V((width, 128), BF16), gout_tail=V((width, 128), BF16),
         dqkv=V((nimg, length, cols), BF16), vsum=V((8, width), F32), ibx=V((nz, 8, win), F32),
         isb=V((8, win), F32), og=V((hid + 16, width), BF16),
         qbs=V((8, cols), F32), qbx=V((nz, 8, cols), F32),
-        gy_s=D((3,)), gzr_s=D((3, nz, 2)), gzl_s=D((3, nz, 2)), g_r=D((3, nz, 2)), o_s=D((2,)), o_r=D((1,)),
-        ag_s=D((4, 14)), ag_r=D((4, 14)), rs_s=D((4, 14)), rs_r=D((4, 14)), z_s=D((3, nz, 2)),
-        z_r=D((3, nz + 1, 2)), zo_s=D((4,)), zo_r=D((4,)), f_s=D((3, 7)), f_r=D((3, 7)), ib_s=D((nz + 7,)),
+        gy_s=D((3,)), gz_s=D((2, nz, 2)), gzl_s=D((2, 2)), g_r=D((3, nz, 2)), o_s=D((nz - 1,)), o_r=D((1,)),
+        ag_s=D((2, 14)), ag_r=D((2, 14)), rs_s=D((2, 14)), rs_r=D((2, 14)), z_s=D((2, 4, 2)),
+        z_r=D((4, nz + 1, 2)), zo_s=D((4,)), zo_r=D((nz + 3,)), f_s=D((2, 7)), f_r=D((4, 7)), ib_s=D((nz + 7,)),
         ib_r=D((nz + 7,)), qb_s=D((1,)), qb_r=D((nz,)), v_s=D((nz,)),
-        v_r=D((nz + 1,)), st_s=D((6,)),
+        v_r=D((nz + 1,)), st_s=D((10,)), ld_s=D((20,)),
     )
     hbm = pl.BlockSpec(memory_space=pl.ANY)
     out, gtok, gq, gk, gv, gin, gout, go, gvec, gib = pl.pallas_call(
@@ -905,18 +1071,18 @@
             jax.ShapeDtypeStruct(tokens.shape, BF16), jax.ShapeDtypeStruct(tokens.shape, BF16),
             jax.ShapeDtypeStruct((rows, width), BF16), jax.ShapeDtypeStruct((rows, width), BF16),
             jax.ShapeDtypeStruct((rows, width), BF16), jax.ShapeDtypeStruct((rows, ff), BF16),
-            jax.ShapeDtypeStruct((ff, rows), BF16), jax.ShapeDtypeStruct((hid + 16, width), BF16),
+            jax.ShapeDtypeStruct((rows, ff), BF16), jax.ShapeDtypeStruct((hid + 16, width), BF16),
             jax.ShapeDtypeStruct((VEC, rows), F32), jax.ShapeDtypeStruct((1, ff), F32),
         ),
-        in_specs=[vmem] * 6,
-        out_specs=[vmem, vmem] + [hbm] * 6 + [vmem, vmem],
+        in_specs=[hbm] * (9 + VEC),
+        out_specs=[hbm] * 10,
         scratch_shapes=list(scratch.values()),
         compiler_params=pltpu.CompilerParams(
             collective_id=0, has_side_effects=True, vmem_limit_bytes=65000 * 1024),
-    )(wp, vec, o_weight, tokens, cotangent, inb)
-    gq, gk, gv, gin, gout, go = [a.astype(F32) for a in (gq, gk, gv, gin, gout, go[:hid])]
-    return (out, gtok, gvec[0], gvec[1], gq, gvec[6], gk, gv, gvec[7], go, gvec[4], gvec[2], gvec[3], gin,
-            gib.reshape(ff), gout, gvec[5])
+    )(tokens, cotangent, q_weight, k_weight, v_weight, in_weight, out_weight.T, o_weight, in_bias, *vec)
+    (gin, gout, gq, gk, gv, go, out, gtok, d_g1, d_s1, d_g2, d_s2, d_ob, d_outb, d_qb, d_vb, gib) = widen(
+        [gin, gout, gq, gk, gv, go], rows, [out, gtok], [gvec, gib])
+    return (out, gtok, d_g1, d_s1, gq, d_qb, gk, gv, d_vb, go, d_ob, d_g2, d_s2, gin, gib, gout.T, d_outb)
 
 
 def mm(a, b, ca, cb):

time: 211 us -> 181 us (0.86)
  the two profiles are of different devices: /device:TPU:11 before, /device:TPU:16 now
where the time goes in v4:
time: 181 us; the launch traced here: 180 us
  Pallas kernels  180 us (99%)
    pallas_call x1, Pallas kernels, layer_fast(): pl.pallas_call(functools.partial(layer_kernel, nz, hid, ffp), out_shape=(...  175 us
    pallas_call x1, Pallas kernels, widen(): pl.pallas_call(functools.partial(widen_kernel, len(mats), len(others), le...  4.98 us

profile of v4, /device:TPU:16, one launch (start us, length us, event | category | flops | bytes accessed | tf_op | source)
XLA Modules:
  0.0 180.5 jit_solution(16093340111332568221)
XLA Ops:
  0.7 174.7 %shard_map.296 = (bf16[2,64,1152]{2,1,0:T(8,128)(2,1)}, bf16[2,64,1152]{2,1,0:T(8,128)(2,1)}, bf16[144,1152]{1,0:T(8,128)(2,1)}, bf16[144,1152]{1,0:T(8,128)(2,1...) custom-call(bf16[2,64,1152]{2,1,0:T(8,128)(2,1)} %tok.1, ...), custom_call_target="tpu_custom_call" | custom-call | tf_op jit(solution)/shard_map/pallas_call | solution.py:1068
  175.4 5.0 %shard_map.297 = (f32[144,4304]{1,0:T(8,128)}, f32[144,4304]{1,0:T(8,128)}, f32[144,1152]{1,0:T(8,128)}, f32[144,1152]{1,0:T(8,128)}, f32[144,1152]{1,0:T(8,128)...) custom-call(bf16[144,4304]{1,0:T(8,128)(2,1)} %get-tuple-element.44., ...), custom_call_target="tpu_custom_call" | custom-call | tf_op jit(solution)/shard_map/pallas_call | solution.py:1008

commit v5 on v4

--- a/solution.py
+++ b/solution.py
@@ -33,12 +33,12 @@
 
 
 def gelu_parts(pre_act):
-    tanh_val = jnp.tanh(gelu_coef * (pre_act + gelu_cube * pre_act * pre_act * pre_act))
-    value_part = 0.5 * pre_act * (1.0 + tanh_val)
-    slope_part = 0.5 * (1.0 + tanh_val) + 0.5 * pre_act * (
-        1.0 - tanh_val * tanh_val
-    ) * gelu_coef * (1.0 + 3.0 * gelu_cube * pre_act * pre_act)
-    return value_part, slope_part
+    square = pre_act * pre_act
+    tanh_val = jnp.tanh(pre_act * (gelu_coef + gelu_coef * gelu_cube * square))
+    gate = 0.5 + 0.5 * tanh_val
+    value_part = pre_act * gate
+    slope_part = gate + value_part * (1.0 - gate) * (2.0 * gelu_coef + 6.0 * gelu_coef * gelu_cube * square)
+    return (value_part, slope_part)
 
 
 def dot(a, b, ca, cb):
@@ -52,9 +52,9 @@
     wp, fgrad, ograd, ibgrad, st_q, st_k, st_v, st_in, st_out, vslab, inb, inflat, inrow, vflat0, vflat1, vflat2, vflat3, vflat4, vflat5, vflat6, vflat7, vrows, st_o, st_g, st_vec, st_ib,
     w, ow, xall, call, n1, n2, gb, qkv, probs, mix, act, slope, gp, part, part2, r1, r1b,
     dx, dy, rx, ry, dxb, dyb, rxb, ryb, hid_s, hat2_s, inv2_s, gh_s, vecs, g, rb, rbh, rbo, gin_tail,
-    gout_tail, dqkv, vsum, ibx, isb, og, qbs, qbx,
+    gout_tail, dqkv, vsum, mean1, inv1, ibx, isb, og, qbs, qbx,
     gy_s, gz_s, gzl_s, g_r, o_s, o_r, ag_s, ag_r, rs_s, rs_r, z_s, z_r, zo_s, zo_r, f_s, f_r,
-    ib_s, ib_r, qb_s, qb_r, v_s, v_r, st_s, ld_s,
+    ib_s, ib_r, qb_s, qb_r, v_s, v_r,
 ):
     d, s = lax.axis_index("dp"), lax.axis_index("seq")
     z, y = d // 2, d % 2
@@ -100,14 +100,14 @@
     own_rows = pl.ds(pl.multiple_of(s * own_len, 16), own_len)
     vflat = (vflat0, vflat1, vflat2, vflat3, vflat4, vflat5, vflat6, vflat7)
     vec_loads = list(zip((vin0, vin1, vin2, vin3, vin4, vin5, vin6, vin7), vflat))
-    loads = [pltpu.make_async_copy(a, b, ld_s.at[n]) for n, (a, b) in enumerate(
+    loads = [pltpu.make_async_copy(a, b, rs_s.at[n // 14, n % 14]) for n, (a, b) in enumerate(
         vec_loads + [(q_in, st_q), (k_in, st_k), (v_in, st_v), (in_in, st_in),
          (tok.at[0], xall.at[2 * y, own_rows]), (tok.at[1], xall.at[2 * y + 1, own_rows]), (out_in, st_out),
          (cot_in.at[0], call.at[2 * y, own_rows]), (cot_in.at[1], call.at[2 * y + 1, own_rows]),
          (inb_in, inflat)])]
     for cp in loads:
         cp.start()
-    load_o = pltpu.make_async_copy(ow_in, ow, ld_s.at[len(loads)])
+    load_o = pltpu.make_async_copy(ow_in, ow, rs_s.at[1, 13])
     pl.when(z == s)(lambda: load_o.start())
 
     def build_first():
@@ -179,18 +179,13 @@
         pl.when(has_l)(lambda: wsend(ch, z, 1 - y, src, False, True).start())
 
     def gather_hop(ch, k):
-        def from_left():
+        for sub in range(2):
+            gather_hop1(ch, k, sub)
+
+    def gather_end(ch):
+        for k in range(1, nz):
             for sub in range(2):
-                wrecv(ch, z - k, sub)
-                pl.when(has_r)(lambda: wsend(ch, z - k, sub, wslab(ch, z - k, sub), True).start())
-
-        def from_right():
-            for sub in range(2):
-                wrecv(ch, z + k, sub)
-                pl.when(has_l)(lambda: wsend(ch, z + k, sub, wslab(ch, z + k, sub), False).start())
-
-        pl.when(z - k >= 0)(from_left)
-        pl.when(z + k < nz)(from_right)
+                pl.when(is_end)(lambda: wrecv(ch, plane_at(k), sub))
 
     def gather_hop1(ch, k, sub):
         def from_left():
@@ -201,8 +196,8 @@
             wrecv(ch, z + k, sub)
             pl.when(has_l)(lambda: wsend(ch, z + k, sub, wslab(ch, z + k, sub), False).start())
 
-        pl.when(z - k >= 0)(from_left)
-        pl.when(z + k < nz)(from_right)
+        pl.when(middle & (z - k >= 0))(from_left)
+        pl.when(middle & (z + k < nz))(from_right)
 
     def gather_drain(ch):
         for k in range(nz):
@@ -217,26 +212,45 @@
     def osend(to_right):
         return rc(ow, ow, o_s.at[0 if to_right else 1], o_r.at[0], right if to_right else left)
 
-    def o_own(outer):
-        def go():
+    def o_own(when):
+        def outer():
             load_o.wait()
             pl.when(has_r)(lambda: osend(True).start())
             pl.when(has_l)(lambda: osend(False).start())
-        pl.when((z == s) & (is_end if outer else middle))(go)
-
-    def o_pass(k):
+
+        def inner():
+            load_o.wait()
+            pl.when(z == 1)(lambda: osend(True).start())
+            pl.when(z == 2)(lambda: osend(False).start())
+
+        def last():
+            pl.when(z == 1)(lambda: osend(False).start())
+            pl.when(z == 2)(lambda: osend(True).start())
+        cond = is_end if when == 0 else middle
+        pl.when((z == s) & cond)((outer, inner, last)[when])
+
+    def o_take():
+        osend(True).wait_recv()
+
+    def o_pass(when):
         def go():
-            osend(True).wait_recv()
+            o_take()
             pl.when((z > s) & has_r)(lambda: osend(True).start())
             pl.when((z < s) & has_l)(lambda: osend(False).start())
-        pl.when((z == s + k) | (z == s - k))(go)
+        near = (s == 0) & (z == 1) | (s == 3) & (z == 2)
+        cross = (s == 1) & (z == 2) | (s == 2) & (z == 1)
+        far = (s == 0) & (z == 2) | (s == 3) & (z == 1)
+        pl.when((near, cross, far)[when])(go)
+
+    def o_wait():
+        pl.when((z != s) & is_end)(o_take)
 
     def o_drain():
         pl.when((z >= s) & has_r)(lambda: osend(True).wait_send())
         pl.when((z <= s) & has_l)(lambda: osend(False).wait_send())
 
     def agather(inst, dst):
-        ss, rr = ag_s.at[inst % 2], ag_r.at[inst % 2]
+        ss, rr = (rs_s.at[1], rs_r.at[1]) if inst == 1 else (ag_s, ag_r)
 
         def blk(yy, sq, i):
             return dst.at[2 * yy + i, pl.ds(pl.multiple_of(sq * own_len, 16), own_len)]
@@ -338,6 +352,7 @@
                 return carry
             lax.fori_loop(0, nimg, step, 0)
 
+        def run_c():
             add(0, xo)
             m[0].start()
             add(1, xo)
@@ -371,7 +386,7 @@
             for n in range(8, 14):
                 rc(bdx, bdx, ss.at[n], rr.at[n], x_n).wait_send()
 
-        return run_a, run_b, result, drain
+        return run_a, run_b, result, drain, run_c
 
     zch = [(2 * cols, cols), (cols, cols), (cols // 2, cols // 2), (0, cols // 2)]
     order = (1 - y, y)
@@ -382,10 +397,10 @@
     def gslab(ch, dest, sub):
         return g.at[wrows(dest, sub), pl.ds(*zch[ch])]
 
-    def zsend(ch, where, sub):
+    def zsend(ch, where, sub, outer):
         k = (1, 2, 3, -1)[where]
-        to, slot = (1, nz) if k == 3 else (k, z)
-        return rc(gslab(ch, plane_at(k), sub), rb_at(ch, slot, sub), z_s.at[ch % 2, where, sub],
+        to, slot = (1, (z, nz + 1, nz)[where]) if outer else (k, z)
+        return rc(gslab(ch, plane_at(k), sub), rb_at(ch, slot, sub), z_s.at[(0, 1, 0, 2)[ch], where, sub],
                   z_r.at[ch, slot, sub], away(to))
 
     def zadd(ch, dest, slot, sub):
@@ -394,24 +409,25 @@
         r, cs = wrows(dest, sub), slice(zch[ch][0], sum(zch[ch]))
         g[r, cs] = (g[r, cs].astype(F32) + ref[...].astype(F32)).astype(BF16)
 
-    def z_first(ch):
+    def z_first(ch, parts=(2, 1, 0, 3)):
         def outer():
             for where in (2, 1, 0):
+                if where in parts:
+                    for sub in order:
+                        zsend(ch, where, sub, True).start()
+
+        def inner():
+            if 3 in parts:
                 for sub in order:
-                    zsend(ch, where, sub).start()
-
-        def inner():
-            for where in (3, 0):
-                for sub in order:
-                    zsend(ch, where, sub).start()
+                    zsend(ch, 3, sub, False).start()
         pl.when(is_end)(outer)
         pl.when(middle)(inner)
 
-    def z_merge(ch):
+    def z_merge(ch, where):
         def inner():
             for sub in order:
-                zadd(ch, plane_at(2), nz, sub)
-                zsend(ch, 1, sub).start()
+                zadd(ch, plane_at(where + 1), nz + 1 - where, sub)
+                zsend(ch, where, sub, False).start()
         pl.when(middle)(inner)
 
     def zreduce_own(ch):
@@ -420,18 +436,18 @@
             zadd(ch, z, plane_at(2), sub)
 
         def inner(sub):
-            for k in (-1, 1, 2):
-                zadd(ch, z, plane_at(k), sub)
+            zadd(ch, z, plane_at(-1), sub)
+            zadd(ch, z, plane_at(1), sub)
         for sub in order:
             pl.when(is_end)(functools.partial(outer, sub))
             pl.when(middle)(functools.partial(inner, sub))
 
     def zdrain(ch):
         for sub in range(2):
-            zsend(ch, 0, sub).wait_send()
-            zsend(ch, 1, sub).wait_send()
-            pl.when(is_end)(lambda: zsend(ch, 2, sub).wait_send())
-            pl.when(middle)(lambda: zsend(ch, 3, sub).wait_send())
+            zsend(ch, 0, sub, False).wait_send()
+            zsend(ch, 1, sub, False).wait_send()
+            pl.when(is_end)(lambda: zsend(ch, 2, sub, True).wait_send())
+            pl.when(middle)(lambda: zsend(ch, 3, sub, False).wait_send())
 
     def f_swap(ch):
         src = g.at[wrows(z, 1 - y), pl.ds(*zch[ch])]
@@ -474,8 +490,8 @@
         for n in range(1, 7):
             f_msg(ch, n, rank, core_n).wait_send()
 
-    far_out = ((z == 0) & (s == nz - 1)) | ((z == nz - 1) & (s == 0))
-    adds = middle & (plane_at(2) == s)
+    far_out = is_end & (plane_at(0) != s) & (plane_at(1) != s)
+    adds = middle & ((plane_at(1) == s) | (plane_at(2) == s))
 
     def zo_send(far):
         if far:
@@ -497,10 +513,14 @@
         pl.when(adds)(go)
 
     def zo_last():
+        def outer():
+            zo_add(plane_at(1))
+            zo_add(plane_at(2))
+
         def inner():
-            for k in (-1, 1, 2):
-                zo_add(plane_at(k))
-        pl.when(is_end)(lambda: [zo_add(plane_at(k)) for k in (1, 2)] and None)
+            zo_add(plane_at(-1))
+            zo_add(plane_at(1))
+        pl.when(is_end)(outer)
         pl.when(middle)(inner)
 
     def qb_send():
@@ -608,7 +628,7 @@
         vec_cross().wait_send()
 
     nrank = fgrad.shape[0]
-    stores = [pltpu.make_async_copy(a, b, st_s.at[n]) for n, (a, b) in enumerate(
+    stores = [pltpu.make_async_copy(a, b, ag_s.at[n]) for n, (a, b) in enumerate(
         [(st_q, q_out), (st_k, k_out), (st_v, v_out), (st_in, in_out), (st_out, out_out), (ograd, o_out),
          (st_o, out_ref), (st_g, gtok_ref), (st_vec, vec_out), (st_ib, ib_out)])]
 
@@ -661,10 +681,11 @@
     inrow[...] = inflat[...].astype(F32).reshape(inrow.shape)
     build_bias()
     gather_other(0)
-    o_own(True)
+    o_own(0)
     gather_hop1(0, 1, y)
     ag_x[1]((0, 1))
     gather_hop1(0, 1, 1 - y)
+    o_own(1)
     gather_hop1(0, 2, y)
     vec_pass()
     ag_x[1]((2, 3))
@@ -672,7 +693,8 @@
     ag_c[0]()
     ag_x[2]((0,))
     gather_hop1(0, 2, 1 - y)
-    o_own(False)
+    o_own(2)
+    o_pass(0)
     ag_x[2]((1,))
     vec_end()
     g1, s1 = vecs[0:1], vecs[1:2]
@@ -680,16 +702,21 @@
 
     def ln1_step(b, carry):
         img, r = b // 4, pl.ds(pl.multiple_of((b % 4) * 64, 64), 64)
-        hat, _ = normalize(xall[img, r].astype(F32))
-        n1[img, r] = (hat * g1 + s1).astype(BF16)
+        values = xall[img, r].astype(F32)
+        row_mean = jnp.mean(values, axis=-1, keepdims=True)
+        centred = values - row_mean
+        inverse = lax.rsqrt(jnp.mean(centred * centred, axis=-1, keepdims=True) + eps_norm)
+        n1[img, r] = (centred * inverse * g1 + s1).astype(BF16)
+        mean1[img, r] = jnp.broadcast_to(row_mean, (64, 128))
+        inv1[img, r] = jnp.broadcast_to(inverse, (64, 128))
         return carry
 
-    lax.fori_loop(0, 2 * nimg, ln1_step, 0)
+    lax.fori_loop(0, 4 * nimg, ln1_step, 0)
+    gather_own(1)
     o_pass(1)
-    gather_own(1)
-    lax.fori_loop(2 * nimg, 4 * nimg, ln1_step, 0)
+    o_pass(2)
     gather_other(1)
-    gather_hop(0, 3)
+    gather_end(0)
 
     lane = lax.broadcasted_iota(jnp.int32, (1, cols), 1)
     qb = pltpu.roll(vecs[...], (VEC - rank * qw + width) % width, 1)[2:3, :cols]
@@ -716,25 +743,24 @@
         return carry
 
     lax.fori_loop(0, 2, att_step, 0)
-    o_pass(2)
     ag_c[1]()
     gather_swap(2)
-    gather_hop(1, 1)
     lax.fori_loop(2, nimg, att_step, 0)
-    o_pass(3)
+    o_wait()
 
     def o_part(img):
         part[img] = dot(mix[img], ow[...], 1, 0).astype(BF16)
 
     rs_h = rscatter(0, part, r1, (dx, dy, rx, ry), o_part)
     rs_h[0]()
-    gather_hop(1, 2)
+    rs_h[4]()
+    gather_hop(1, 1)
     gather_drain(0)
     gather_own(2)
     gather_other(2)
     rs_h[1]()
+    gather_hop(1, 2)
     ag_c[2]()
-    gather_hop(2, 1)
     rs_h[3]()
     ag_x[3]()
     ag_n = agather(2, n2)
@@ -746,8 +772,9 @@
         inv2_s[i] = jnp.broadcast_to(inv, (own_len, 128))
         n2[2 * y + i, own_rows] = (hat * g2 + s2).astype(BF16)
     ag_n[0]()
+    gather_hop(2, 1)
     ag_n[1]()
-    gather_hop(1, 3)
+    gather_end(1)
     gather_hop(2, 2)
     ag_n[2]()
 
@@ -756,15 +783,16 @@
 
     def in_step(img, carry):
         pre = dot(n2[img], w[:, in_win : in_win + win], 1, 0) + inb[0:1]
-        a, sl = gelu_parts(pre)
-        act[img] = jnp.where(valid, pltpu.roll(a, shift, 1), 0.0).astype(BF16)
-        slope[img] = jnp.where(valid, pltpu.roll(sl, shift, 1), 0.0)
+        a, sl = gelu_parts(pltpu.roll(pre, shift, 1))
+        act[img] = jnp.where(valid, a, 0.0).astype(BF16)
+        slope[img] = jnp.where(valid, sl, 0.0)
         return carry
     lax.fori_loop(0, nimg, in_step, 0)
 
     rtile = width // 3
 
     def gout_step(t, carry):
+        t = 1 + sg * (1 - t)
         r = pl.ds(pl.multiple_of(t * rtile, rtile), rtile)
         acc = jnp.zeros((rtile, win), F32)
         for img in range(nimg):
@@ -772,9 +800,13 @@
         gout_tail[r] = acc[:, 0 : 2 * cols - out_win].astype(BF16)
         g[r, 2 * cols : 3 * cols] = acc[:, 2 * cols - out_win :].astype(BF16)
         return carry
-    lax.fori_loop(0, 3, gout_step, 0)
-    z_first(0)
-    gather_hop(2, 3)
+    lax.fori_loop(0, 1, gout_step, 0)
+    z_first(0, (2,))
+    lax.fori_loop(1, 2, gout_step, 0)
+    z_first(0, (1,))
+    lax.fori_loop(2, 3, gout_step, 0)
+    z_first(0, (0, 3))
+    gather_end(2)
 
     def gp_step(img, carry):
         ga = dot(call[img], w[:, out_win : out_win + win], 1, 0) * slope[img]
@@ -788,6 +820,7 @@
 
     rs_g2 = rscatter(2, part, r1, (dx, dy, rx, ry), gn2_part)
     rs_g2[0]()
+    rs_g2[4]()
 
     def gin_step(t, carry):
         r = pl.ds(pl.multiple_of(t * rtile, rtile), rtile)
@@ -802,8 +835,8 @@
 
     lax.fori_loop(0, 3, gin_step, 0)
     z_first(1)
-    z_merge(0)
     rs_g2[1]()
+    z_merge(0, 1)
 
     sums = [jnp.zeros((1, width), F32) for _ in range(6)]
     ag_g = agather(3, gb)
@@ -821,11 +854,19 @@
         sums[5] = sums[5] + jnp.sum(up, axis=0, keepdims=True)
     rs_g2[3]()
     ag_c[3]()
+    ag_n[3]()
     ag_g[0]()
     for n in range(2, 6):
         vsum[n : n + 1] = sums[n]
     vsum[6:8] = jnp.zeros((2, width), F32)
     vsum[0:2] = jnp.zeros((2, width), F32)
+    z_merge(0, 0)
+
+    def out_part(img):
+        part2[img] = dot(act[img], w[:, out_win : out_win + win], 1, 1).astype(BF16)
+
+    rs_o = rscatter(1, part2, r1b, (dxb, dyb, rxb, ryb), out_part)
+    rs_o[0]()
     ag_g[1]()
     ag_g[2]()
 
@@ -835,9 +876,10 @@
     og[0:qw] = gacc.astype(BF16)
     og[qw:] = jnp.zeros((16, width), BF16)
     zo_first()
-    z_merge(1)
+    ib_pass()
     zreduce_own(0)
     f_begin(0)
+    rs_o[4]()
 
     def attb_step(img, carry):
         proj, gbi = qkv[img], gb[img]
@@ -858,11 +900,20 @@
             dv.append(dot(p.astype(BF16), gm, 0, 0).astype(BF16))
         pad = jnp.zeros((length, cols - VEC - 3 * qw), BF16)
         dqkv[img] = jnp.concatenate([zero] + dq + dk + dv + [pad], axis=1)
-        pr = dot(dqkv[img], w[:, 0:cols], 1, 1)
-        hat, _ = normalize(xall[img].astype(F32))
+        part[img] = dot(dqkv[img], w[:, 0:cols], 1, 1).astype(BF16)
+        return carry
+
+    def ln1_sum_step(img, carry):
+        pr = part[img].astype(F32)
+        hat = (xall[img].astype(F32) - mean1[img][:, 0:1]) * inv1[img][:, 0:1]
         vsum[0:1] = vsum[0:1] + jnp.sum(pr * hat, axis=0, keepdims=True)
         vsum[1:2] = vsum[1:2] + jnp.sum(pr, axis=0, keepdims=True)
-        part[img] = pr.astype(BF16)
+        return carry
+
+    def vcol_step(t, carry):
+        r = pl.ds(pl.multiple_of(t * rtile, rtile), rtile)
+        vcol = jnp.transpose(jnp.concatenate([vsum[:, r], jnp.zeros((120, rtile), F32)], axis=0), (1, 0))
+        g[r, 0:128] = (g[r, 0:128].astype(F32) + vcol).astype(BF16)
         return carry
 
     def gn1_part(img):
@@ -874,55 +925,53 @@
         acc = jnp.zeros((rtile, cols), F32)
         for img in range(nimg):
             acc = acc + dot(n1[img, :, r], dqkv[img], 0, 0)
-        vcol = jnp.transpose(jnp.concatenate([vsum[:, r], jnp.zeros((120, rtile), F32)], axis=0), (1, 0))
-        g[r, 0:128] = (acc[:, 0:128] + vcol).astype(BF16)
-        g[r, 128 : cols - 128] = acc[:, 128 : cols - 128].astype(BF16)
+        g[r, 0 : cols - 128] = acc[:, 0 : cols - 128].astype(BF16)
         g[r, cols - 128 : cols] = (acc[:, cols - 128 :] + gin_tail[r].astype(F32)).astype(BF16)
         return carry
 
     lax.fori_loop(0, 2, attb_step, 0)
     f_spread(0)
-    ib_pass()
+    ib_mid()
+    z_merge(1, 1)
     lax.fori_loop(2, nimg, attb_step, 0)
-    ib_mid()
+    rs_o[1]()
     qb_begin()
     lax.fori_loop(0, 3, gqkv_step, 0)
+    zdrain(0)
+    z_first(2)
+    rs_g1[0]()
+    rs_g1[4]()
+    z_merge(1, 0)
+    lax.fori_loop(0, nimg, ln1_sum_step, 0)
+    lax.fori_loop(0, 3, vcol_step, 0)
+    z_first(3)
+    f_relay(0)
+    ib_last()
+    rs_g1[1]()
     zo_merge()
-    zdrain(0)
-    zdrain(1)
-    z_first(2)
-    z_first(3)
-    ib_last()
-    rs_g1[0]()
-    f_relay(0)
-    rs_g1[1]()
-    z_merge(2)
     zreduce_own(1)
     f_begin(1)
+    z_merge(2, 1)
+    f_spread(1)
+    z_merge(2, 0)
 
     for i in range(2):
         gn1 = rs_g1[2](i)
         hat, inv = normalize(xall[2 * y + i, own_rows].astype(F32))
         st_g[i] = (gh_s[i] + norm_back(gn1, g1, hat, inv)).astype(BF16)
+    ag_g[3]()
     stores[7].start()
-    z_merge(3)
-
-    def out_part(img):
-        part2[img] = dot(act[img], w[:, out_win : out_win + win], 1, 1).astype(BF16)
-
-    rs_o = rscatter(1, part2, r1b, (dxb, dyb, rxb, ryb), out_part)
-    rs_o[0]()
-    f_spread(1)
+    f_relay(1)
+    pl.when(z == s)(o_here)
+    z_merge(3, 1)
+    z_merge(3, 0)
     f_drain(0)
     zreduce_own(2)
     f_begin(2)
-    rs_o[1]()
-    f_relay(1)
     f_spread(2)
     f_drain(1)
     zreduce_own(3)
     f_begin(3)
-    pl.when(z == s)(o_here)
     f_end(0)
     f_end(1)
     emit_out()
@@ -944,13 +993,12 @@
 
     for ch in (1, 2):
         gather_drain(ch)
+    for ch in (1, 2, 3):
+        zdrain(ch)
     for ch in (2, 3):
-        zdrain(ch)
         f_drain(ch)
     o_drain()
     vec_drain()
-    for a in (ag_n, ag_g):
-        a[3]()
     rs_o[3]()
     rs_g1[3]()
     pl.when(z != s)(lambda: zo_send(False).wait_send())
@@ -1052,17 +1100,18 @@
         dxb=V(half, BF16), dyb=V(half, BF16), rxb=V((2,) + half, BF16), ryb=V((2,) + half, BF16),
         hid_s=V((2,) + half, F32), hat2_s=V((2,) + half, F32), inv2_s=V((2, own_len, 128), F32),
         gh_s=V((2,) + half, F32), vecs=V((VEC, width), F32),
-        g=V((2 * nz * rows, total), BF16), rb=V((2, nz + 1, 2, rows, cols), BF16),
-        rbh=V((2, nz + 1, 2, rows, cols // 2), BF16),
+        g=V((2 * nz * rows, total), BF16), rb=V((2, nz + 2, 2, rows, cols), BF16),
+        rbh=V((2, nz + 2, 2, rows, cols // 2), BF16),
         rbo=V((nz + 1, hid + 16, width), BF16), gin_tail=V((width, 128), BF16), gout_tail=V((width, 128), BF16),
-        dqkv=V((nimg, length, cols), BF16), vsum=V((8, width), F32), ibx=V((nz, 8, win), F32),
+        dqkv=V((nimg, length, cols), BF16), vsum=V((8, width), F32),
+        mean1=V((nimg, length, 128), F32), inv1=V((nimg, length, 128), F32), ibx=V((nz, 8, win), F32),
         isb=V((8, win), F32), og=V((hid + 16, width), BF16),
         qbs=V((8, cols), F32), qbx=V((nz, 8, cols), F32),
         gy_s=D((3,)), gz_s=D((2, nz, 2)), gzl_s=D((2, 2)), g_r=D((3, nz, 2)), o_s=D((nz - 1,)), o_r=D((1,)),
-        ag_s=D((2, 14)), ag_r=D((2, 14)), rs_s=D((2, 14)), rs_r=D((2, 14)), z_s=D((2, 4, 2)),
-        z_r=D((4, nz + 1, 2)), zo_s=D((4,)), zo_r=D((nz + 3,)), f_s=D((2, 7)), f_r=D((4, 7)), ib_s=D((nz + 7,)),
+        ag_s=D((14,)), ag_r=D((14,)), rs_s=D((2, 14)), rs_r=D((2, 14)), z_s=D((3, 4, 2)),
+        z_r=D((4, nz + 2, 2)), zo_s=D((4,)), zo_r=D((nz + 3,)), f_s=D((2, 7)), f_r=D((4, 7)), ib_s=D((nz + 7,)),
         ib_r=D((nz + 7,)), qb_s=D((1,)), qb_r=D((nz,)), v_s=D((nz,)),
-        v_r=D((nz + 1,)), st_s=D((10,)), ld_s=D((20,)),
+        v_r=D((nz + 1,)),
     )
     hbm = pl.BlockSpec(memory_space=pl.ANY)
     out, gtok, gq, gk, gv, gin, gout, go, gvec, gib = pl.pallas_call(

time: 181 us -> 163 us (0.901)
  the two profiles are of different devices: /device:TPU:16 before, /device:TPU:1 now
where the time goes in v5:
time: 163 us
  Pallas kernels  162 us (99%)
    pallas_call x1, Pallas kernels, layer_fast(): pl.pallas_call(functools.partial(layer_kernel, nz, hid, ffp), out_shape=(...  157 us
    pallas_call x1, Pallas kernels, widen(): pl.pallas_call(functools.partial(widen_kernel, len(mats), len(others), le...  4.98 us

profile of v5, /device:TPU:1, one launch (start us, length us, event | category | flops | bytes accessed | tf_op | source)
XLA Modules:
  0.0 163.3 jit_solution(13079077260399646400)
XLA Ops:
  0.7 157.5 %shard_map.296 = (bf16[2,64,1152]{2,1,0:T(8,128)(2,1)}, bf16[2,64,1152]{2,1,0:T(8,128)(2,1)}, bf16[144,1152]{1,0:T(8,128)(2,1)}, bf16[144,1152]{1,0:T(8,128)(2,1...) custom-call(bf16[2,64,1152]{2,1,0:T(8,128)(2,1)} %tok.1, ...), custom_call_target="tpu_custom_call" | custom-call | tf_op jit(solution)/shard_map/pallas_call | solution.py:1117
  158.1 5.0 %shard_map.297 = (f32[144,4304]{1,0:T(8,128)}, f32[144,4304]{1,0:T(8,128)}, f32[144,1152]{1,0:T(8,128)}, f32[144,1152]{1,0:T(8,128)}, f32[144,1152]{1,0:T(8,128)...) custom-call(bf16[144,4304]{1,0:T(8,128)(2,1)} %get-tuple-element.44., ...), custom_call_target="tpu_custom_call" | custom-call | tf_op jit(solution)/shard_map/pallas_call | solution.py:1056

commit v6 on v5

--- a/solution.py
+++ b/solution.py
@@ -209,45 +209,52 @@
         rc(wp.at[1 - y, :, pl.ds(ch * cols, cols)], wslab(ch, z, y), gy_s.at[ch], g_r.at[ch, z, y],
            y_n).wait_send()
 
-    def osend(to_right):
-        return rc(ow, ow, o_s.at[0 if to_right else 1], o_r.at[0], right if to_right else left)
+    split = width // 256 * 128 + 128
+
+    def osend(to_right, half):
+        part_of = ow.at[:, pl.ds(0, split)] if half == 0 else ow.at[:, pl.ds(split, width - split)]
+        return rc(part_of, part_of, o_s.at[0 if to_right else 1, half], o_r.at[half], right if to_right else left)
 
     def o_own(when):
         def outer():
             load_o.wait()
-            pl.when(has_r)(lambda: osend(True).start())
-            pl.when(has_l)(lambda: osend(False).start())
+            for half in range(2):
+                pl.when(has_r)(lambda: osend(True, half).start())
+                pl.when(has_l)(lambda: osend(False, half).start())
 
         def inner():
             load_o.wait()
-            pl.when(z == 1)(lambda: osend(True).start())
-            pl.when(z == 2)(lambda: osend(False).start())
+            for half in range(2):
+                pl.when(z == 1)(lambda: osend(True, half).start())
+                pl.when(z == 2)(lambda: osend(False, half).start())
 
         def last():
-            pl.when(z == 1)(lambda: osend(False).start())
-            pl.when(z == 2)(lambda: osend(True).start())
+            for half in range(2):
+                pl.when(z == 1)(lambda: osend(False, half).start())
+                pl.when(z == 2)(lambda: osend(True, half).start())
         cond = is_end if when == 0 else middle
         pl.when((z == s) & cond)((outer, inner, last)[when])
 
-    def o_take():
-        osend(True).wait_recv()
-
-    def o_pass(when):
+    def o_pass(when, half):
         def go():
-            o_take()
-            pl.when((z > s) & has_r)(lambda: osend(True).start())
-            pl.when((z < s) & has_l)(lambda: osend(False).start())
+            osend(True, half).wait_recv()
+            pl.when((z > s) & has_r)(lambda: osend(True, half).start())
+            pl.when((z < s) & has_l)(lambda: osend(False, half).start())
         near = (s == 0) & (z == 1) | (s == 3) & (z == 2)
         cross = (s == 1) & (z == 2) | (s == 2) & (z == 1)
         far = (s == 0) & (z == 2) | (s == 3) & (z == 1)
         pl.when((near, cross, far)[when])(go)
 
     def o_wait():
-        pl.when((z != s) & is_end)(o_take)
+        def go():
+            osend(True, 0).wait_recv()
+            osend(True, 1).wait_recv()
+        pl.when((z != s) & is_end)(go)
 
     def o_drain():
-        pl.when((z >= s) & has_r)(lambda: osend(True).wait_send())
-        pl.when((z <= s) & has_l)(lambda: osend(False).wait_send())
+        for half in range(2):
+            pl.when((z >= s) & has_r)(lambda: osend(True, half).wait_send())
+            pl.when((z <= s) & has_l)(lambda: osend(False, half).wait_send())
 
     def agather(inst, dst):
         ss, rr = (rs_s.at[1], rs_r.at[1]) if inst == 1 else (ag_s, ag_r)
@@ -540,8 +547,9 @@
             zz = (z + k) % nz
             rc(qbs, qbx.at[zz], qb_s.at[0], qb_r.at[zz], core_n).wait_recv()
             total = total + qbx[zz]
-        og[qw:, 0:cols] = jnp.concatenate([total, total], axis=0).astype(BF16)
-        ograd[...] = og[...]
+        ograd[0:qw] = og[...]
+        ograd[qw:, 0:cols] = jnp.concatenate([total, total], axis=0).astype(BF16)
+        ograd[qw:, cols:] = jnp.zeros((16, width - cols), BF16)
         rc(ograd, ograd, zo_s.at[2], zo_r.at[nz + 1], x_n).start()
         rc(ograd, ograd, zo_s.at[3], zo_r.at[nz + 2], core_n).start()
 
@@ -688,13 +696,14 @@
     o_own(1)
     gather_hop1(0, 2, y)
     vec_pass()
+    o_pass(0, 0)
     ag_x[1]((2, 3))
+    o_pass(0, 1)
     gather_swap(1)
     ag_c[0]()
     ag_x[2]((0,))
     gather_hop1(0, 2, 1 - y)
     o_own(2)
-    o_pass(0)
     ag_x[2]((1,))
     vec_end()
     g1, s1 = vecs[0:1], vecs[1:2]
@@ -711,10 +720,13 @@
         inv1[img, r] = jnp.broadcast_to(inverse, (64, 128))
         return carry
 
-    lax.fori_loop(0, 4 * nimg, ln1_step, 0)
+    o_pass(1, 0)
+    lax.fori_loop(0, 2 * nimg, ln1_step, 0)
+    o_pass(2, 0)
+    lax.fori_loop(2 * nimg, 4 * nimg, ln1_step, 0)
+    o_pass(1, 1)
+    o_pass(2, 1)
     gather_own(1)
-    o_pass(1)
-    o_pass(2)
     gather_other(1)
     gather_end(0)
 
@@ -812,7 +824,7 @@
         ga = dot(call[img], w[:, out_win : out_win + win], 1, 0) * slope[img]
         gp[img] = pltpu.roll(ga, win - shift, 1).astype(BF16)
         return carry
-    lax.fori_loop(0, nimg, gp_step, 0)
+    lax.fori_loop(0, nimg, gp_step, 0, unroll=2)
     ib_begin()
 
     def gn2_part(img):
@@ -873,12 +885,8 @@
     gacc = jnp.zeros((qw, width), F32)
     for img in range(nimg):
         gacc = gacc + dot(mix[img], gb[img], 0, 0)
-    og[0:qw] = gacc.astype(BF16)
-    og[qw:] = jnp.zeros((16, width), BF16)
+    og[...] = gacc.astype(BF16)
     zo_first()
-    ib_pass()
-    zreduce_own(0)
-    f_begin(0)
     rs_o[4]()
 
     def attb_step(img, carry):
@@ -900,7 +908,6 @@
             dv.append(dot(p.astype(BF16), gm, 0, 0).astype(BF16))
         pad = jnp.zeros((length, cols - VEC - 3 * qw), BF16)
         dqkv[img] = jnp.concatenate([zero] + dq + dk + dv + [pad], axis=1)
-        part[img] = dot(dqkv[img], w[:, 0:cols], 1, 1).astype(BF16)
         return carry
 
     def ln1_sum_step(img, carry):
@@ -917,10 +924,11 @@
         return carry
 
     def gn1_part(img):
-        pass
+        part[img] = dot(dqkv[img], w[:, 0:cols], 1, 1).astype(BF16)
     rs_g1 = rscatter(4, part, r1, (dx, dy, rx, ry), gn1_part)
 
     def gqkv_step(t, carry):
+        t = 1 + sg * (1 - t)
         r = pl.ds(pl.multiple_of(t * rtile, rtile), rtile)
         acc = jnp.zeros((rtile, cols), F32)
         for img in range(nimg):
@@ -929,42 +937,44 @@
         g[r, cols - 128 : cols] = (acc[:, cols - 128 :] + gin_tail[r].astype(F32)).astype(BF16)
         return carry
 
-    lax.fori_loop(0, 2, attb_step, 0)
-    f_spread(0)
-    ib_mid()
+    lax.fori_loop(0, 1, attb_step, 0)
+    ib_pass()
+    zreduce_own(0)
+    f_begin(0)
+    lax.fori_loop(1, 3, attb_step, 0)
     z_merge(1, 1)
-    lax.fori_loop(2, nimg, attb_step, 0)
+    lax.fori_loop(3, nimg, attb_step, 0)
+    zdrain(0)
+    lax.fori_loop(0, 1, gqkv_step, 0)
+    z_first(2, (2,))
+    lax.fori_loop(1, 2, gqkv_step, 0)
+    z_first(2, (1,))
+    lax.fori_loop(2, 3, gqkv_step, 0)
+    z_first(2, (0, 3))
     rs_o[1]()
-    qb_begin()
-    lax.fori_loop(0, 3, gqkv_step, 0)
-    zdrain(0)
-    z_first(2)
     rs_g1[0]()
     rs_g1[4]()
+    qb_begin()
     z_merge(1, 0)
     lax.fori_loop(0, nimg, ln1_sum_step, 0)
     lax.fori_loop(0, 3, vcol_step, 0)
     z_first(3)
+    f_spread(0)
+    ib_mid()
+    zo_merge()
+    z_merge(2, 1)
+    zreduce_own(1)
+    f_begin(1)
+    rs_g1[1]()
+    z_merge(2, 0)
     f_relay(0)
     ib_last()
-    rs_g1[1]()
-    zo_merge()
-    zreduce_own(1)
-    f_begin(1)
-    z_merge(2, 1)
     f_spread(1)
-    z_merge(2, 0)
-
-    for i in range(2):
-        gn1 = rs_g1[2](i)
-        hat, inv = normalize(xall[2 * y + i, own_rows].astype(F32))
-        st_g[i] = (gh_s[i] + norm_back(gn1, g1, hat, inv)).astype(BF16)
-    ag_g[3]()
-    stores[7].start()
+    z_merge(3, 1)
+
+    z_merge(3, 0)
+    pl.when(z == s)(o_here)
     f_relay(1)
-    pl.when(z == s)(o_here)
-    z_merge(3, 1)
-    z_merge(3, 0)
     f_drain(0)
     zreduce_own(2)
     f_begin(2)
@@ -977,6 +987,12 @@
     emit_out()
     f_relay(2)
     f_spread(3)
+    for i in range(2):
+        gn1 = rs_g1[2](i)
+        hat, inv = normalize(xall[2 * y + i, own_rows].astype(F32))
+        st_g[i] = (gh_s[i] + norm_back(gn1, g1, hat, inv)).astype(BF16)
+    ag_g[3]()
+    stores[7].start()
     for i in range(2):
         st_o[i] = (hid_s[i] + rs_o[2](i) + out_b).astype(BF16)
     stores[6].start()
@@ -1102,12 +1118,12 @@
         gh_s=V((2,) + half, F32), vecs=V((VEC, width), F32),
         g=V((2 * nz * rows, total), BF16), rb=V((2, nz + 2, 2, rows, cols), BF16),
         rbh=V((2, nz + 2, 2, rows, cols // 2), BF16),
-        rbo=V((nz + 1, hid + 16, width), BF16), gin_tail=V((width, 128), BF16), gout_tail=V((width, 128), BF16),
+        rbo=V((nz + 1, hid, width), BF16), gin_tail=V((width, 128), BF16), gout_tail=V((width, 128), BF16),
         dqkv=V((nimg, length, cols), BF16), vsum=V((8, width), F32),
         mean1=V((nimg, length, 128), F32), inv1=V((nimg, length, 128), F32), ibx=V((nz, 8, win), F32),
-        isb=V((8, win), F32), og=V((hid + 16, width), BF16),
+        isb=V((8, win), F32), og=V((hid, width), BF16),
         qbs=V((8, cols), F32), qbx=V((nz, 8, cols), F32),
-        gy_s=D((3,)), gz_s=D((2, nz, 2)), gzl_s=D((2, 2)), g_r=D((3, nz, 2)), o_s=D((nz - 1,)), o_r=D((1,)),
+        gy_s=D((3,)), gz_s=D((2, nz, 2)), gzl_s=D((2, 2)), g_r=D((3, nz, 2)), o_s=D((2, 2)), o_r=D((2,)),
         ag_s=D((14,)), ag_r=D((14,)), rs_s=D((2, 14)), rs_r=D((2, 14)), z_s=D((3, 4, 2)),
         z_r=D((4, nz + 2, 2)), zo_s=D((4,)), zo_r=D((nz + 3,)), f_s=D((2, 7)), f_r=D((4, 7)), ib_s=D((nz + 7,)),
         ib_r=D((nz + 7,)), qb_s=D((1,)), qb_r=D((nz,)), v_s=D((nz,)),

time: 163 us -> 158 us (0.969)
  Pallas kernels: 162 us -> 157 us
    pallas_call x1, Pallas kernels: 157 us -> 152 us  [layer_fast(): pl.pallas_call(functools.partial(layer_kernel, nz, hid, ffp), out_shape=(...]
where the time goes in v6:
time: 158 us
  Pallas kernels  157 us (99%)
    pallas_call x1, Pallas kernels, layer_fast(): pl.pallas_call(functools.partial(layer_kernel, nz, hid, ffp), out_shape=(...  152 us
    pallas_call x1, Pallas kernels, widen(): pl.pallas_call(functools.partial(widen_kernel, len(mats), len(others), le...  4.98 us

profile of v6, /device:TPU:1, one launch (start us, length us, event | category | flops | bytes accessed | tf_op | source)
XLA Modules:
  0.0 157.8 jit_solution(4823972767015136126)
XLA Ops:
  0.7 151.9 %shard_map.296 = (bf16[2,64,1152]{2,1,0:T(8,128)(2,1)}, bf16[2,64,1152]{2,1,0:T(8,128)(2,1)}, bf16[144,1152]{1,0:T(8,128)(2,1)}, bf16[144,1152]{1,0:T(8,128)(2,1...) custom-call(bf16[2,64,1152]{2,1,0:T(8,128)(2,1)} %tok.1, ...), custom_call_target="tpu_custom_call" | custom-call | tf_op jit(solution)/shard_map/pallas_call | solution.py:1133
  152.6 5.0 %shard_map.297 = (f32[144,4304]{1,0:T(8,128)}, f32[144,4304]{1,0:T(8,128)}, f32[144,1152]{1,0:T(8,128)}, f32[144,1152]{1,0:T(8,128)}, f32[144,1152]{1,0:T(8,128)...) custom-call(bf16[144,4304]{1,0:T(8,128)(2,1)} %get-tuple-element.44., ...), custom_call_target="tpu_custom_call" | custom-call | tf_op jit(solution)/shard_map/pallas_call | solution.py:1072

commit v7 on v6

--- a/solution.py
+++ b/solution.py
@@ -101,8 +101,8 @@
     vflat = (vflat0, vflat1, vflat2, vflat3, vflat4, vflat5, vflat6, vflat7)
     vec_loads = list(zip((vin0, vin1, vin2, vin3, vin4, vin5, vin6, vin7), vflat))
     loads = [pltpu.make_async_copy(a, b, rs_s.at[n // 14, n % 14]) for n, (a, b) in enumerate(
-        vec_loads + [(q_in, st_q), (k_in, st_k), (v_in, st_v), (in_in, st_in),
-         (tok.at[0], xall.at[2 * y, own_rows]), (tok.at[1], xall.at[2 * y + 1, own_rows]), (out_in, st_out),
+        [(q_in, st_q), (k_in, st_k), (v_in, st_v), (in_in, st_in),
+         (tok.at[0], xall.at[2 * y, own_rows]), (tok.at[1], xall.at[2 * y + 1, own_rows])] + vec_loads + [(out_in, st_out),
          (cot_in.at[0], call.at[2 * y, own_rows]), (cot_in.at[1], call.at[2 * y + 1, own_rows]),
          (inb_in, inflat)])]
     for cp in loads:
@@ -138,12 +138,8 @@
         for t in range(8):
             pl.when(rank == t)(functools.partial(go, t))
 
-    for cp in loads[: VEC + 6]:
+    for cp in loads[:6]:
         cp.wait()
-    vrows[...] = jnp.zeros_like(vrows)
-    for n in range(VEC):
-        vrows[n : n + 1, 0:rows8] = vflat[n][...].astype(F32).reshape(1, rows8)
-    vslab[y, z] = vrows[...].astype(BF16)
     build_first()
     pl.semaphore_wait(barrier, 3 + len(column))
 
@@ -681,8 +677,14 @@
     ag_x = agather(0, xall)
     ag_c = agather(1, call)
     ag_x[0]()
+    gather_own(0)
+    for cp in loads[6 : VEC + 6]:
+        cp.wait()
+    vrows[...] = jnp.zeros_like(vrows)
+    for n in range(VEC):
+        vrows[n : n + 1, 0:rows8] = vflat[n][...].astype(F32).reshape(1, rows8)
+    vslab[y, z] = vrows[...].astype(BF16)
     vec_begin()
-    gather_own(0)
     for cp in loads[VEC + 6 :]:
         cp.wait()
     build_rest()

time: 158 us -> 158 us (level)
  no operation moved by 1% of the time
where the time goes in v7:
time: 158 us
  Pallas kernels  157 us (99%)
    pallas_call x1, Pallas kernels, layer_fast(): pl.pallas_call(functools.partial(layer_kernel, nz, hid, ffp), out_shape=(...  152 us
    pallas_call x1, Pallas kernels, widen(): pl.pallas_call(functools.partial(widen_kernel, len(mats), len(others), le...  4.98 us

profile of v7, /device:TPU:1, one launch (start us, length us, event | category | flops | bytes accessed | tf_op | source)
XLA Modules:
  0.0 157.6 jit_solution(6453400304839061446)
XLA Ops:
  0.7 151.8 %shard_map.296 = (bf16[2,64,1152]{2,1,0:T(8,128)(2,1)}, bf16[2,64,1152]{2,1,0:T(8,128)(2,1)}, bf16[144,1152]{1,0:T(8,128)(2,1)}, bf16[144,1152]{1,0:T(8,128)(2,1...) custom-call(bf16[2,64,1152]{2,1,0:T(8,128)(2,1)} %tok.1, ...), custom_call_target="tpu_custom_call" | custom-call | tf_op jit(solution)/shard_map/pallas_call | solution.py:1135
  152.5 5.0 %shard_map.297 = (f32[144,4304]{1,0:T(8,128)}, f32[144,4304]{1,0:T(8,128)}, f32[144,1152]{1,0:T(8,128)}, f32[144,1152]{1,0:T(8,128)}, f32[144,1152]{1,0:T(8,128)...) custom-call(bf16[144,4304]{1,0:T(8,128)(2,1)} %get-tuple-element.44., ...), custom_call_target="tpu_custom_call" | custom-call | tf_op jit(solution)/shard_map/pallas_call | solution.py:1074
